TPU v7x, 128 devices: a whole 4x4x4 slice. The times are simulated.
128 devices in a mesh: expert: 8 (over z, x_hi), dp: 16 (over x_lo, y, core).
Axes of the slice: x: 4 (x_hi: 2, x_lo: 2; x = x_hi * 2 + x_lo), y: 4, z: 4, core: 2. Of those that a mesh axis runs over, the one named last changes fastest.
Arguments:
- tokens: bfloat16 [16384, 3584], P(('expert', 'dp')), may hold values from -24 to 24
- cotangent: bfloat16 [16384, 3584], P(('expert', 'dp')), may hold values from -1.5 to 1.5
- block_expert: int32 [1024, 1], P(('expert', 'dp')), may hold values from 0 to 7; in each aligned block of 8 rows (0 to 7, 8 to 15, ...) at most 2 rows name the same one
- block_count: int32 [1024], P(('expert', 'dp')), may hold values from 8 to 16
- old_owner: int32 [8], replicated, may hold values from 0 to 7, as said below
- new_owner: int32 [8], replicated, may hold values from 0 to 7, as said below
- up_weight: float32 [8, 3584, 1024], P('expert', 'dp'), may hold values from -0.09375 to 0.09375
- down_weight: float32 [8, 1024, 3584], P('expert', 'dp'), may hold values from -0.1875 to 0.1875
- up_first: float32 [8, 3584, 1024], P('expert', 'dp'), may hold values from -6 to 6
- up_second: float32 [8, 3584, 1024], P('expert', 'dp'), may hold values from 1 to 100
- down_first: float32 [8, 1024, 3584], P('expert', 'dp'), may hold values from -6 to 6
- down_second: float32 [8, 1024, 3584], P('expert', 'dp'), may hold values from 1 to 100
Outputs:
- token_grad: bfloat16 [16384, 3584], P(('expert', 'dp'))
- up_weight_new: float32 [8, 3584, 1024], P('expert', 'dp')
- down_weight_new: float32 [8, 1024, 3584], P('expert', 'dp')
- up_first_new: float32 [8, 3584, 1024], P('expert', 'dp')
- up_second_new: float32 [8, 3584, 1024], P('expert', 'dp')
- down_first_new: float32 [8, 1024, 3584], P('expert', 'dp')
- down_second_new: float32 [8, 1024, 3584], P('expert', 'dp')
Inputs may be any that keep to these rules, and one draw needn't show every extreme that they name: `block_expert`: among the 8 blocks of one device, at most 2 are routed to any one expert, and in every draw some device routes exactly 2 blocks to some expert. A permutation: each slot appears once, and expert k is held by slot old_owner[k] before the step. A permutation: each slot appears once, and expert k is held by slot new_owner[k] after the step.
All inputs are finite; a program needn't handle non-finite values.
Results may differ from a plain program's by a relative error of at most 0.019.
Values may be sent and summed in bfloat16 or wider, within the bound.
No kernel may reach another device: no remote copies, remote signals or barrier semaphores. Data moves between devices by JAX's collectives and lax.ppermute only.
A program may use at most 192 MiB of HBM per device.

v0:
```python
import jax
import jax.numpy as jnp
from jax import lax
from jax.sharding import PartitionSpec as P

beta_one = 0.9
beta_two = 0.95
bias_one = 1.0 - 0.9**10
bias_two = 1.0 - 0.95**10
rate_value = 0.01
decay_value = 0.1
eps_value = 1e-08


def side_by_side(arrays, axis, split_dim, concat_dim, along):
    ends, at = ([], 0)
    for a in arrays[:-1]:
        at += a.shape[along]
        ends.append(at)
    both = jnp.concatenate(arrays, axis=along)
    return tuple(
        jnp.split(
            lax.all_to_all(both, axis, split_axis=split_dim, concat_axis=concat_dim, tiled=True),
            ends,
            axis=along,
        )
    )


def for_sending(array):

    def short(part):
        return part.astype(jnp.bfloat16) if part.dtype == jnp.float32 else part

    return jax.tree.map(short, array)


def cut_along(array, dim, peers):
    lengths = array.shape
    tiles = array.reshape(*lengths[:dim], peers, lengths[dim] // peers, *lengths[dim + 1 :])
    return jnp.moveaxis(tiles, dim, 0)


def sum_together(arrays, axis, dims):
    peers = lax.axis_size(axis)
    tiles = [cut_along(a, dim, peers) for a, dim in zip(arrays, dims)]
    lines = jnp.concatenate([b.reshape(peers, -1) for b in tiles], axis=1)
    span = max(16, -(-lines.shape[1] // 1024) * 8)
    lines = jnp.pad(lines, ((0, 0), (0, span * 128 - lines.shape[1]))).reshape(-1, 128)
    flat, at, finished = (lax.psum_scatter(lines, axis, tiled=True).reshape(-1), 0, [])
    for b in tiles:
        part = b[0]
        finished.append(flat[at : at + part.size].reshape(part.shape))
        at += part.size
    return tuple(finished)


def silu_parts(pre_act):
    sigma = jax.nn.sigmoid(pre_act)
    return (pre_act * sigma, sigma * (1.0 + pre_act * (1.0 - sigma)))


def adam_update(weight, moment, second, gradient):
    moment_new = beta_one * moment + (1.0 - beta_one) * gradient
    second_new = beta_two * second + (1.0 - beta_two) * gradient * gradient
    update = moment_new / bias_one / (jnp.sqrt(second_new / bias_two) + eps_value)
    return (weight - rate_value * (update + decay_value * weight), moment_new, second_new)


def contract_rows(left, right):
    return lax.dot_general(
        left, right, (((0,), (0,)), ((), ())), preferred_element_type=jnp.float32
    )


def move_state(states, old_owner, new_owner):
    groups = lax.axis_size("expert")
    labels = jnp.arange(groups, dtype=jnp.int32)
    incoming = jnp.sum(jnp.where(new_owner[:, None] == labels[None, :], labels[:, None], 0), axis=0)
    source = jnp.sum(jnp.where(labels[:, None] == incoming[None, :], old_owner[:, None], 0), axis=0)
    spread = (
        lax.all_to_all(
            states[0].astype(jnp.bfloat16), "expert", split_axis=2, concat_axis=0, tiled=True
        ).astype(jnp.float32),
        lax.all_to_all(
            states[1].astype(jnp.bfloat16), "expert", split_axis=2, concat_axis=0, tiled=True
        ).astype(jnp.float32),
        *tuple(
            (
                part.astype(jnp.float32)
                for part in side_by_side(
                    (states[2].astype(jnp.bfloat16), states[3].astype(jnp.bfloat16)),
                    "expert",
                    2,
                    0,
                    1,
                )
            )
        ),
        *tuple(
            (
                part.astype(jnp.float32)
                for part in side_by_side(
                    (states[4].astype(jnp.bfloat16), states[5].astype(jnp.bfloat16)),
                    "expert",
                    2,
                    0,
                    1,
                )
            )
        ),
    )
    ordered = [jnp.take(member, source, axis=0) for member in spread]
    return (
        lax.all_to_all(for_sending(ordered[0]), "expert", split_axis=0, concat_axis=2, tiled=True),
        lax.all_to_all(for_sending(ordered[1]), "expert", split_axis=0, concat_axis=2, tiled=True),
        lax.all_to_all(for_sending(ordered[2]), "expert", split_axis=0, concat_axis=2, tiled=True),
        lax.all_to_all(for_sending(ordered[3]), "expert", split_axis=0, concat_axis=2, tiled=True),
        lax.all_to_all(for_sending(ordered[4]), "expert", split_axis=0, concat_axis=2, tiled=True),
        lax.all_to_all(for_sending(ordered[5]), "expert", split_axis=0, concat_axis=2, tiled=True),
    )


def local(
    tokens,
    cotangent,
    block_expert,
    block_count,
    old_owner,
    new_owner,
    up_weight,
    down_weight,
    up_first,
    up_second,
    down_first,
    down_second,
):
    groups = lax.axis_size("expert")
    tok_rows, features = tokens.shape
    block_num = block_count.shape[0]
    block_len = tok_rows // block_num
    capacity = 2 * block_num // groups
    states = (up_weight, down_weight, up_first, up_second, down_first, down_second)
    states = move_state(states, old_owner, new_owner)
    up_state, down_state, up_moment, up_square, down_moment, down_square = states
    labels = jnp.arange(groups, dtype=jnp.int32)
    block_ids = block_expert[:, 0]
    target = jnp.sum(
        jnp.where(block_ids[:, None] == labels[None, :], new_owner[None, :], 0), axis=1
    )
    earlier = (
        jnp.arange(block_num, dtype=jnp.int32)[:, None]
        > jnp.arange(block_num, dtype=jnp.int32)[None, :]
    )
    same_id = block_ids[:, None] == block_ids[None, :]
    position = jnp.sum(same_id & earlier, axis=1)
    slot_of = target * capacity + position
    placing = (jnp.arange(groups * capacity, dtype=jnp.int32)[:, None] == slot_of[None, :]).astype(
        jnp.bfloat16
    )
    alive = jnp.arange(block_len, dtype=jnp.int32)[None, :] < block_count[:, None]
    zero_value = jnp.zeros((), jnp.bfloat16)
    token_blocks = jnp.where(
        alive[:, :, None], tokens.reshape(block_num, block_len, features), zero_value
    )
    grad_blocks = jnp.where(
        alive[:, :, None], cotangent.reshape(block_num, block_len, features), zero_value
    )
    send_x = jnp.einsum(
        "sb,btf->stf", placing, token_blocks, preferred_element_type=jnp.float32
    ).astype(jnp.bfloat16)
    send_dy = jnp.einsum(
        "sb,btf->stf", placing, grad_blocks, preferred_element_type=jnp.float32
    ).astype(jnp.bfloat16)
    send_x = send_x.reshape(groups, capacity * block_len, features)
    send_dy = send_dy.reshape(groups, capacity * block_len, features)
    recv_x, recv_dy = side_by_side((send_x, send_dy), "expert", 0, 0, 1)
    inputs = recv_x.reshape(groups * capacity * block_len, features)
    upstream = recv_dy.reshape(groups * capacity * block_len, features)
    up_full, down_full = (
        lax.all_gather(up_state.astype(jnp.bfloat16), "dp", axis=1, tiled=True),
        lax.all_gather(down_state.astype(jnp.bfloat16), "dp", axis=1, tiled=True),
    )
    up_mat = up_full[0]
    down_mat = down_full[0]
    pre_act = jnp.dot(inputs, up_mat, preferred_element_type=jnp.float32)
    active, slopes = silu_parts(pre_act)
    hidden = active.astype(jnp.bfloat16)
    back_grad = lax.dot_general(
        upstream, down_mat, (((1,), (1,)), ((), ())), preferred_element_type=jnp.float32
    )
    pre_grad = (back_grad * slopes).astype(jnp.bfloat16)
    input_grad = lax.dot_general(
        pre_grad, up_mat, (((1,), (1,)), ((), ())), preferred_element_type=jnp.float32
    ).astype(jnp.bfloat16)
    returned = lax.all_to_all(
        input_grad.reshape(groups, capacity * block_len, features),
        "expert",
        split_axis=0,
        concat_axis=0,
        tiled=True,
    )
    token_grad = jnp.einsum(
        "sb,stf->btf",
        placing,
        returned.reshape(groups * capacity, block_len, features),
        preferred_element_type=jnp.float32,
    )
    token_grad = token_grad.astype(jnp.bfloat16).reshape(tok_rows, features)
    up_grad, down_grad = tuple(
        (
            part.astype(jnp.float32)
            for part in sum_together(
                (
                    contract_rows(inputs, pre_grad)[None].astype(jnp.bfloat16),
                    contract_rows(hidden, upstream)[None].astype(jnp.bfloat16),
                ),
                "dp",
                (1, 1),
            )
        )
    )
    up_new = adam_update(up_state, up_moment, up_square, up_grad)
    down_new = adam_update(down_state, down_moment, down_square, down_grad)
    results = (up_new[0], down_new[0], up_new[1], up_new[2], down_new[1], down_new[2])
    return (token_grad, results[0], results[1], results[2], results[3], results[4], results[5])


def solution(mesh):
    return jax.shard_map(
        local,
        mesh=mesh,
        in_specs=(
            P(("expert", "dp"), None),
            P(("expert", "dp"), None),
            P(("expert", "dp"), None),
            P(("expert", "dp")),
            P(),
            P(),
            P("expert", "dp", None),
            P("expert", "dp", None),
            P("expert", "dp", None),
            P("expert", "dp", None),
            P("expert", "dp", None),
            P("expert", "dp", None),
        ),
        out_specs=(
            P(("expert", "dp"), None),
            P("expert", "dp", None),
            P("expert", "dp", None),
            P("expert", "dp", None),
            P("expert", "dp", None),
            P("expert", "dp", None),
            P("expert", "dp", None),
        ),
        check_vma=False,
    )
```

profile of v0, /device:TPU:4, one launch (start us, length us, event | category | flops | bytes accessed | tf_op | source)
XLA Modules:
  0.0 478.4 jit_solution(16317052749526854198)
XLA Ops:
  15.5 8.5 %all-to-all-start.3 = ((bf16[8,2,14336]{2,1,0:T(2,128)(2,1)}), bf16[8,2,14336]{2,1,0:T(2,128)(2,1)}, u32[]{:S(2)}, u32[]{:S(2)}) async-start(bf16[8,2,14336]{2,1,0:T(2,128)(2,1)} %reshape.515), calls=%async_computation.3 | async-start | bytes 917504 | tf_op jit(solution)/shard_map/all_to_all | solution.py:82
  26.1 7.4 %reduce.2 = bf16[1024,448]{1,0:T(8,128)(2,1)S(1)} reduce(bf16[1024,1,448]{2,1,0:T(2,128)(2,1)S(1)} %bitcast.114, bf16[]{:T(256)} %broadcast.318), dimensions={1}, to_apply=%bitcast.95.reduce_sub_computation | reduce | bytes 1835010
  35.6 7.2 %all-to-all-start.6 = ((bf16[8,2,28672]{2,1,0:T(2,128)(2,1)}), bf16[8,2,28672]{2,1,0:T(2,128)(2,1)S(1)}, u32[]{:S(2)}, u32[]{:S(2)}) async-start(bf16[8,2,28672]{2,1,0:T(2,128)(2,1)} %reshape.517), calls=%async_computation.6 | async-start | bytes 1835008 | tf_op jit(solution)/shard_map/all_to_all | solution.py:23
  48.0 7.4 %all-to-all-done.6 = bf16[8,2,28672]{2,1,0:T(2,128)(2,1)S(1)} async-done(((bf16[8,2,28672]{2,1,0:T(2,128)(2,1)}), bf16[8,2,28672]{2,1,0:T(2,128)(2,1)S(1)}, u32[]{:S(2)}, u32[]{:S(2)}) %all-to-all-start.6) | async-done | bytes 917536 | tf_op jit(solution)/shard_map/all_to_all | solution.py:23
  60.4 13.6 %all_to_all.136 = bf16[8,224,128]{2,1,0:T(8,128)(2,1)S(1)} all-to-all(bf16[8,224,128]{2,1,0:T(8,128)(2,1)S(1)} %get-tuple-element.31), channel_id=1, replica_groups=mesh['expert'=8,'dp'=16] {'expert'}, dimensions={0} | all-to-all | bytes 917504 | tf_op jit(solution)/shard_map/all_to_all | solution.py:115
  77.4 19.7 %reduce.1 = bf16[3584,64]{1,0:T(8,128)(2,1)S(1)} reduce(bf16[3584,1,64]{2,1,0:T(2,128)(2,1)S(1)} %bitcast.119, bf16[]{:T(256)} %broadcast.318), dimensions={1}, to_apply=%bitcast.91.reduce_sub_computation | reduce | bytes 917506
  98.5 6.0 %all-to-all-start.1 = ((bf16[8,2,14336]{2,1,0:T(2,128)(2,1)}), bf16[8,2,14336]{2,1,0:T(2,128)(2,1)S(1)}, u32[]{:S(2)}, u32[]{:S(2)}) async-start(bf16[8,2,14336]{2,1,0:T(2,128)(2,1)} %reshape.513), calls=%async_computation.1 | async-start | bytes 917504 | tf_op jit(solution)/shard_map/all_to_all | solution.py:85
  111.5 6.8 %fusion.39 = bf16[3584,1,128]{2,1,0:T(2,128)(2,1)} fusion(bf16[1,64,3584]{1,0,2:T(2,128)(2,1)S(1)} %copy.151, bf16[1,64,3584]{1,0,2:T(2,128)(2,1)} %copy.150), kind=kLoop, calls=%fused_computation.87 | loop fusion | flops 1835008 | bytes 1835008
  118.3 20.7 %reduce = bf16[3584,128]{1,0:T(8,128)(2,1)S(1)} reduce(bf16[3584,1,128]{2,1,0:T(2,128)(2,1)} %fusion.39, bf16[]{:T(256)} %broadcast.318), dimensions={1}, to_apply=%fusion.39.reduce_sub_computation | reduce | bytes 1835010
  141.0 7.2 %all-to-all-start.9 = ((bf16[8,2,28672]{2,1,0:T(2,128)(2,1)}), bf16[8,2,28672]{2,1,0:T(2,128)(2,1)S(1)}, u32[]{:S(2)}, u32[]{:S(2)}) async-start(bf16[8,2,28672]{2,1,0:T(2,128)(2,1)} %reshape.519), calls=%async_computation.10 | async-start | bytes 1835008 | tf_op jit(solution)/shard_map/all_to_all | solution.py:23
  163.5 13.8 %all_to_all.137 = bf16[8,64,448]{2,1,0:T(8,128)(2,1)S(1)} all-to-all(bf16[8,64,448]{2,1,0:T(8,128)(2,1)S(1)} %get-tuple-element.28), channel_id=1, replica_groups=mesh['expert'=8,'dp'=16] {'expert'}, dimensions={0} | all-to-all | bytes 917504 | tf_op jit(solution)/shard_map/all_to_all | solution.py:116
  184.2 78.7 %all_to_all.138 = bf16[8,64,3584]{2,1,0:T(8,128)(2,1)S(1)} all-to-all(bf16[8,64,3584]{2,1,0:T(8,128)(2,1)S(1)} %pad_maximum_fusion.1), channel_id=1, replica_groups=mesh['expert'=8,'dp'=16] {'expert'}, dimensions={0} | all-to-all | bytes 7340032 | tf_op jit(solution)/shard_map/all_to_all | solution.py:23
  275.8 7.2 %reshape_transpose_reshape.7 = bf16[16,229376]{1,0:T(8,128)(2,1)} reshape(bf16[1024,3584]{1,0:T(8,128)(2,1)} %convolution_convert_fusion) | data formatting | bytes 14680064 | tf_op jit(solution)/shard_map/reshape;transpose;reshape | solution.py:47
  294.1 7.2 %reshape_transpose_reshape.6 = bf16[16,229376]{1,0:T(8,128)(2,1)} reshape(bf16[3584,1024]{1,0:T(8,128)(2,1)} %convolution_convert_fusion.1) | data formatting | bytes 14680064 | tf_op jit(solution)/shard_map/reshape;transpose;reshape | solution.py:47
  301.4 16.3 %pad_maximum_fusion = bf16[16,458752]{1,0:T(8,128)(2,1)} fusion(bf16[16,229376]{1,0:T(8,128)(2,1)} %reshape_transpose_reshape.7, bf16[16,229376]{1,0:T(8,128)(2,1)} %reshape_transpose_reshape.6), kind=kLoop, calls=%fused_computation.6 | loop fusion | flops 29360128 | bytes 29360128 | tf_op jit(solution)/shard_map/concatenate | solution.py:47
  317.7 18.9 %reshape.430 = bf16[57344,128]{1,0:T(8,128)(2,1)} reshape(bf16[16,458752]{1,0:T(8,128)(2,1)} %pad_maximum_fusion) | data formatting | bytes 29360128 | tf_op jit(solution)/shard_map/reshape | solution.py:49
  337.6 15.1 %all_to_all.139 = bf16[8,224,128]{2,1,0:T(8,128)(2,1)} all-to-all(bf16[8,224,128]{2,1,0:T(8,128)(2,1)S(1)} %copy-done.9), channel_id=1, replica_groups=mesh['expert'=8,'dp'=16] {'expert'}, dimensions={0} | all-to-all | bytes 917504 | tf_op jit(solution)/shard_map/all_to_all | solution.py:117
  352.7 15.3 %all_to_all.140 = bf16[8,224,128]{2,1,0:T(8,128)(2,1)} all-to-all(bf16[8,224,128]{2,1,0:T(8,128)(2,1)S(1)} %copy-done.8), channel_id=1, replica_groups=mesh['expert'=8,'dp'=16] {'expert'}, dimensions={0} | all-to-all | bytes 917504 | tf_op jit(solution)/shard_map/all_to_all | solution.py:118
  368.1 16.0 %all_to_all.141 = bf16[8,64,448]{2,1,0:T(8,128)(2,1)} all-to-all(bf16[8,64,448]{2,1,0:T(8,128)(2,1)S(1)} %get-tuple-element.27), channel_id=1, replica_groups=mesh['expert'=8,'dp'=16] {'expert'}, dimensions={0} | all-to-all | bytes 917504 | tf_op jit(solution)/shard_map/all_to_all | solution.py:119
  384.0 6.8 %all-to-all-start.11 = ((bf16[8,64,448]{2,1,0:T(8,128)(2,1)}), bf16[8,64,448]{2,1,0:T(8,128)(2,1)S(1)}, u32[]{:S(2)}, u32[]{:S(2)}) async-start(bf16[8,64,448]{2,1,0:T(8,128)(2,1)} %get-tuple-element.26), calls=%async_computation.12 | async-start | bytes 1048576 | tf_op jit(solution)/shard_map/all_to_all | solution.py:120
  390.8 6.5 %fusion.6 = bf16[256,3584]{1,0:T(8,128)(2,1)} fusion(bf16[256,1024]{1,0:T(8,128)(2,1)S(1)} %copy-done.20, bf16[1,3584,1024]{2,1,0:T(8,128)(2,1)} %all-gather.5.cloned.1.call-done), kind=kOutput, calls=%fused_computation.15 | convolution fusion | flops 1879965696 | bytes 9699328 | tf_op jit(solution)/shard_map/dot_general | solution.py:193
  400.5 7.3 %all-to-all-start.5 = ((bf16[8,32,3584]{2,1,0:T(8,128)(2,1)}), bf16[8,32,3584]{2,1,0:T(8,128)(2,1)S(1)}, u32[]{:S(2)}, u32[]{:S(2)}) async-start(bf16[8,32,3584]{2,1,0:T(8,128)(2,1)} %bitcast.134), calls=%async_computation.5 | async-start | bytes 3670016 | tf_op jit(solution)/shard_map/all_to_all | solution.py:196
  417.1 16.9 %all-to-all-done.5 = bf16[8,32,3584]{2,1,0:T(8,128)(2,1)S(1)} async-done(((bf16[8,32,3584]{2,1,0:T(8,128)(2,1)}), bf16[8,32,3584]{2,1,0:T(8,128)(2,1)S(1)}, u32[]{:S(2)}, u32[]{:S(2)}) %all-to-all-start.5) | async-done | bytes 1835040 | tf_op jit(solution)/shard_map/all_to_all | solution.py:196
  437.2 24.9 %reduce-scatter.2.cloned.1.call-done = bf16[3584,128]{1,0:T(8,128)(2,1)} async-done(((bf16[57344,128]{1,0:T(8,128)(2,1)}), bf16[3584,128]{1,0:T(8,128)(2,1)}) %reduce-scatter.2.cloned.1.call-update) | async-done | bytes 917520 | tf_op jit(solution)/shard_map/reduce_scatter | solution.py:50
  (143 shorter events, 108.3 us)
Async XLA Ops:
  9.3 14.8 %copy-start.13 = (f32[1,224,1024]{2,1,0:T(8,128)S(1)}, f32[1,224,1024]{2,1,0:T(8,128)}, u32[]{:S(2)}) copy-start(f32[1,224,1024]{2,1,0:T(8,128)} %param.25) | copy-start | bytes 2752516
  13.8 10.3 %copy-start.14 = (f32[1,224,1024]{2,1,0:T(8,128)S(1)}, f32[1,224,1024]{2,1,0:T(8,128)}, u32[]{:S(2)}) copy-start(f32[1,224,1024]{2,1,0:T(8,128)} %param.24) | copy-start | bytes 2752516
  15.5 20.1 %all-to-all-start.3 = ((bf16[8,2,14336]{2,1,0:T(2,128)(2,1)}), bf16[8,2,14336]{2,1,0:T(2,128)(2,1)}, u32[]{:S(2)}, u32[]{:S(2)}) async-start(bf16[8,2,14336]{2,1,0:T(2,128)(2,1)} %reshape.515), calls=%async_computation.3 | async-start | bytes 917504 | tf_op jit(solution)/shard_map/all_to_all | solution.py:82
  33.5 9.3 %copy-start.21 = (s32[8]{0:T(128)S(1)}, s32[8]{0:T(128)}, u32[]{:S(2)}) copy-start(s32[8]{0:T(128)} %param.21) | copy-start | bytes 100
  33.5 9.3 %copy-start.22 = (s32[8,1]{0,1:T(1,128)S(1)}, s32[8,1]{0,1:T(1,128)}, u32[]{:S(2)}) copy-start(s32[8,1]{0,1:T(1,128)} %param.18) | copy-start | bytes 100
  33.5 9.5 %copy-start.24 = (s32[8]{0:T(128)S(1)}, s32[8]{0:T(128)}, u32[]{:S(2)}) copy-start(s32[8]{0:T(128)} %param.20) | copy-start | bytes 100
  35.6 19.8 %all-to-all-start.6 = ((bf16[8,2,28672]{2,1,0:T(2,128)(2,1)}), bf16[8,2,28672]{2,1,0:T(2,128)(2,1)S(1)}, u32[]{:S(2)}, u32[]{:S(2)}) async-start(bf16[8,2,28672]{2,1,0:T(2,128)(2,1)} %reshape.517), calls=%async_computation.6 | async-start | bytes 1835008 | tf_op jit(solution)/shard_map/all_to_all | solution.py:23
  42.8 221.6 %all-gather.5.cloned.1.call-start = ((), (), s32[]{:S(2)}) async-start(), calls=%async_computation.14 | async-start | bytes 7798784 | tf_op jit(solution)/shard_map/all_gather | solution.py:181
  60.4 14.4 %copy-start.15 = (f32[1,64,3584]{2,1,0:T(8,128)S(1)}, f32[1,64,3584]{2,1,0:T(8,128)}, u32[]{:S(2)}) copy-start(f32[1,64,3584]{2,1,0:T(8,128)} %param.23) | copy-start | bytes 2752516
  97.1 7.5 %copy-start.16 = (f32[1,64,3584]{2,1,0:T(8,128)S(1)}, f32[1,64,3584]{2,1,0:T(8,128)}, u32[]{:S(2)}) copy-start(f32[1,64,3584]{2,1,0:T(8,128)} %param.27) | copy-start | bytes 2752516
  98.5 41.7 %all-to-all-start.1 = ((bf16[8,2,14336]{2,1,0:T(2,128)(2,1)}), bf16[8,2,14336]{2,1,0:T(2,128)(2,1)S(1)}, u32[]{:S(2)}, u32[]{:S(2)}) async-start(bf16[8,2,14336]{2,1,0:T(2,128)(2,1)} %reshape.513), calls=%async_computation.1 | async-start | bytes 917504 | tf_op jit(solution)/shard_map/all_to_all | solution.py:85
  141.0 18.4 %all-to-all-start.9 = ((bf16[8,2,28672]{2,1,0:T(2,128)(2,1)}), bf16[8,2,28672]{2,1,0:T(2,128)(2,1)S(1)}, u32[]{:S(2)}, u32[]{:S(2)}) async-start(bf16[8,2,28672]{2,1,0:T(2,128)(2,1)} %reshape.519), calls=%async_computation.10 | async-start | bytes 1835008 | tf_op jit(solution)/shard_map/all_to_all | solution.py:23
  148.2 134.9 %all-gather.3.cloned.1.call-start = ((), (), s32[]{:S(2)}) async-start(), calls=%async_computation.13 | async-start | bytes 7798784 | tf_op jit(solution)/shard_map/all_gather | solution.py:182
  163.5 15.7 %copy-start.23 = (s32[8]{0:T(128)S(1)}, s32[8]{0:T(128)}, u32[]{:S(2)}) copy-start(s32[8]{0:T(128)} %param.19) | copy-start | bytes 100
  163.5 15.7 %copy-start.17 = (bf16[128,3584]{1,0:T(8,128)(2,1)S(1)}, bf16[128,3584]{1,0:T(8,128)(2,1)}, u32[]{:S(2)}) copy-start(bf16[128,3584]{1,0:T(8,128)(2,1)} %param.17) | copy-start | bytes 2752516
  179.0 283.1 %reduce-scatter.2.cloned.1.call-start = ((), (), s32[]{:S(2)}) async-start(), calls=%async_computation.15 | async-start | bytes 15597568 | tf_op jit(solution)/shard_map/reduce_scatter | solution.py:50
  264.4 6.3 %copy-start.7 = (bf16[8,32,3584]{2,1,0:T(8,128)(2,1)S(1)}, bf16[8,32,3584]{2,1,0:T(8,128)(2,1)}, u32[]{:S(2)}) copy-start(bf16[8,32,3584]{2,1,0:T(8,128)(2,1)} %get-tuple-element.19) | copy-start | bytes 5505028
  289.0 5.1 %copy-start.19 = (bf16[256,1024]{1,0:T(8,128)(2,1)}, bf16[256,1024]{1,0:T(8,128)(2,1)S(1)}, u32[]{:S(2)}) copy-start(bf16[256,1024]{1,0:T(8,128)(2,1)S(1)} %fusion.13) | copy-start | bytes 1572868
  336.6 16.1 %copy-start.8 = (bf16[8,224,128]{2,1,0:T(8,128)(2,1)S(1)}, bf16[8,224,128]{2,1,0:T(8,128)(2,1)}, u32[]{:S(2)}) copy-start(bf16[8,224,128]{2,1,0:T(8,128)(2,1)} %get-tuple-element.29) | copy-start | bytes 1376260
  337.6 53.2 %copy-start.20 = (bf16[256,1024]{1,0:T(8,128)(2,1)S(1)}, bf16[256,1024]{1,0:T(8,128)(2,1)}, u32[]{:S(2)}) copy-start(bf16[256,1024]{1,0:T(8,128)(2,1)} %copy-done.19) | copy-start | bytes 1572868
  384.0 15.7 %all-to-all-start.11 = ((bf16[8,64,448]{2,1,0:T(8,128)(2,1)}), bf16[8,64,448]{2,1,0:T(8,128)(2,1)S(1)}, u32[]{:S(2)}, u32[]{:S(2)}) async-start(bf16[8,64,448]{2,1,0:T(8,128)(2,1)} %get-tuple-element.26), calls=%async_computation.12 | async-start | bytes 1048576 | tf_op jit(solution)/shard_map/all_to_all | solution.py:120
  400.5 33.4 %all-to-all-start.5 = ((bf16[8,32,3584]{2,1,0:T(8,128)(2,1)}), bf16[8,32,3584]{2,1,0:T(8,128)(2,1)S(1)}, u32[]{:S(2)}, u32[]{:S(2)}) async-start(bf16[8,32,3584]{2,1,0:T(8,128)(2,1)} %bitcast.134), calls=%async_computation.5 | async-start | bytes 3670016 | tf_op jit(solution)/shard_map/all_to_all | solution.py:196
  465.5 3.8 copy-start.2
  465.5 3.8 copy-start.3
  (11 other events, 17.5 us)
Sparse Core Ops, SparseCore 0:
  74.9 51.0 all-gather.4
  179.1 79.7 all-gather.2
  336.8 125.2 reduce-scatter.1
where the time goes:
time: 484 us; the launch traced here: 478 us
  blocking collectives  152 us (31%)
  local copies, waits for them, and re-layouts  92.4 us (19%)
  other arithmetic  90.6 us (19%)
  waiting for transfers between devices  52.6 us (11%)
  starting transfers between devices  43.3 us (9%)
  matrix products  32.5 us (7%)
  between operations  14.7 us (3%)
    all_to_all x1, blocking collectives, side_by_side(): lax.all_to_all(both, axis, split_axis=split_dim, concat_axis=concat_dim,...  78.7 us
    unnamed x5, other arithmetic  58.7 us
    reduce_scatter x1, waiting for transfers between devices, sum_together(): lax.psum_scatter(lines, axis, tiled=True).reshape(-1)  24.9 us
    unnamed x64, local copies, waits for them, and re-layouts  20.1 us
    reshape x1, local copies, waits for them, and re-layouts, sum_together(): jnp.pad(lines, ((0, 0), (0, span * 128 - lines.shape[1]))).reshape(-1, 128)  18.9 us
    all_to_all x1, waiting for transfers between devices, local(): lax.all_to_all(input_grad.reshape(groups, capacity * block_len, features)...  16.9 us
    concatenate x1, other arithmetic, sum_together(): lines = jnp.concatenate([b.reshape(peers, -1) for b in tiles], axis=1)  16.3 us
    all_to_all x1, blocking collectives, move_state(): lax.all_to_all(for_sending(ordered[4]), 'expert', split_axis=0, concat_ax...  16 us
  transfers between devices with their start and end apart: 9, of which 5 were waited for; matrix products, arithmetic and copies ran while one was open for 28% of the time, Pallas kernels for 0%

commit v1 on v0

v1 whole, which is shorter than its diff:
```python
import jax
import jax.numpy as jnp
from jax import lax
from jax.experimental import pallas as pl
from jax.experimental.pallas import tpu as pltpu
from jax.sharding import Mesh
from jax.sharding import PartitionSpec as P

beta_one = 0.9
beta_two = 0.95
bias_one = 1.0 - 0.9**10
bias_two = 1.0 - 0.95**10
rate_value = 0.01
decay_value = 0.1
eps_value = 1e-08

F32 = jnp.float32
BF = jnp.bfloat16
NX, NY, NC = 2, 4, 2
LANE = 128


def row_order():
    return [x * NY * NC + y * NC + c for c in range(NC) for y in range(NY) for x in range(NX)]


def inverse(order):
    back = [0] * len(order)
    for p, r in enumerate(order):
        back[r] = p
    return back


def lanes_taken(value, order):
    width = value.shape[1] // len(order)
    return jnp.concatenate([value[:, r * width : (r + 1) * width] for r in order], axis=1)


def cast_body(up_ref, down_ref, u_ref, w_ref):
    u_ref[...] = lanes_taken(up_ref[...], row_order()).astype(BF)
    w_ref[...] = down_ref[...].astype(BF)


def cast_weights(up, down):
    return pl.pallas_call(
        cast_body,
        out_shape=(jax.ShapeDtypeStruct(up.shape, BF), jax.ShapeDtypeStruct(down.shape, BF)),
        name="cast_weights",
    )(up, down)


def slot_of_block(ids_ref, own_ref, b):
    mine = ids_ref[b, 0]
    place = jnp.int32(0)
    for e in range(b):
        place = place + (ids_ref[e, 0] == mine).astype(jnp.int32)
    return own_ref[mine] * 2 + place


def dispatch_body(ids_ref, count_ref, own_ref, tok_ref, cot_ref, sx_ref, sdy_ref):
    blocks, rows, _ = tok_ref.shape
    sx_ref[...] = jnp.zeros(sx_ref.shape, BF)
    sdy_ref[...] = jnp.zeros(sdy_ref.shape, BF)
    at = lax.broadcasted_iota(jnp.int32, (rows, 1), 0)
    for b in range(blocks):
        slot = slot_of_block(ids_ref, own_ref, b)
        alive = at < count_ref[b]
        x = jnp.where(alive, tok_ref[b].astype(F32), 0.0)
        dy = jnp.where(alive, cot_ref[b].astype(F32), 0.0)
        sx_ref[slot] = lanes_taken(x, row_order()).astype(BF)
        sdy_ref[slot] = dy.astype(BF)


def smem():
    return pl.BlockSpec(memory_space=pltpu.SMEM)


def vmem():
    return pl.BlockSpec(memory_space=pltpu.VMEM)


def dispatch(ids, count, owner, tokens, cotangent):
    blocks, rows, width = tokens.shape
    out = jax.ShapeDtypeStruct((2 * blocks, rows, width), BF)
    return pl.pallas_call(
        dispatch_body,
        in_specs=[smem(), smem(), smem(), vmem(), vmem()],
        out_shape=(out, out),
        name="dispatch",
    )(ids, count, owner, tokens, cotangent)


def combine_body(ids_ref, own_ref, ret_ref, out_ref):
    for b in range(out_ref.shape[0]):
        slot = slot_of_block(ids_ref, own_ref, b)
        out_ref[b] = lanes_taken(ret_ref[slot].astype(F32), inverse(row_order())).astype(BF)


def combine(ids, owner, returned):
    slots, rows, width = returned.shape
    return pl.pallas_call(
        combine_body,
        in_specs=[smem(), smem(), vmem()],
        out_shape=jax.ShapeDtypeStruct((slots // 2, rows, width), BF),
        name="combine",
    )(ids, owner, returned)


def to_tiles(rows8):
    n = rows8.shape[1] // LANE
    return jnp.concatenate([rows8[:, i * LANE : (i + 1) * LANE] for i in range(n)], axis=0)


def from_tiles(tiles):
    n = tiles.shape[0] // 8
    return jnp.concatenate([tiles[i * 8 : (i + 1) * 8] for i in range(n)], axis=1)


def pack_body(a_ref, b_ref, c_ref, d_ref, e_ref, f_ref, out_ref):
    for i, ref in enumerate((a_ref, b_ref, c_ref)):
        out_ref[0, i] = ref[...].astype(BF)
    for i, ref in enumerate((d_ref, e_ref, f_ref)):
        out_ref[0, 3 + i] = to_tiles(ref[...]).astype(BF)


def pack_states(ups, downs, groups):
    rows, cols = ups[0].shape
    drows, dcols = downs[0].shape
    wide, tall = cols // groups, drows // groups
    up_spec = pl.BlockSpec((rows, wide), lambda i: (0, i))
    down_spec = pl.BlockSpec((tall, dcols), lambda i: (i, 0))
    return pl.pallas_call(
        pack_body,
        grid=(groups,),
        in_specs=[up_spec] * 3 + [down_spec] * 3,
        out_specs=pl.BlockSpec((1, 6, rows, wide), lambda i: (i, 0, 0, 0)),
        out_shape=jax.ShapeDtypeStruct((groups, 6, rows, wide), BF),
        name="pack_states",
    )(*ups, *downs)


def order_body(source_ref, in_ref, out_ref):
    out_ref[...] = in_ref[...]


def order_states(source, shares):
    groups, rest = shares.shape[0], shares.shape[1:]
    zeros = (0,) * len(rest)
    return pl.pallas_call(
        order_body,
        grid_spec=pltpu.PrefetchScalarGridSpec(
            num_scalar_prefetch=1,
            grid=(groups,),
            in_specs=[pl.BlockSpec((1,) + rest, lambda i, s: (s[i],) + zeros)],
            out_specs=pl.BlockSpec((1,) + rest, lambda i, s: (i,) + zeros),
        ),
        out_shape=jax.ShapeDtypeStruct(shares.shape, BF),
        name="order_states",
    )(source, shares)


def sum_body(source_ref, in_ref, out_ref):
    both = in_ref[0].astype(F32)
    out_ref[0] = (both[0] + both[1]).astype(BF)


def sum_order(source, shares):
    groups, pair, rows, wide = shares.shape
    return pl.pallas_call(
        sum_body,
        grid_spec=pltpu.PrefetchScalarGridSpec(
            num_scalar_prefetch=1,
            grid=(groups,),
            in_specs=[pl.BlockSpec((1, pair, rows, wide), lambda i, s: (s[i], 0, 0, 0))],
            out_specs=pl.BlockSpec((1, rows, wide), lambda i, s: (i, 0, 0)),
        ),
        out_shape=jax.ShapeDtypeStruct((groups, rows, wide), BF),
        name="sum_order",
    )(source, shares)


def weight_grad_body(half_ref, a_ref, ao_ref, b_ref, bo_ref, out_ref):
    dims = (((0,), (0,)), ((), ()))
    total = lax.dot_general(a_ref[...], b_ref[...], dims, preferred_element_type=F32)
    total += lax.dot_general(ao_ref[...], bo_ref[...], dims, preferred_element_type=F32)
    out_ref[...] = total.astype(BF)


def weight_grad(half, a, a_other, b, b_other, step, name):
    rows, width = a.shape
    cols = b.shape[1]
    steps = width // 2 // step
    left = pl.BlockSpec((rows, step), lambda i, h: (0, h[0] * steps + i))
    right = pl.BlockSpec((rows, cols), lambda i, h: (0, 0))
    return pl.pallas_call(
        weight_grad_body,
        grid_spec=pltpu.PrefetchScalarGridSpec(
            num_scalar_prefetch=1,
            grid=(steps,),
            in_specs=[left, left, right, right],
            out_specs=pl.BlockSpec((step, cols), lambda i, h: (i, 0)),
        ),
        out_shape=jax.ShapeDtypeStruct((width // 2, cols), BF),
        name=name,
    )(half, a, a_other, b, b_other)


def pack_up_body(in_ref, out_ref):
    value = lanes_taken(in_ref[0].astype(F32), inverse(row_order())).astype(BF)
    for i in range(out_ref.shape[0]):
        out_ref[i, 0] = value[:, i * LANE : (i + 1) * LANE]


def pack_up_grad(grad, groups):
    pair, rows, cols = grad.shape
    wide = cols // groups
    return pl.pallas_call(
        pack_up_body,
        grid=(pair,),
        in_specs=[pl.BlockSpec((1, rows, cols), lambda i: (i, 0, 0))],
        out_specs=pl.BlockSpec((groups, 1, rows, wide), lambda i: (0, i, 0, 0)),
        out_shape=jax.ShapeDtypeStruct((groups, pair, rows, wide), BF),
        name="pack_up_grad",
    )(grad)


def pack_down_body(in_ref, out_ref):
    for i in range(out_ref.shape[0]):
        out_ref[i, 0] = to_tiles(in_ref[0, i * 8 : (i + 1) * 8].astype(F32)).astype(BF)


def pack_down_grad(grad, groups):
    pair, rows, cols = grad.shape
    tall = rows // groups * cols // LANE
    return pl.pallas_call(
        pack_down_body,
        grid=(pair,),
        in_specs=[pl.BlockSpec((1, rows, cols), lambda i: (i, 0, 0))],
        out_specs=pl.BlockSpec((groups, 1, tall, LANE), lambda i: (0, i, 0, 0)),
        out_shape=jax.ShapeDtypeStruct((groups, pair, tall, LANE), BF),
        name="pack_down_grad",
    )(grad)


def adam_update(weight, moment, second, gradient):
    moment_new = beta_one * moment + (1.0 - beta_one) * gradient
    second_new = beta_two * second + (1.0 - beta_two) * gradient * gradient
    update = moment_new / bias_one / (jnp.sqrt(second_new / bias_two) + eps_value)
    return (weight - rate_value * (update + decay_value * weight), moment_new, second_new)


def adam_up_body(state_ref, grad_ref, w_ref, m_ref, v_ref):
    w, m, v = (state_ref[0, i].astype(F32) for i in range(3))
    w_ref[...], m_ref[...], v_ref[...] = adam_update(w, m, v, grad_ref[0].astype(F32))


def adam_down_body(state_ref, grad_ref, w_ref, m_ref, v_ref):
    w, m, v = (state_ref[0, i].astype(F32) for i in range(3))
    new = adam_update(w, m, v, grad_ref[0].astype(F32))
    for ref, value in zip((w_ref, m_ref, v_ref), new):
        ref[...] = from_tiles(value)


def adam(body, states, which, grad, out_block, out_index, out_shape, name):
    groups, _, rows, wide = states.shape
    out_spec = pl.BlockSpec(out_block, out_index)
    return pl.pallas_call(
        body,
        grid=(groups,),
        in_specs=[
            pl.BlockSpec((1, 3, rows, wide), lambda i: (i, which, 0, 0)),
            pl.BlockSpec((1, rows, wide), lambda i: (i, 0, 0)),
        ],
        out_specs=[out_spec] * 3,
        out_shape=[jax.ShapeDtypeStruct(out_shape, F32)] * 3,
        name=name,
    )(states, grad)


def silu_parts(pre_act):
    sigma = jax.nn.sigmoid(pre_act)
    return (pre_act * sigma, sigma * (1.0 + pre_act * (1.0 - sigma)))


def exchange(array, axis):
    return lax.all_to_all(array, axis, split_axis=0, concat_axis=0, tiled=True)


def from_partner(array):
    return lax.ppermute(array, "core", [(0, 1), (1, 0)])


def local(
    tokens,
    cotangent,
    block_expert,
    block_count,
    old_owner,
    new_owner,
    up_weight,
    down_weight,
    up_first,
    up_second,
    down_first,
    down_second,
):
    groups = lax.axis_size("expert")
    tok_rows, features = tokens.shape
    blocks = block_count.shape[0]
    rows = tok_rows // blocks
    labels = jnp.arange(groups, dtype=jnp.int32)
    incoming = jnp.sum(jnp.where(new_owner[:, None] == labels[None, :], labels[:, None], 0), axis=0)
    source = jnp.sum(jnp.where(labels[:, None] == incoming[None, :], old_owner[:, None], 0), axis=0)
    half = lax.axis_index("core").astype(jnp.int32).reshape(1)

    up_short, down_short = cast_weights(up_weight[0], down_weight[0])
    up_pair = lax.all_gather(up_short, "x", axis=0, tiled=True)
    up_mat = lax.all_gather(up_pair, ("core", "y"), axis=0, tiled=True)
    down_pair = lax.all_gather(down_short, "x", axis=0, tiled=True)
    down_mat = lax.all_gather(down_pair, ("core", "y"), axis=0, tiled=True)

    send_x, send_dy = dispatch(
        block_expert,
        block_count,
        old_owner,
        tokens.reshape(blocks, rows, features),
        cotangent.reshape(blocks, rows, features),
    )
    send_x, send_dy, _ = lax.optimization_barrier((send_x, send_dy, down_pair))
    inputs = exchange(send_x, "expert").reshape(-1, features)
    upstream = exchange(send_dy, "expert").reshape(-1, features)
    inputs_other, upstream_other = from_partner(inputs), from_partner(upstream)

    packed = pack_states(
        (up_weight[0], up_first[0], up_second[0]),
        (down_weight[0], down_first[0], down_second[0]),
        groups,
    )
    packed, _ = lax.optimization_barrier((packed, upstream))
    shares = exchange(packed, "expert")

    pre_act = jnp.dot(inputs, up_mat, preferred_element_type=F32)
    active, slopes = silu_parts(pre_act)
    hidden = active.astype(BF)
    hidden_other = from_partner(hidden)
    down_part = weight_grad(
        half, hidden, hidden_other, upstream, upstream_other, 128, "down_part"
    )
    down_sum = lax.psum_scatter(down_part, "y", scatter_dimension=0, tiled=True)
    back = lax.dot_general(upstream, down_mat, (((1,), (1,)), ((), ())), preferred_element_type=F32)
    pre_grad = (back * slopes).astype(BF)
    pre_grad_other = from_partner(pre_grad)
    up_part = weight_grad(half, inputs, inputs_other, pre_grad, pre_grad_other, 256, "up_part")
    up_sum = lax.psum_scatter(up_part, "y", scatter_dimension=0, tiled=True)
    input_grad = lax.dot_general(
        pre_grad, up_mat, (((1,), (1,)), ((), ())), preferred_element_type=F32
    ).astype(BF)

    ordered = order_states(source, shares)
    ordered, _ = lax.optimization_barrier((ordered, up_part))
    states = exchange(ordered, "expert")

    returned = exchange(input_grad.reshape(-1, rows, features), "expert")
    token_grad = combine(block_expert, old_owner, returned).reshape(tok_rows, features)

    def moved(packed_grad):
        shape = packed_grad.shape
        spread = exchange(packed_grad.reshape((-1,) + shape[2:]), ("expert", "x"))
        return exchange(sum_order(source, spread.reshape(shape)), "expert")

    down_grad = moved(pack_down_grad(down_sum.reshape(NX, -1, features), groups))
    up_grad = moved(pack_up_grad(up_sum.reshape(NX, -1, up_mat.shape[1]), groups))

    up_shape, down_shape = up_weight.shape[1:], down_weight.shape[1:]
    down_new = adam(
        adam_down_body, states, 1, down_grad,
        (down_shape[0] // groups, down_shape[1]), lambda i: (i, 0), down_shape, "adam_down",
    )
    up_new = adam(
        adam_up_body, states, 0, up_grad,
        (up_shape[0], up_shape[1] // groups), lambda i: (0, i), up_shape, "adam_up",
    )
    return (
        token_grad,
        up_new[0][None],
        down_new[0][None],
        up_new[1][None],
        up_new[2][None],
        down_new[1][None],
        down_new[2][None],
    )


def solution(mesh):
    fine = Mesh(
        mesh.devices.reshape(mesh.devices.shape[0], NX, NY, NC), ("expert", "x", "y", "core")
    )
    every = ("expert", "x", "y", "core")
    dp = ("x", "y", "core")
    state = P("expert", dp, None)
    return jax.shard_map(
        local,
        mesh=fine,
        in_specs=(P(every, None), P(every, None), P(every, None), P(every), P(), P())
        + (state,) * 6,
        out_specs=(P(every, None),) + (state,) * 6,
        check_vma=False,
    )
```

time: 484 us -> 344 us (0.71)
  blocking collectives: 152 us -> 58.3 us
  other arithmetic: 90.6 us -> 0.68 us
  local copies, waits for them, and re-layouts: 92.4 us -> 3.52 us
  waiting for transfers between devices: 52.6 us -> 127 us
  Pallas kernels: 0 us -> 63.8 us
  matrix products: 32.5 us -> 18.7 us
  starting transfers between devices: 43.3 us -> 54 us
    all_to_all x6 -> x1, blocking collectives: 152 us -> 30.3 us  [exchange(): return lax.all_to_all(array, axis, split_axis=0, concat_axis=0, tiled=True)]
    all_to_all x6 -> x8, waiting for transfers between devices: 27.6 us -> 103 us  [exchange(): return lax.all_to_all(array, axis, split_axis=0, concat_axis=0, tiled=True)]
    pallas_call x0 -> x13, Pallas kernels: none -> 63.8 us  [the longest x2 13.9 us: weight_grad(): pl.pallas_call(weight_grad_body, grid_spec=pltpu.PrefetchScalarGridSpec(n...]
    unnamed x5 -> x0, other arithmetic: 58.7 us -> none
    all_gather x0 -> x2, blocking collectives: none -> 28.1 us  [the longest x1 14.6 us: local(): up_pair = lax.all_gather(up_short, 'x', axis=0, tiled=True)]
    reduce_scatter x1 -> x2, waiting for transfers between devices: 24.9 us -> 0.01 us  [the longest x1 0.01 us: local(): down_sum = lax.psum_scatter(down_part, 'y', scatter_dimension=0, tiled=True)]
    convert_element_type x18 -> x0, local copies, waits for them, and re-layouts: 23 us -> none  [the longest x3 3.4 us: adam_update(): moment_new = beta_one * moment + (1.0 - beta_one) * gradient]
    all_gather x2, waiting for transfers between devices: 0.01 us -> 19.4 us  [the longest x1 19.4 us: local(): down_mat = lax.all_gather(down_pair, ('core', 'y'), axis=0, tiled=True)]
  transfers between devices with their start and end apart: 9 -> 16, of which waited for: 5 -> 10; matrix products, arithmetic and copies ran while one was open for 28% -> 6% of each run, Pallas kernels for 0% -> 14%
where the time goes in v1:
time: 344 us; the launch traced here: 340 us
  waiting for transfers between devices  127 us (37%)
  Pallas kernels  63.8 us (19%)
  blocking collectives  58.3 us (17%)
  starting transfers between devices  54 us (16%)
  matrix products  18.7 us (5%)
  between operations  13.9 us (4%)
  local copies, waits for them, and re-layouts  3.52 us (1%)
    all_to_all x8, waiting for transfers between devices, exchange(): return lax.all_to_all(array, axis, split_axis=0, concat_axis=0, tiled=True)  103 us
    all_to_all x8, starting transfers between devices, exchange(): return lax.all_to_all(array, axis, split_axis=0, concat_axis=0, tiled=True)  53 us
    all_to_all x1, blocking collectives, exchange(): return lax.all_to_all(array, axis, split_axis=0, concat_axis=0, tiled=True)  30.3 us
    all_gather x1, waiting for transfers between devices, local(): down_mat = lax.all_gather(down_pair, ('core', 'y'), axis=0, tiled=True)  19.4 us
    all_gather x1, blocking collectives, local(): up_pair = lax.all_gather(up_short, 'x', axis=0, tiled=True)  14.6 us
    pallas_call x2, Pallas kernels, weight_grad(): pl.pallas_call(weight_grad_body, grid_spec=pltpu.PrefetchScalarGridSpec(n...  13.9 us
    all_gather x1, blocking collectives, local(): down_pair = lax.all_gather(down_short, 'x', axis=0, tiled=True)  13.5 us
    pallas_call x2, Pallas kernels, adam(): pl.pallas_call(body, grid=(groups,), in_specs=[pl.BlockSpec((1, 3, rows,...  11.8 us
  transfers between devices with their start and end apart: 16, of which 10 were waited for; matrix products, arithmetic and copies ran while one was open for 6% of the time, Pallas kernels for 14%

profile of v1, /device:TPU:4, one launch (start us, length us, event | category | flops | bytes accessed | tf_op | source)
XLA Modules:
  0.0 340.4 jit_solution(8456066171457814170)
XLA Ops:
  9.8 14.6 %all_gather.14 = bf16[448,1024]{1,0:T(8,128)(2,1)} all-gather(bf16[224,1024]{1,0:T(8,128)(2,1)} %get-tuple-element.26), channel_id=1, replica_groups=mesh['expert'=8,'x'=2,'y'=4,'core'=2] {'x'}, dimensions={0}, use_global_device_ids=true | all-gather | bytes 1376256 | tf_op jit(solution)/shard_map/all_gather | solution.py:317
  24.4 13.5 %all_gather.12 = bf16[128,3584]{1,0:T(8,128)(2,1)} all-gather(bf16[64,3584]{1,0:T(8,128)(2,1)} %get-tuple-element.23), channel_id=1, replica_groups=mesh['expert'=8,'x'=2,'y'=4,'core'=2] {'x'}, dimensions={0}, use_global_device_ids=true | all-gather | bytes 1376256 | tf_op jit(solution)/shard_map/all_gather | solution.py:319
  42.5 30.3 %all_to_all.45 = bf16[16,16,3584]{2,1,0:T(8,128)(2,1)} all-to-all(bf16[16,16,3584]{2,1,0:T(8,128)(2,1)} %get-tuple-element.25), channel_id=1, replica_groups=mesh['expert'=8,'x'=2,'y'=4,'core'=2] {'expert'}, dimensions={0} | all-to-all | bytes 3670016 | tf_op jit(solution)/shard_map/all_to_all | solution.py:286
  72.8 6.2 %all-to-all-start = ((bf16[16,16,3584]{2,1,0:T(8,128)(2,1)}), bf16[16,16,3584]{2,1,0:T(8,128)(2,1)S(1)}, u32[]{:S(2)}, u32[]{:S(2)}) async-start(bf16[16,16,3584]{2,1,0:T(8,128)(2,1)} %get-tuple-element.24), calls=%async_computation | async-start | bytes 3670016 | tf_op jit(solution)/shard_map/all_to_all | solution.py:286
  79.0 6.7 %multiply_convert_fusion = (bf16[256,1024]{1,0:T(8,128)(2,1)S(1)}, f32[256,1024]{1,0:T(8,128)}) fusion(bf16[256,3584]{1,0:T(8,128)(2,1)} %bitcast.35, bf16[3584,1024]{1,0:T(8,128)(2,1)} %all-gather.5.cloned.1.call-done), kind=kOutput, calls=%fused_computation.3 | convolution fusion | flops 1880358912 | bytes 10747904 | tf_op jit(solution)/shard_map/dot_general | solution.py:342
  85.7 14.1 %all-to-all-done = bf16[16,16,3584]{2,1,0:T(8,128)(2,1)S(1)} async-done(((bf16[16,16,3584]{2,1,0:T(8,128)(2,1)}), bf16[16,16,3584]{2,1,0:T(8,128)(2,1)S(1)}, u32[]{:S(2)}, u32[]{:S(2)}) %all-to-all-start) | async-done | bytes 1835040 | tf_op jit(solution)/shard_map/all_to_all | solution.py:286
  99.8 19.4 %all-gather.3.cloned.1.call-done = bf16[1024,3584]{1,0:T(8,128)(2,1)} async-done(((bf16[128,3584]{1,0:T(8,128)(2,1)}), bf16[1024,3584]{1,0:T(8,128)(2,1)}) %all-gather.3.cloned.1.call-update) | async-done | bytes 7340048 | tf_op jit(solution)/shard_map/all_gather | solution.py:320
  126.9 7.6 %up_part.1 = bf16[1792,1024]{1,0:T(8,128)(2,1)} custom-call(s32[1]{0:T(128)} %bitcast.12.half_ref, bf16[256,3584]{1,0:T(8,128)(2,1)} %bitcast.36, bf16[256,3584]{1,0:T(8,128)(2,1)} %collective-permute-done.ao_ref, bf16[256,1024]{1,0:T(8,128)(2,1)} %copy-done.6, bf16[256,1024]{1,0:T(8,128)(2,1)} %collective-permute-done.1.bo_ref), custom_call_target="tpu_custom_call" | custom-call | tf_op jit(solution)/shard_map/up_part/pallas_call | solution.py:195
  140.4 6.4 %down_part.1 = bf16[512,3584]{1,0:T(8,128)(2,1)} custom-call(s32[1]{0:T(128)} %bitcast.12.half_ref, bf16[256,1024]{1,0:T(8,128)(2,1)} %copy-done.8, bf16[256,1024]{1,0:T(8,128)(2,1)} %copy-done.9, bf16[256,3584]{1,0:T(8,128)(2,1)} %bitcast.33, bf16[256,3584]{1,0:T(8,128)(2,1)} %copy-done.3), custom_call_target="tpu_custom_call" | custom-call | tf_op jit(solution)/shard_map/down_part/pallas_call | solution.py:195
  146.8 6.6 %pack_states.1 = bf16[8,6,224,128]{3,2,1,0:T(8,128)(2,1)} custom-call(f32[224,1024]{1,0:T(8,128)} %bitcast.40, f32[224,1024]{1,0:T(8,128)} %bitcast.49, f32[224,1024]{1,0:T(8,128)} %bitcast.50, f32[64,3584]{1,0:T(8,128)} %bitcast.42, f32[64,3584]{1,0:T(8,128)} %bitcast.51, f32[64,3584]{1,0:T(8,128)} %bitcast.52), custom_call_target="tpu_custom_call" | custom-call | tf_op jit(solution)/shard_map/pack_states/pallas_call | solution.py:132
  153.4 7.5 %all-to-all-start.3 = ((bf16[8,6,224,128]{3,2,1,0:T(8,128)(2,1)}), bf16[8,6,224,128]{3,2,1,0:T(8,128)(2,1)S(1)}, u32[]{:S(2)}, u32[]{:S(2)}) async-start(bf16[8,6,224,128]{3,2,1,0:T(8,128)(2,1)} %pack_states.1), calls=%async_computation.3 | async-start | bytes 5505024 | tf_op jit(solution)/shard_map/all_to_all | solution.py:286
  161.0 6.5 %convolution_convert_fusion = bf16[256,3584]{1,0:T(8,128)(2,1)} fusion(bf16[256,1024]{1,0:T(8,128)(2,1)S(1)} %copy-done.7, bf16[3584,1024]{1,0:T(8,128)(2,1)} %all-gather.5.cloned.1.call-done), kind=kOutput, calls=%fused_computation | convolution fusion | flops 1879965696 | bytes 9699328 | tf_op jit(solution)/shard_map/dot_general | solution.py:355
  167.5 26.7 %all-to-all-done.3.in_ref = bf16[8,6,224,128]{3,2,1,0:T(8,128)(2,1)S(1)} async-done(((bf16[8,6,224,128]{3,2,1,0:T(8,128)(2,1)}), bf16[8,6,224,128]{3,2,1,0:T(8,128)(2,1)S(1)}, u32[]{:S(2)}, u32[]{:S(2)}) %all-to-all-start.3) | async-done | bytes 2752544 | tf_op jit(solution)/shard_map/all_to_all | solution.py:286
  194.2 6.9 %all-to-all-start.2 = ((bf16[16,16,3584]{2,1,0:T(8,128)(2,1)}), bf16[16,16,3584]{2,1,0:T(8,128)(2,1)}, u32[]{:S(2)}, u32[]{:S(2)}) async-start(bf16[16,16,3584]{2,1,0:T(8,128)(2,1)} %bitcast.43), calls=%async_computation.2 | async-start | bytes 3670016 | tf_op jit(solution)/shard_map/all_to_all | solution.py:286
  201.8 6.7 %order_states.1 = bf16[8,6,224,128]{3,2,1,0:T(8,128)(2,1)} custom-call(s32[8]{0:T(128)} %select_reduce_fusion.source_ref, bf16[8,6,224,128]{3,2,1,0:T(8,128)(2,1)} %copy-done.1), custom_call_target="tpu_custom_call" | custom-call | tf_op jit(solution)/shard_map/order_states/pallas_call | solution.py:149
  208.5 15.3 %all-to-all-done.2.ret_ref = bf16[16,16,3584]{2,1,0:T(8,128)(2,1)} async-done(((bf16[16,16,3584]{2,1,0:T(8,128)(2,1)}), bf16[16,16,3584]{2,1,0:T(8,128)(2,1)}, u32[]{:S(2)}, u32[]{:S(2)}) %all-to-all-start.2) | async-done | bytes 1835040 | tf_op jit(solution)/shard_map/all_to_all | solution.py:286
  223.7 6.3 %all-to-all-start.4 = ((bf16[8,6,224,128]{3,2,1,0:T(8,128)(2,1)}), bf16[8,6,224,128]{3,2,1,0:T(8,128)(2,1)S(1)}, u32[]{:S(2)}, u32[]{:S(2)}) async-start(bf16[8,6,224,128]{3,2,1,0:T(8,128)(2,1)} %order_states.1), calls=%async_computation.4 | async-start | bytes 5505024 | tf_op jit(solution)/shard_map/all_to_all | solution.py:286
  232.2 29.9 %all-to-all-done.4.state_ref = bf16[8,6,224,128]{3,2,1,0:T(8,128)(2,1)S(1)} async-done(((bf16[8,6,224,128]{3,2,1,0:T(8,128)(2,1)}), bf16[8,6,224,128]{3,2,1,0:T(8,128)(2,1)S(1)}, u32[]{:S(2)}, u32[]{:S(2)}) %all-to-all-start.4) | async-done | bytes 2752544 | tf_op jit(solution)/shard_map/all_to_all | solution.py:286
  262.1 6.8 %all-to-all-start.5 = ((bf16[16,224,128]{2,1,0:T(8,128)(2,1)}), bf16[16,224,128]{2,1,0:T(8,128)(2,1)}, u32[]{:S(2)}, u32[]{:S(2)}) async-start(bf16[16,224,128]{2,1,0:T(8,128)(2,1)} %bitcast.37), calls=%async_computation.6 | async-start | bytes 1835008 | tf_op jit(solution)/shard_map/all_to_all | solution.py:286
  270.9 10.0 %all-to-all-done.5 = bf16[16,224,128]{2,1,0:T(8,128)(2,1)} async-done(((bf16[16,224,128]{2,1,0:T(8,128)(2,1)}), bf16[16,224,128]{2,1,0:T(8,128)(2,1)}, u32[]{:S(2)}, u32[]{:S(2)}) %all-to-all-start.5) | async-done | bytes 917536 | tf_op jit(solution)/shard_map/all_to_all | solution.py:286
  280.9 7.0 %all-to-all-start.7 = ((bf16[16,224,128]{2,1,0:T(8,128)(2,1)}), bf16[16,224,128]{2,1,0:T(8,128)(2,1)}, u32[]{:S(2)}, u32[]{:S(2)}) async-start(bf16[16,224,128]{2,1,0:T(8,128)(2,1)} %bitcast.38), calls=%async_computation.9 | async-start | bytes 1835008 | tf_op jit(solution)/shard_map/all_to_all | solution.py:286
  299.0 6.3 %all-to-all-start.6 = ((bf16[8,224,128]{2,1,0:T(8,128)(2,1)}), bf16[8,224,128]{2,1,0:T(8,128)(2,1)S(1)}, u32[]{:S(2)}, u32[]{:S(2)}) async-start(bf16[8,224,128]{2,1,0:T(8,128)(2,1)} %sum_order.2), calls=%async_computation.7 | async-start | bytes 917504 | tf_op jit(solution)/shard_map/all_to_all | solution.py:286
  312.6 6.1 %all-to-all-start.8 = ((bf16[8,224,128]{2,1,0:T(8,128)(2,1)}), bf16[8,224,128]{2,1,0:T(8,128)(2,1)S(1)}, u32[]{:S(2)}, u32[]{:S(2)}) async-start(bf16[8,224,128]{2,1,0:T(8,128)(2,1)} %sum_order.3), calls=%async_computation.10 | async-start | bytes 917504 | tf_op jit(solution)/shard_map/all_to_all | solution.py:286
  321.3 5.9 %adam_up.1 = (f32[224,1024]{1,0:T(8,128)}, f32[224,1024]{1,0:T(8,128)}, f32[224,1024]{1,0:T(8,128)}) custom-call(bf16[8,6,224,128]{3,2,1,0:T(8,128)(2,1)} %copy-done, bf16[8,224,128]{2,1,0:T(8,128)(2,1)} %copy-done.4), custom_call_target="tpu_custom_call" | custom-call | tf_op jit(solution)/shard_map/adam_up/pallas_call | solution.py:267
  (60 shorter events, 53.4 us)
Async XLA Ops:
  7.2 71.8 %all-gather.5.cloned.1.call-start = ((), (), s32[]{:S(2)}) async-start(), calls=%async_computation.12 | async-start | bytes 8257536 | tf_op jit(solution)/shard_map/all_gather | solution.py:318
  9.8 28.2 %copy-start.11 = (s32[8,1]{0,1:T(1,128)S(1)}, s32[8,1]{0,1:T(1,128)}, u32[]{:S(2)}) copy-start(s32[8,1]{0,1:T(1,128)} %param.14) | copy-start | bytes 100
  24.4 94.9 %all-gather.3.cloned.1.call-start = ((), (), s32[]{:S(2)}) async-start(), calls=%async_computation.11 | async-start | bytes 8257536 | tf_op jit(solution)/shard_map/all_gather | solution.py:320
  72.8 27.0 %all-to-all-start = ((bf16[16,16,3584]{2,1,0:T(8,128)(2,1)}), bf16[16,16,3584]{2,1,0:T(8,128)(2,1)S(1)}, u32[]{:S(2)}, u32[]{:S(2)}) async-start(bf16[16,16,3584]{2,1,0:T(8,128)(2,1)} %get-tuple-element.24), calls=%async_computation | async-start | bytes 3670016 | tf_op jit(solution)/shard_map/all_to_all | solution.py:286
  79.0 151.1 %reduce-scatter.3.cloned.1.call-start = ((), (), s32[]{:S(2)}) async-start(), calls=%async_computation.13 | async-start | bytes 4587520 | tf_op jit(solution)/shard_map/reduce_scatter | solution.py:354
  79.0 46.1 %collective-permute-start = (bf16[256,3584]{1,0:T(8,128)(2,1)}, bf16[256,3584]{1,0:T(8,128)(2,1)}, u32[]{:S(2)}, u32[]{:S(2)}) collective-permute-start(bf16[256,3584]{1,0:T(8,128)(2,1)} %bitcast.34), channel_id=1, source_target_pairs={{0,1},{1,0},{2,3},{3,2},{4,5},{5,4},{6,7},{7,6},{8,9},{9,8},{10,11... | collective-permute-start | bytes 5505032 | tf_op jit(solution)/shard_map/ppermute | solution.py:290
  85.7 49.2 %copy-start.8 = (bf16[256,1024]{1,0:T(8,128)(2,1)}, bf16[256,1024]{1,0:T(8,128)(2,1)S(1)}, u32[]{:S(2)}) copy-start(bf16[256,1024]{1,0:T(8,128)(2,1)S(1)} %get-tuple-element.35.a_ref) | copy-start | bytes 1572868
  99.8 34.7 %copy-start.2 = (bf16[16,16,3584]{2,1,0:T(8,128)(2,1)}, bf16[16,16,3584]{2,1,0:T(8,128)(2,1)S(1)}, u32[]{:S(2)}) copy-start(bf16[16,16,3584]{2,1,0:T(8,128)(2,1)S(1)} %all-to-all-done) | copy-start | bytes 5505028
  124.7 2.1 collective-permute-start.1
  134.5 134.4 %reduce-scatter.5.cloned.1.call-start = ((), (), s32[]{:S(2)}) async-start(), calls=%async_computation.14 | async-start | bytes 4587520 | tf_op jit(solution)/shard_map/reduce_scatter | solution.py:349
  134.5 3.9 %collective-permute-start.3 = (bf16[256,3584]{1,0:T(8,128)(2,1)S(1)}, bf16[256,3584]{1,0:T(8,128)(2,1)S(1)}, u32[]{:S(2)}, u32[]{:S(2)}) collective-permute-start(bf16[256,3584]{1,0:T(8,128)(2,1)S(1)} %bitcast.32), channel_id=1, source_target_pairs={{0,1},{1,0},{2,3},{3,2},{4,5},{5,4},{6,7},{7,6},{8,9},{9,8},{10,11... | collective-permute-start | bytes 5505032 | tf_op jit(solution)/shard_map/ppermute | solution.py:290
  134.9 4.8 %collective-permute-start.2 = (bf16[256,1024]{1,0:T(8,128)(2,1)S(1)}, bf16[256,1024]{1,0:T(8,128)(2,1)S(1)}, u32[]{:S(2)}, u32[]{:S(2)}) collective-permute-start(bf16[256,1024]{1,0:T(8,128)(2,1)S(1)} %get-tuple-element.35.a_ref), channel_id=1, source_target_pairs={{0,1},{1,0},{2,3},{3,2},{4,5},{5,4},{6,7},{7,6},{8,9},{9,8},{10,11... | collective-permute-start | bytes 1572872 | tf_op jit(solution)/shard_map/ppermute | solution.py:290
  153.4 40.8 %all-to-all-start.3 = ((bf16[8,6,224,128]{3,2,1,0:T(8,128)(2,1)}), bf16[8,6,224,128]{3,2,1,0:T(8,128)(2,1)S(1)}, u32[]{:S(2)}, u32[]{:S(2)}) async-start(bf16[8,6,224,128]{3,2,1,0:T(8,128)(2,1)} %pack_states.1), calls=%async_computation.3 | async-start | bytes 5505024 | tf_op jit(solution)/shard_map/all_to_all | solution.py:286
  167.5 33.6 %copy-start.12 = (s32[8]{0:T(128)S(1)}, s32[8]{0:T(128)}, u32[]{:S(2)}) copy-start(s32[8]{0:T(128)} %param.17) | copy-start | bytes 100
  167.5 33.7 %copy-start.10 = (s32[8]{0:T(128)S(1)}, s32[8]{0:T(128)}, u32[]{:S(2)}) copy-start(s32[8]{0:T(128)} %own_ref.3) | copy-start | bytes 100
  194.2 7.6 %copy-start.1 = (bf16[8,6,224,128]{3,2,1,0:T(8,128)(2,1)}, bf16[8,6,224,128]{3,2,1,0:T(8,128)(2,1)S(1)}, u32[]{:S(2)}) copy-start(bf16[8,6,224,128]{3,2,1,0:T(8,128)(2,1)S(1)} %all-to-all-done.3.in_ref) | copy-start | bytes 8257540
  194.2 29.5 %all-to-all-start.2 = ((bf16[16,16,3584]{2,1,0:T(8,128)(2,1)}), bf16[16,16,3584]{2,1,0:T(8,128)(2,1)}, u32[]{:S(2)}, u32[]{:S(2)}) async-start(bf16[16,16,3584]{2,1,0:T(8,128)(2,1)} %bitcast.43), calls=%async_computation.2 | async-start | bytes 3670016 | tf_op jit(solution)/shard_map/all_to_all | solution.py:286
  223.7 38.4 %all-to-all-start.4 = ((bf16[8,6,224,128]{3,2,1,0:T(8,128)(2,1)}), bf16[8,6,224,128]{3,2,1,0:T(8,128)(2,1)S(1)}, u32[]{:S(2)}, u32[]{:S(2)}) async-start(bf16[8,6,224,128]{3,2,1,0:T(8,128)(2,1)} %order_states.1), calls=%async_computation.4 | async-start | bytes 5505024 | tf_op jit(solution)/shard_map/all_to_all | solution.py:286
  262.1 18.8 %copy-start = (bf16[8,6,224,128]{3,2,1,0:T(8,128)(2,1)}, bf16[8,6,224,128]{3,2,1,0:T(8,128)(2,1)S(1)}, u32[]{:S(2)}) copy-start(bf16[8,6,224,128]{3,2,1,0:T(8,128)(2,1)S(1)} %all-to-all-done.4.state_ref) | copy-start | bytes 8257540
  262.1 18.8 %all-to-all-start.5 = ((bf16[16,224,128]{2,1,0:T(8,128)(2,1)}), bf16[16,224,128]{2,1,0:T(8,128)(2,1)}, u32[]{:S(2)}, u32[]{:S(2)}) async-start(bf16[16,224,128]{2,1,0:T(8,128)(2,1)} %bitcast.37), calls=%async_computation.6 | async-start | bytes 1835008 | tf_op jit(solution)/shard_map/all_to_all | solution.py:286
  280.9 18.1 %all-to-all-start.7 = ((bf16[16,224,128]{2,1,0:T(8,128)(2,1)}), bf16[16,224,128]{2,1,0:T(8,128)(2,1)}, u32[]{:S(2)}, u32[]{:S(2)}) async-start(bf16[16,224,128]{2,1,0:T(8,128)(2,1)} %bitcast.38), calls=%async_computation.9 | async-start | bytes 1835008 | tf_op jit(solution)/shard_map/all_to_all | solution.py:286
  299.0 13.5 %all-to-all-start.6 = ((bf16[8,224,128]{2,1,0:T(8,128)(2,1)}), bf16[8,224,128]{2,1,0:T(8,128)(2,1)S(1)}, u32[]{:S(2)}, u32[]{:S(2)}) async-start(bf16[8,224,128]{2,1,0:T(8,128)(2,1)} %sum_order.2), calls=%async_computation.7 | async-start | bytes 917504 | tf_op jit(solution)/shard_map/all_to_all | solution.py:286
  312.6 8.8 %copy-start.4 = (bf16[8,224,128]{2,1,0:T(8,128)(2,1)}, bf16[8,224,128]{2,1,0:T(8,128)(2,1)S(1)}, u32[]{:S(2)}) copy-start(bf16[8,224,128]{2,1,0:T(8,128)(2,1)S(1)} %all-to-all-done.6.grad_ref) | copy-start | bytes 1376260
  312.6 14.7 %all-to-all-start.8 = ((bf16[8,224,128]{2,1,0:T(8,128)(2,1)}), bf16[8,224,128]{2,1,0:T(8,128)(2,1)S(1)}, u32[]{:S(2)}, u32[]{:S(2)}) async-start(bf16[8,224,128]{2,1,0:T(8,128)(2,1)} %sum_order.3), calls=%async_computation.10 | async-start | bytes 917504 | tf_op jit(solution)/shard_map/all_to_all | solution.py:286
  (5 other events, 12.5 us)
Sparse Core Ops, SparseCore 0:
  24.5 47.5 all-gather.4
  73.8 45.3 all-gather.2
  134.6 42.6 reduce-scatter.2
  179.6 42.2 reduce-scatter.4

commit v2 on v1

v2 whole, which is shorter than its diff:
```python
import jax
import jax.numpy as jnp
from jax import lax
from jax.experimental import pallas as pl
from jax.experimental.pallas import tpu as pltpu
from jax.sharding import Mesh
from jax.sharding import PartitionSpec as P


beta_one = 0.9
beta_two = 0.95
bias_one = 1.0 - 0.9**10
bias_two = 1.0 - 0.95**10
rate_value = 0.01
decay_value = 0.1
eps_value = 1e-08

F32 = jnp.float32
BF = jnp.bfloat16
NX, NY, NC = 2, 4, 2
LANE = 128


def row_order():
    return [x * NY * NC + y * NC + c for c in range(NC) for y in range(NY) for x in range(NX)]


def inverse(order):
    back = [0] * len(order)
    for p, r in enumerate(order):
        back[r] = p
    return back


def lanes_taken(value, order):
    width = value.shape[1] // len(order)
    return jnp.concatenate([value[:, r * width : (r + 1) * width] for r in order], axis=1)


def cast_body(up_ref, down_ref, u_ref, w_ref):
    u_ref[...] = lanes_taken(up_ref[...], row_order()).astype(BF)
    w_ref[...] = down_ref[...].astype(BF)


def cast_weights(up, down):
    return pl.pallas_call(
        cast_body,
        out_shape=(jax.ShapeDtypeStruct(up.shape, BF), jax.ShapeDtypeStruct(down.shape, BF)),
        name="cast_weights",
    )(up, down)


def slot_of_block(ids_ref, own_ref, b):
    mine = ids_ref[b, 0]
    place = jnp.int32(0)
    for e in range(b):
        place = place + (ids_ref[e, 0] == mine).astype(jnp.int32)
    return own_ref[mine] * 2 + place


def dispatch_body(ids_ref, count_ref, own_ref, tok_ref, cot_ref, sx_ref, sdy_ref):
    blocks, rows, _ = tok_ref.shape
    sx_ref[...] = jnp.zeros(sx_ref.shape, BF)
    sdy_ref[...] = jnp.zeros(sdy_ref.shape, BF)
    at = lax.broadcasted_iota(jnp.int32, (rows, 1), 0)
    for b in range(blocks):
        slot = slot_of_block(ids_ref, own_ref, b)
        alive = at < count_ref[b]
        x = jnp.where(alive, tok_ref[b].astype(F32), 0.0)
        dy = jnp.where(alive, cot_ref[b].astype(F32), 0.0)
        sx_ref[slot] = lanes_taken(x, row_order()).astype(BF)
        sdy_ref[slot] = dy.astype(BF)


def smem():
    return pl.BlockSpec(memory_space=pltpu.SMEM)


def vmem():
    return pl.BlockSpec(memory_space=pltpu.VMEM)


def dispatch(ids, count, owner, tokens, cotangent):
    blocks, rows, width = tokens.shape
    out = jax.ShapeDtypeStruct((2 * blocks, rows, width), BF)
    return pl.pallas_call(
        dispatch_body,
        in_specs=[smem(), smem(), smem(), vmem(), vmem()],
        out_shape=(out, out),
        name="dispatch",
    )(ids, count, owner, tokens, cotangent)


def combine_body(ids_ref, own_ref, ret_ref, out_ref):
    for b in range(out_ref.shape[0]):
        slot = slot_of_block(ids_ref, own_ref, b)
        out_ref[b] = lanes_taken(ret_ref[slot].astype(F32), inverse(row_order())).astype(BF)


def combine(ids, owner, returned):
    slots, rows, width = returned.shape
    return pl.pallas_call(
        combine_body,
        in_specs=[smem(), smem(), vmem()],
        out_shape=jax.ShapeDtypeStruct((slots // 2, rows, width), BF),
        name="combine",
    )(ids, owner, returned)


def to_tiles(rows8):
    n = rows8.shape[1] // LANE
    return jnp.concatenate([rows8[:, i * LANE : (i + 1) * LANE] for i in range(n)], axis=0)


def from_tiles(tiles):
    n = tiles.shape[0] // 8
    return jnp.concatenate([tiles[i * 8 : (i + 1) * 8] for i in range(n)], axis=1)


def pack_body(a_ref, b_ref, c_ref, d_ref, e_ref, f_ref, out_ref):
    for g in range(out_ref.shape[0]):
        for i, ref in enumerate((a_ref, b_ref, c_ref)):
            out_ref[g, i] = ref[:, g * LANE : (g + 1) * LANE].astype(BF)
        for i, ref in enumerate((d_ref, e_ref, f_ref)):
            out_ref[g, 3 + i] = to_tiles(ref[g * 8 : (g + 1) * 8]).astype(BF)


def pack_states(ups, downs, groups):
    rows, cols = ups[0].shape
    return pl.pallas_call(
        pack_body,
        out_shape=jax.ShapeDtypeStruct((groups, 6, rows, cols // groups), BF),
        name="pack_states",
    )(*ups, *downs)


def order_body(source_ref, in_ref, out_ref):
    for g in range(out_ref.shape[0]):
        out_ref[g] = in_ref[source_ref[g]]


def order_states(source, shares):
    return pl.pallas_call(
        order_body,
        in_specs=[smem(), vmem()],
        out_shape=jax.ShapeDtypeStruct(shares.shape, BF),
        name="order_states",
    )(source, shares)


def sum_body(source_ref, in_ref, out_ref):
    for g in range(out_ref.shape[0]):
        both = in_ref[source_ref[g]].astype(F32)
        out_ref[g] = (both[0] + both[1]).astype(BF)


def sum_order(source, shares):
    groups, _, rows, wide = shares.shape
    return pl.pallas_call(
        sum_body,
        in_specs=[smem(), vmem()],
        out_shape=jax.ShapeDtypeStruct((groups, rows, wide), BF),
        name="sum_order",
    )(source, shares)


def weight_grad_body(half_ref, a_ref, ao_ref, b_ref, bo_ref, out_ref):
    dims = (((0,), (0,)), ((), ()))
    total = lax.dot_general(a_ref[...], b_ref[...], dims, preferred_element_type=F32)
    total += lax.dot_general(ao_ref[...], bo_ref[...], dims, preferred_element_type=F32)
    out_ref[...] = total.astype(BF)


def weight_grad(half, a, a_other, b, b_other, step):
    rows, width = a.shape
    cols = b.shape[1]
    steps = width // 2 // step
    left = pl.BlockSpec((rows, step), lambda i, h: (0, h[0] * steps + i))
    right = pl.BlockSpec((rows, cols), lambda i, h: (0, 0))
    return pl.pallas_call(
        weight_grad_body,
        grid_spec=pltpu.PrefetchScalarGridSpec(
            num_scalar_prefetch=1,
            grid=(steps,),
            in_specs=[left, left, right, right],
            out_specs=pl.BlockSpec((step, cols), lambda i, h: (i, 0)),
        ),
        out_shape=jax.ShapeDtypeStruct((width // 2, cols), BF),
    )(half, a, a_other, b, b_other)


def pack_up_body(in_ref, out_ref):
    for x in range(in_ref.shape[0]):
        value = lanes_taken(in_ref[x].astype(F32), inverse(row_order())).astype(BF)
        for i in range(out_ref.shape[0]):
            out_ref[i, x] = value[:, i * LANE : (i + 1) * LANE]


def pack_down_body(in_ref, out_ref):
    for x in range(in_ref.shape[0]):
        for i in range(out_ref.shape[0]):
            out_ref[i, x] = to_tiles(in_ref[x, i * 8 : (i + 1) * 8].astype(F32)).astype(BF)


def pack_grad(body, grad, groups):
    pair, rows, cols = grad.shape
    return pl.pallas_call(
        body,
        out_shape=jax.ShapeDtypeStruct((groups, pair, rows * cols // groups // LANE, LANE), BF),
    )(grad)


def adam_update(weight, moment, second, gradient):
    moment_new = beta_one * moment + (1.0 - beta_one) * gradient
    second_new = beta_two * second + (1.0 - beta_two) * gradient * gradient
    update = moment_new / bias_one / (jnp.sqrt(second_new / bias_two) + eps_value)
    return (weight - rate_value * (update + decay_value * weight), moment_new, second_new)


def adam_share(state_ref, grad_ref, g):
    w, m, v = (state_ref[g, i].astype(F32) for i in range(3))
    return adam_update(w, m, v, grad_ref[g].astype(F32))


def adam_up_body(state_ref, grad_ref, *outs):
    for g in range(grad_ref.shape[0]):
        for ref, value in zip(outs, adam_share(state_ref, grad_ref, g)):
            ref[:, g * LANE : (g + 1) * LANE] = value


def adam_down_body(state_ref, grad_ref, *outs):
    for g in range(grad_ref.shape[0]):
        for ref, value in zip(outs, adam_share(state_ref, grad_ref, g)):
            ref[g * 8 : (g + 1) * 8] = from_tiles(value)


def adam(body, states, which, grad, shape):
    groups, _, rows, wide = states.shape
    full = pl.BlockSpec(shape, lambda i: (0, 0))
    return pl.pallas_call(
        body,
        grid=(1,),
        in_specs=[
            pl.BlockSpec((groups, 3, rows, wide), lambda i: (0, which, 0, 0)),
            pl.BlockSpec((groups, rows, wide), lambda i: (0, 0, 0)),
        ],
        out_specs=[full] * 3,
        out_shape=[jax.ShapeDtypeStruct(shape, F32)] * 3,
    )(states, grad)


def silu_parts(pre_act):
    sigma = jax.nn.sigmoid(pre_act)
    return (pre_act * sigma, sigma * (1.0 + pre_act * (1.0 - sigma)))


def exchange(array, axis):
    return lax.all_to_all(array, axis, split_axis=0, concat_axis=0, tiled=True)


def from_partner(array):
    return lax.ppermute(array, "core", [(0, 1), (1, 0)])


def step(
    tokens,
    cotangent,
    block_expert,
    block_count,
    old_owner,
    new_owner,
    up_weight,
    down_weight,
    up_first,
    up_second,
    down_first,
    down_second,
):
    groups = lax.axis_size("expert")
    tok_rows, features = tokens.shape
    blocks = block_count.shape[0]
    rows = tok_rows // blocks
    labels = jnp.arange(groups, dtype=jnp.int32)
    incoming = jnp.sum(jnp.where(new_owner[:, None] == labels[None, :], labels[:, None], 0), axis=0)
    source = jnp.sum(jnp.where(labels[:, None] == incoming[None, :], old_owner[:, None], 0), axis=0)
    half = lax.axis_index("core").astype(jnp.int32).reshape(1)

    up_short, down_short = cast_weights(up_weight[0], down_weight[0])
    up_mat = lax.all_gather(up_short, ("core", "y", "x"), axis=0, tiled=True)
    down_pair = lax.all_gather(down_short, "x", axis=0, tiled=True)
    down_mat = lax.all_gather(down_pair, ("core", "y"), axis=0, tiled=True)

    packed = pack_states(
        (up_weight[0], up_first[0], up_second[0]),
        (down_weight[0], down_first[0], down_second[0]),
        groups,
    )
    packed, _ = lax.optimization_barrier((packed, down_pair))
    shares = exchange(packed, "expert")

    send_x, send_dy = dispatch(
        block_expert,
        block_count,
        old_owner,
        tokens.reshape(blocks, rows, features),
        cotangent.reshape(blocks, rows, features),
    )
    send_x, shares = lax.optimization_barrier((send_x, shares))
    inputs = exchange(send_x, "expert")
    send_dy, inputs = lax.optimization_barrier((send_dy, inputs))
    inputs = inputs.reshape(-1, features)
    upstream = exchange(send_dy, "expert").reshape(-1, features)
    inputs_other, upstream_other = from_partner(inputs), from_partner(upstream)

    ordered = order_states(source, shares)
    ordered, upstream = lax.optimization_barrier((ordered, upstream))
    states = exchange(ordered, "expert")

    pre_act = jnp.dot(inputs, up_mat, preferred_element_type=F32)
    active, slopes = silu_parts(pre_act)
    hidden = active.astype(BF)
    hidden_other = from_partner(hidden)
    down_part = weight_grad(half, hidden, hidden_other, upstream, upstream_other, 128)
    down_sum = lax.psum_scatter(down_part, "y", scatter_dimension=0, tiled=True)
    upstream, _ = lax.optimization_barrier((upstream, down_part))
    back = lax.dot_general(upstream, down_mat, (((1,), (1,)), ((), ())), preferred_element_type=F32)
    pre_grad = (back * slopes).astype(BF)
    pre_grad_other = from_partner(pre_grad)
    up_part = weight_grad(half, inputs, inputs_other, pre_grad, pre_grad_other, 256)
    up_sum = lax.psum_scatter(up_part, "y", scatter_dimension=0, tiled=True)
    pre_grad, up_part = lax.optimization_barrier((pre_grad, up_part))
    input_grad = lax.dot_general(
        pre_grad, up_mat, (((1,), (1,)), ((), ())), preferred_element_type=F32
    ).astype(BF)
    input_grad, states = lax.optimization_barrier((input_grad, states))
    returned = exchange(input_grad.reshape(-1, rows, features), "expert")
    token_grad = combine(block_expert, old_owner, returned).reshape(tok_rows, features)

    def moved(packed_grad):
        shape = packed_grad.shape
        spread = exchange(packed_grad.reshape((-1,) + shape[2:]), ("expert", "x"))
        ordered_grad = sum_order(source, spread.reshape(shape))
        return exchange(ordered_grad, "expert")

    up_shape, down_shape = up_weight.shape[1:], down_weight.shape[1:]
    down_packed = pack_grad(pack_down_body, down_sum.reshape(NX, -1, features), groups)
    down_grad = moved(down_packed)
    down_new = adam(adam_down_body, states, 1, down_grad, down_shape)

    up_sum, down_new, token_grad = lax.optimization_barrier((up_sum, down_new, token_grad))
    up_packed = pack_grad(pack_up_body, up_sum.reshape(NX, -1, up_shape[1]), groups)
    up_grad = moved(up_packed)
    up_new = adam(adam_up_body, states, 0, up_grad, up_shape)
    return (
        token_grad,
        up_new[0][None],
        down_new[0][None],
        up_new[1][None],
        up_new[2][None],
        down_new[1][None],
        down_new[2][None],
    )


def solution(mesh):
    fine = Mesh(
        mesh.devices.reshape(mesh.devices.shape[0], NX, NY, NC), ("expert", "x", "y", "core")
    )
    every = ("expert", "x", "y", "core")
    dp = ("x", "y", "core")
    state = P("expert", dp, None)
    return jax.shard_map(
        step,
        mesh=fine,
        in_specs=(P(every, None), P(every, None), P(every, None), P(every), P(), P())
        + (state,) * 6,
        out_specs=(P(every, None),) + (state,) * 6,
        check_vma=False,
    )
```

time: 344 us -> 343 us (level)
  blocking collectives: 58.3 us -> 110 us
  waiting for transfers between devices: 127 us -> 107 us
  starting transfers between devices: 54 us -> 36.5 us
  Pallas kernels: 63.8 us -> 47.3 us
    all_to_all x1 -> x4, blocking collectives: 30.3 us -> 93.9 us  [exchange(): return lax.all_to_all(array, axis, split_axis=0, concat_axis=0, tiled=True)]
    all_gather x2, waiting for transfers between devices: 19.4 us -> 0.01 us  [the longest x1 0.01 us: step(): up_mat = lax.all_gather(up_short, ('core', 'y', 'x'), axis=0, tiled=True)]
    reduce_scatter x2, waiting for transfers between devices: 0.01 us -> 17.9 us  [the longest x1 17.9 us: step(): down_sum = lax.psum_scatter(down_part, 'y', scatter_dimension=0, tiled=True)]
    all_to_all x8 -> x5, starting transfers between devices: 53 us -> 35.3 us  [exchange(): return lax.all_to_all(array, axis, split_axis=0, concat_axis=0, tiled=True)]
    pallas_call x8, Pallas kernels: 40.7 us -> 24.2 us  [the longest x2 7.32 us: adam(): pl.pallas_call(body, grid=(1,), in_specs=[pl.BlockSpec((groups, 3, rows,...]
    all_to_all x8 -> x5, waiting for transfers between devices: 103 us -> 87.2 us  [exchange(): return lax.all_to_all(array, axis, split_axis=0, concat_axis=0, tiled=True)]
    all_gather x2 -> x1, blocking collectives: 28.1 us -> 16 us  [step(): down_pair = lax.all_gather(down_short, 'x', axis=0, tiled=True)]
    ppermute x4, waiting for transfers between devices: 5.07 us -> 1.54 us  [from_partner(): return lax.ppermute(array, 'core', [(0, 1), (1, 0)])]
  transfers between devices with their start and end apart: 16 -> 13, of which waited for: 10 -> 7; matrix products, arithmetic and copies ran while one was open for 6% -> 6% of each run, Pallas kernels for 14% -> 11%
where the time goes in v2:
time: 343 us; the launch traced here: 339 us
  blocking collectives  110 us (32%)
  waiting for transfers between devices  107 us (31%)
  Pallas kernels  47.3 us (14%)
  starting transfers between devices  36.5 us (11%)
  matrix products  19.2 us (6%)
  between operations  13.8 us (4%)
  local copies, waits for them, and re-layouts  5.08 us (1%)
    all_to_all x4, blocking collectives, exchange(): return lax.all_to_all(array, axis, split_axis=0, concat_axis=0, tiled=True)  93.9 us
    all_to_all x5, waiting for transfers between devices, exchange(): return lax.all_to_all(array, axis, split_axis=0, concat_axis=0, tiled=True)  87.2 us
    all_to_all x5, starting transfers between devices, exchange(): return lax.all_to_all(array, axis, split_axis=0, concat_axis=0, tiled=True)  35.3 us
    reduce_scatter x1, waiting for transfers between devices, step(): down_sum = lax.psum_scatter(down_part, 'y', scatter_dimension=0, tiled=True)  17.9 us
    all_gather x1, blocking collectives, step(): down_pair = lax.all_gather(down_short, 'x', axis=0, tiled=True)  16 us
    pallas_call x2, Pallas kernels, weight_grad(): pl.pallas_call(weight_grad_body, grid_spec=pltpu.PrefetchScalarGridSpec(n...  13.9 us
    pallas_call x2, Pallas kernels, adam(): pl.pallas_call(body, grid=(1,), in_specs=[pl.BlockSpec((groups, 3, rows,...  7.32 us
  transfers between devices with their start and end apart: 13, of which 7 were waited for; matrix products, arithmetic and copies ran while one was open for 6% of the time, Pallas kernels for 11%

profile of v2, /device:TPU:4, one launch (start us, length us, event | category | flops | bytes accessed | tf_op | source)
XLA Modules:
  0.0 339.2 jit_solution(6821312989988181430)
XLA Ops:
  9.9 16.0 %all_gather.9 = bf16[128,3584]{1,0:T(8,128)(2,1)} all-gather(bf16[64,3584]{1,0:T(8,128)(2,1)} %get-tuple-element.35), channel_id=1, replica_groups=mesh['expert'=8,'x'=2,'y'=4,'core'=2] {'x'}, dimensions={0}, use_global_device_ids=true | all-gather | bytes 1376256 | tf_op jit(solution)/shard_map/all_gather | solution.py:290
  25.9 4.6 %pack_states.1 = bf16[8,6,224,128]{3,2,1,0:T(8,128)(2,1)} custom-call(f32[224,1024]{1,0:T(8,128)} %bitcast.38, f32[224,1024]{1,0:T(8,128)} %bitcast.47, f32[224,1024]{1,0:T(8,128)} %bitcast.48, f32[64,3584]{1,0:T(8,128)} %bitcast.40, f32[64,3584]{1,0:T(8,128)} %bitcast.49, f32[64,3584]{1,0:T(8,128)} %bitcast.50), custom_call_target="tpu_custom_call" | custom-call | tf_op jit(solution)/shard_map/pack_states/pallas_call | solution.py:130
  30.5 9.6 %all-to-all-start = ((bf16[8,6,224,128]{3,2,1,0:T(8,128)(2,1)}), bf16[8,6,224,128]{3,2,1,0:T(8,128)(2,1)S(1)}, u32[]{:S(2)}, u32[]{:S(2)}) async-start(bf16[8,6,224,128]{3,2,1,0:T(8,128)(2,1)} %pack_states.1), calls=%async_computation | async-start | bytes 5505024 | tf_op jit(solution)/shard_map/all_to_all | solution.py:258
  40.8 3.9 %dispatch.1 = (bf16[16,16,3584]{2,1,0:T(8,128)(2,1)}, bf16[16,16,3584]{2,1,0:T(8,128)(2,1)}) custom-call(s32[8,1]{1,0:T(8,128)} %copy.21.ids_ref, s32[8]{0:T(128)} %count_ref.1, s32[8]{0:T(128)} %own_ref.3, bf16[8,16,3584]{2,1,0:T(8,128)(2,1)} %bitcast.42, bf16[8,16,3584]{2,1,0:T(8,128)(2,1)} %bitcast.43), custom_call_target="tpu_custom_call" | custom-call | tf_op jit(solution)/shard_map/dispatch/pallas_call | solution.py:86
  44.6 42.3 %all-to-all-done.in_ref = bf16[8,6,224,128]{3,2,1,0:T(8,128)(2,1)S(1)} async-done(((bf16[8,6,224,128]{3,2,1,0:T(8,128)(2,1)}), bf16[8,6,224,128]{3,2,1,0:T(8,128)(2,1)S(1)}, u32[]{:S(2)}, u32[]{:S(2)}) %all-to-all-start) | async-done | bytes 2752544 | tf_op jit(solution)/shard_map/all_to_all | solution.py:258
  86.9 34.2 %all_to_all.45 = bf16[16,16,3584]{2,1,0:T(8,128)(2,1)} all-to-all(bf16[16,16,3584]{2,1,0:T(8,128)(2,1)} %get-tuple-element.37), channel_id=1, replica_groups=mesh['expert'=8,'x'=2,'y'=4,'core'=2] {'expert'}, dimensions={0} | all-to-all | bytes 3670016 | tf_op jit(solution)/shard_map/all_to_all | solution.py:258
  121.0 27.4 %all_to_all.46 = bf16[16,16,3584]{2,1,0:T(8,128)(2,1)} all-to-all(bf16[16,16,3584]{2,1,0:T(8,128)(2,1)S(1)} %copy-done.6), channel_id=1, replica_groups=mesh['expert'=8,'x'=2,'y'=4,'core'=2] {'expert'}, dimensions={0} | all-to-all | bytes 3670016 | tf_op jit(solution)/shard_map/all_to_all | solution.py:258
  148.4 6.7 %multiply_convert_fusion = (bf16[256,1024]{1,0:T(8,128)(2,1)S(1)}, f32[256,1024]{1,0:T(8,128)}) fusion(bf16[256,3584]{1,0:T(8,128)(2,1)} %bitcast.31, bf16[3584,1024]{1,0:T(8,128)(2,1)} %all-gather.3.cloned.1.call-done), kind=kOutput, calls=%fused_computation.3 | convolution fusion | flops 1880358912 | bytes 10747904 | tf_op jit(solution)/shard_map/dot_general | solution.py:319
  161.2 6.4 %shard_map.171 = bf16[512,3584]{1,0:T(8,128)(2,1)} custom-call(s32[1]{0:T(128)} %bitcast.half_ref, bf16[256,1024]{1,0:T(8,128)(2,1)} %copy-done.9, bf16[256,1024]{1,0:T(8,128)(2,1)} %copy-done.10, bf16[256,3584]{1,0:T(8,128)(2,1)} %bitcast.10.b_ref, bf16[256,3584]{1,0:T(8,128)(2,1)} %copy-done.4), custom_call_target="tpu_custom_call" | custom-call | tf_op jit(solution)/shard_map/pallas_call | solution.py:180
  169.1 6.0 %fusion.b_ref = bf16[256,1024]{1,0:T(8,128)(2,1)S(1)} fusion(bf16[256,3584]{1,0:T(8,128)(2,1)} %bitcast.10.b_ref, bf16[1024,3584]{1,0:T(8,128)(2,1)} %all-gather.5.cloned.1.call-done, f32[256,1024]{1,0:T(8,128)} %get-tuple-element.60), kind=kOutput, calls=%fused_computation.2 | convolution fusion | flops 1881407488 | bytes 10747904 | tf_op jit(solution)/shard_map/dot_general | solution.py:326
  178.0 7.6 %shard_map.172 = bf16[1792,1024]{1,0:T(8,128)(2,1)} custom-call(s32[1]{0:T(128)} %bitcast.half_ref, bf16[256,3584]{1,0:T(8,128)(2,1)} %bitcast.32, bf16[256,3584]{1,0:T(8,128)(2,1)} %collective-permute-done.ao_ref, bf16[256,1024]{1,0:T(8,128)(2,1)} %copy-done.7, bf16[256,1024]{1,0:T(8,128)(2,1)} %copy-done.11), custom_call_target="tpu_custom_call" | custom-call | tf_op jit(solution)/shard_map/pallas_call | solution.py:180
  185.7 6.2 %all-to-all-start.3 = ((bf16[8,6,224,128]{3,2,1,0:T(8,128)(2,1)}), bf16[8,6,224,128]{3,2,1,0:T(8,128)(2,1)S(1)}, u32[]{:S(2)}, u32[]{:S(2)}) async-start(bf16[8,6,224,128]{3,2,1,0:T(8,128)(2,1)} %order_states.1), calls=%async_computation.4 | async-start | bytes 5505024 | tf_op jit(solution)/shard_map/all_to_all | solution.py:258
  191.9 17.9 %reduce-scatter.5.cloned.1.call-done = bf16[128,3584]{1,0:T(8,128)(2,1)} async-done(((bf16[512,3584]{1,0:T(8,128)(2,1)}), bf16[128,3584]{1,0:T(8,128)(2,1)}) %reduce-scatter.5.cloned.1.call-update) | async-done | bytes 917520 | tf_op jit(solution)/shard_map/reduce_scatter | solution.py:324
  212.0 13.5 %all-to-all-done.3.state_ref = bf16[8,6,224,128]{3,2,1,0:T(8,128)(2,1)S(1)} async-done(((bf16[8,6,224,128]{3,2,1,0:T(8,128)(2,1)}), bf16[8,6,224,128]{3,2,1,0:T(8,128)(2,1)S(1)}, u32[]{:S(2)}, u32[]{:S(2)}) %all-to-all-start.3) | async-done | bytes 2752544 | tf_op jit(solution)/shard_map/all_to_all | solution.py:258
  225.5 6.8 %all-to-all-start.4 = ((bf16[16,224,128]{2,1,0:T(8,128)(2,1)}), bf16[16,224,128]{2,1,0:T(8,128)(2,1)}, u32[]{:S(2)}, u32[]{:S(2)}) async-start(bf16[16,224,128]{2,1,0:T(8,128)(2,1)} %bitcast.34), calls=%async_computation.6 | async-start | bytes 1835008 | tf_op jit(solution)/shard_map/all_to_all | solution.py:258
  232.3 6.5 %convolution_convert_fusion = bf16[256,3584]{1,0:T(8,128)(2,1)} fusion(bf16[256,1024]{1,0:T(8,128)(2,1)S(1)} %copy-done.8, bf16[3584,1024]{1,0:T(8,128)(2,1)} %all-gather.3.cloned.1.call-done), kind=kOutput, calls=%fused_computation | convolution fusion | flops 1879965696 | bytes 9699328 | tf_op jit(solution)/shard_map/dot_general | solution.py:332
  238.8 6.7 %all-to-all-done.4 = bf16[16,224,128]{2,1,0:T(8,128)(2,1)} async-done(((bf16[16,224,128]{2,1,0:T(8,128)(2,1)}), bf16[16,224,128]{2,1,0:T(8,128)(2,1)}, u32[]{:S(2)}, u32[]{:S(2)}) %all-to-all-start.4) | async-done | bytes 917536 | tf_op jit(solution)/shard_map/all_to_all | solution.py:258
  245.5 6.6 %all-to-all-start.6 = ((bf16[16,16,3584]{2,1,0:T(8,128)(2,1)}), bf16[16,16,3584]{2,1,0:T(8,128)(2,1)S(1)}, u32[]{:S(2)}, u32[]{:S(2)}) async-start(bf16[16,16,3584]{2,1,0:T(8,128)(2,1)} %bitcast.41), calls=%async_computation.8 | async-start | bytes 3670016 | tf_op jit(solution)/shard_map/all_to_all | solution.py:258
  254.2 19.7 %all-to-all-done.6.ret_ref = bf16[16,16,3584]{2,1,0:T(8,128)(2,1)S(1)} async-done(((bf16[16,16,3584]{2,1,0:T(8,128)(2,1)}), bf16[16,16,3584]{2,1,0:T(8,128)(2,1)S(1)}, u32[]{:S(2)}, u32[]{:S(2)}) %all-to-all-start.6) | async-done | bytes 1835040 | tf_op jit(solution)/shard_map/all_to_all | solution.py:258
  273.9 6.0 %all-to-all-start.5 = ((bf16[8,224,128]{2,1,0:T(8,128)(2,1)}), bf16[8,224,128]{2,1,0:T(8,128)(2,1)S(1)}, u32[]{:S(2)}, u32[]{:S(2)}) async-start(bf16[8,224,128]{2,1,0:T(8,128)(2,1)} %sum_order.2), calls=%async_computation.7 | async-start | bytes 917504 | tf_op jit(solution)/shard_map/all_to_all | solution.py:258
  282.6 5.0 %all-to-all-done.5.grad_ref = bf16[8,224,128]{2,1,0:T(8,128)(2,1)S(1)} async-done(((bf16[8,224,128]{2,1,0:T(8,128)(2,1)}), bf16[8,224,128]{2,1,0:T(8,128)(2,1)S(1)}, u32[]{:S(2)}, u32[]{:S(2)}) %all-to-all-start.5) | async-done | bytes 458784 | tf_op jit(solution)/shard_map/all_to_all | solution.py:258
  294.5 18.3 %all_to_all.47 = bf16[16,224,128]{2,1,0:T(8,128)(2,1)} all-to-all(bf16[16,224,128]{2,1,0:T(8,128)(2,1)} %bitcast.36), channel_id=1, replica_groups=mesh['expert'=8,'x'=2,'y'=4,'core'=2] {'expert','x'}, dimensions={0} | all-to-all | bytes 1835008 | tf_op jit(solution)/shard_map/all_to_all | solution.py:258
  314.9 14.1 %all_to_all.48.grad_ref = bf16[8,224,128]{2,1,0:T(8,128)(2,1)} all-to-all(bf16[8,224,128]{2,1,0:T(8,128)(2,1)} %sum_order.3), channel_id=1, replica_groups=mesh['expert'=8,'x'=2,'y'=4,'core'=2] {'expert'}, dimensions={0} | all-to-all | bytes 917504 | tf_op jit(solution)/shard_map/all_to_all | solution.py:258
  329.0 3.7 %shard_map.176 = (f32[224,1024]{1,0:T(8,128)}, f32[224,1024]{1,0:T(8,128)}, f32[224,1024]{1,0:T(8,128)}) custom-call(bf16[8,6,224,128]{3,2,1,0:T(8,128)(2,1)} %copy-done, bf16[8,224,128]{2,1,0:T(8,128)(2,1)} %all_to_all.48.grad_ref), custom_call_target="tpu_custom_call" | custom-call | tf_op jit(solution)/shard_map/pallas_call | solution.py:240
  (60 shorter events, 29.8 us)
Async XLA Ops:
  7.2 141.2 %all-gather.3.cloned.1.call-start = ((), (), s32[]{:S(2)}) async-start(), calls=%async_computation.11 | async-start | bytes 7798784 | tf_op jit(solution)/shard_map/all_gather | solution.py:289
  9.8 159.3 %all-gather.5.cloned.1.call-start = ((), (), s32[]{:S(2)}) async-start(), calls=%async_computation.12 | async-start | bytes 8257536 | tf_op jit(solution)/shard_map/all_gather | solution.py:291
  30.5 9.6 %copy-start.13 = (s32[8,1]{0,1:T(1,128)S(1)}, s32[8,1]{0,1:T(1,128)}, u32[]{:S(2)}) copy-start(s32[8,1]{0,1:T(1,128)} %param.14) | copy-start | bytes 100
  30.5 56.4 %all-to-all-start = ((bf16[8,6,224,128]{3,2,1,0:T(8,128)(2,1)}), bf16[8,6,224,128]{3,2,1,0:T(8,128)(2,1)S(1)}, u32[]{:S(2)}, u32[]{:S(2)}) async-start(bf16[8,6,224,128]{3,2,1,0:T(8,128)(2,1)} %pack_states.1), calls=%async_computation | async-start | bytes 5505024 | tf_op jit(solution)/shard_map/all_to_all | solution.py:258
  40.1 169.7 %reduce-scatter.5.cloned.1.call-start = ((), (), s32[]{:S(2)}) async-start(), calls=%async_computation.14 | async-start | bytes 4587520 | tf_op jit(solution)/shard_map/reduce_scatter | solution.py:324
  86.9 61.5 %copy-start.1 = (bf16[8,6,224,128]{3,2,1,0:T(8,128)(2,1)}, bf16[8,6,224,128]{3,2,1,0:T(8,128)(2,1)S(1)}, u32[]{:S(2)}) copy-start(bf16[8,6,224,128]{3,2,1,0:T(8,128)(2,1)S(1)} %all-to-all-done.in_ref) | copy-start | bytes 8257540
  86.9 34.2 %copy-start.6 = (bf16[16,16,3584]{2,1,0:T(8,128)(2,1)S(1)}, bf16[16,16,3584]{2,1,0:T(8,128)(2,1)}, u32[]{:S(2)}) copy-start(bf16[16,16,3584]{2,1,0:T(8,128)(2,1)} %get-tuple-element.40) | copy-start | bytes 5505028
  148.4 11.4 %collective-permute-start.2 = (bf16[256,3584]{1,0:T(8,128)(2,1)}, bf16[256,3584]{1,0:T(8,128)(2,1)S(1)}, u32[]{:S(2)}, u32[]{:S(2)}) collective-permute-start(bf16[256,3584]{1,0:T(8,128)(2,1)} %bitcast.10.b_ref), channel_id=1, source_target_pairs={{0,1},{1,0},{2,3},{3,2},{4,5},{5,4},{6,7},{7,6},{8,9},{9,8},{10,11... | collective-permute-start | bytes 5505032 | tf_op jit(solution)/shard_map/ppermute | solution.py:262
  148.4 7.2 %copy-start.14 = (s32[8]{0:T(128)S(1)}, s32[8]{0:T(128)}, u32[]{:S(2)}) copy-start(s32[8]{0:T(128)} %param.17) | copy-start | bytes 100
  148.4 7.3 %copy-start.12 = (s32[8]{0:T(128)S(1)}, s32[8]{0:T(128)}, u32[]{:S(2)}) copy-start(s32[8]{0:T(128)} %own_ref.3) | copy-start | bytes 100
  155.1 4.7 %copy-start.9 = (bf16[256,1024]{1,0:T(8,128)(2,1)}, bf16[256,1024]{1,0:T(8,128)(2,1)S(1)}, u32[]{:S(2)}) copy-start(bf16[256,1024]{1,0:T(8,128)(2,1)S(1)} %get-tuple-element.59.a_ref) | copy-start | bytes 1572868
  155.1 4.7 %collective-permute-start.1 = (bf16[256,1024]{1,0:T(8,128)(2,1)S(1)}, bf16[256,1024]{1,0:T(8,128)(2,1)S(1)}, u32[]{:S(2)}, u32[]{:S(2)}) collective-permute-start(bf16[256,1024]{1,0:T(8,128)(2,1)S(1)} %get-tuple-element.59.a_ref), channel_id=1, source_target_pairs={{0,1},{1,0},{2,3},{3,2},{4,5},{5,4},{6,7},{7,6},{8,9},{9,8},{10,11... | collective-permute-start | bytes 1572872 | tf_op jit(solution)/shard_map/ppermute | solution.py:262
  167.6 1.5 copy-start.2
  167.6 124.5 %reduce-scatter.3.cloned.1.call-start = ((), (), s32[]{:S(2)}) async-start(), calls=%async_computation.13 | async-start | bytes 4587520 | tf_op jit(solution)/shard_map/reduce_scatter | solution.py:330
  169.1 6.6 %collective-permute-start = (bf16[256,3584]{1,0:T(8,128)(2,1)S(1)}, bf16[256,3584]{1,0:T(8,128)(2,1)}, u32[]{:S(2)}, u32[]{:S(2)}) collective-permute-start(bf16[256,3584]{1,0:T(8,128)(2,1)S(1)} %bitcast.33), channel_id=1, source_target_pairs={{0,1},{1,0},{2,3},{3,2},{4,5},{5,4},{6,7},{7,6},{8,9},{9,8},{10,11... | collective-permute-start | bytes 5505032 | tf_op jit(solution)/shard_map/ppermute | solution.py:262
  175.1 2.1 copy-start.7
  175.1 2.1 collective-permute-start.3
  185.7 39.9 %all-to-all-start.3 = ((bf16[8,6,224,128]{3,2,1,0:T(8,128)(2,1)}), bf16[8,6,224,128]{3,2,1,0:T(8,128)(2,1)S(1)}, u32[]{:S(2)}, u32[]{:S(2)}) async-start(bf16[8,6,224,128]{3,2,1,0:T(8,128)(2,1)} %order_states.1), calls=%async_computation.4 | async-start | bytes 5505024 | tf_op jit(solution)/shard_map/all_to_all | solution.py:258
  191.9 40.4 %copy-start.8 = (bf16[256,1024]{1,0:T(8,128)(2,1)S(1)}, bf16[256,1024]{1,0:T(8,128)(2,1)}, u32[]{:S(2)}) copy-start(bf16[256,1024]{1,0:T(8,128)(2,1)} %copy-done.7) | copy-start | bytes 1572868
  225.5 13.3 %copy-start = (bf16[8,6,224,128]{3,2,1,0:T(8,128)(2,1)}, bf16[8,6,224,128]{3,2,1,0:T(8,128)(2,1)S(1)}, u32[]{:S(2)}) copy-start(bf16[8,6,224,128]{3,2,1,0:T(8,128)(2,1)S(1)} %all-to-all-done.3.state_ref) | copy-start | bytes 8257540
  225.5 20.0 %all-to-all-start.4 = ((bf16[16,224,128]{2,1,0:T(8,128)(2,1)}), bf16[16,224,128]{2,1,0:T(8,128)(2,1)}, u32[]{:S(2)}, u32[]{:S(2)}) async-start(bf16[16,224,128]{2,1,0:T(8,128)(2,1)} %bitcast.34), calls=%async_computation.6 | async-start | bytes 1835008 | tf_op jit(solution)/shard_map/all_to_all | solution.py:258
  245.5 28.4 %all-to-all-start.6 = ((bf16[16,16,3584]{2,1,0:T(8,128)(2,1)}), bf16[16,16,3584]{2,1,0:T(8,128)(2,1)S(1)}, u32[]{:S(2)}, u32[]{:S(2)}) async-start(bf16[16,16,3584]{2,1,0:T(8,128)(2,1)} %bitcast.41), calls=%async_computation.8 | async-start | bytes 3670016 | tf_op jit(solution)/shard_map/all_to_all | solution.py:258
  273.9 6.1 %copy-start.3 = (bf16[16,16,3584]{2,1,0:T(8,128)(2,1)}, bf16[16,16,3584]{2,1,0:T(8,128)(2,1)S(1)}, u32[]{:S(2)}) copy-start(bf16[16,16,3584]{2,1,0:T(8,128)(2,1)S(1)} %all-to-all-done.6.ret_ref) | copy-start | bytes 5505028
  273.9 13.8 %all-to-all-start.5 = ((bf16[8,224,128]{2,1,0:T(8,128)(2,1)}), bf16[8,224,128]{2,1,0:T(8,128)(2,1)S(1)}, u32[]{:S(2)}, u32[]{:S(2)}) async-start(bf16[8,224,128]{2,1,0:T(8,128)(2,1)} %sum_order.2), calls=%async_computation.7 | async-start | bytes 917504 | tf_op jit(solution)/shard_map/all_to_all | solution.py:258
  (4 other events, 4.2 us)
Sparse Core Ops, SparseCore 0:
  10.3 68.3 all-gather.2
  80.4 48.5 all-gather.4
  167.7 41.9 reduce-scatter.4
  212.0 42.2 reduce-scatter.2

commit v3 on v2

v3 whole, which is shorter than its diff:
```python
import jax
import jax.numpy as jnp
from jax import lax
from jax.experimental import pallas as pl
from jax.experimental.pallas import tpu as pltpu
from jax.sharding import Mesh
from jax.sharding import PartitionSpec as P


beta_one = 0.9
beta_two = 0.95
bias_one = 1.0 - 0.9**10
bias_two = 1.0 - 0.95**10
rate_value = 0.01
decay_value = 0.1
eps_value = 1e-08

F32 = jnp.float32
BF = jnp.bfloat16
NX, NY, NC = 2, 4, 2
LANE = 128


def row_order():
    return [x * NY * NC + y * NC + c for c in range(NC) for y in range(NY) for x in range(NX)]


def inverse(order):
    back = [0] * len(order)
    for p, r in enumerate(order):
        back[r] = p
    return back


def lanes_taken(value, order):
    width = value.shape[1] // len(order)
    return jnp.concatenate([value[:, r * width : (r + 1) * width] for r in order], axis=1)


def pack_weights_body(up_ref, down_ref, u_ref, w_ref):
    for g in range(u_ref.shape[0]):
        u_ref[g] = up_ref[:, g * LANE : (g + 1) * LANE].astype(BF)
        w_ref[g] = down_ref[g * 8 : (g + 1) * 8].astype(BF)


def pack_weights(up, down, groups):
    return pl.pallas_call(
        pack_weights_body,
        out_shape=(
            jax.ShapeDtypeStruct((groups, up.shape[0], LANE), BF),
            jax.ShapeDtypeStruct((groups, down.shape[0] // groups, down.shape[1]), BF),
        ),
        name="pack_weights",
    )(up, down)


def unpack_up_body(in_ref, out_ref):
    groups = in_ref.shape[0] // NX
    rows = in_ref.shape[1]
    for x in range(NX):
        value = jnp.concatenate([in_ref[g * NX + x].astype(F32) for g in range(groups)], axis=1)
        out_ref[x * rows : (x + 1) * rows] = lanes_taken(value, row_order()).astype(BF)


def unpack_down_body(in_ref, out_ref):
    groups = in_ref.shape[0] // NX
    rows = in_ref.shape[1]
    for x in range(NX):
        value = jnp.concatenate([in_ref[g * NX + x].astype(F32) for g in range(groups)], axis=0)
        out_ref[x * groups * rows : (x + 1) * groups * rows] = value.astype(BF)


def unpack(body, shares, shape):
    return pl.pallas_call(body, out_shape=jax.ShapeDtypeStruct(shape, BF))(shares)


def slot_of_block(ids_ref, own_ref, b):
    mine = ids_ref[b, 0]
    place = jnp.int32(0)
    for e in range(b):
        place = place + (ids_ref[e, 0] == mine).astype(jnp.int32)
    return own_ref[mine] * 2 + place


def dispatch_body(ids_ref, count_ref, own_ref, tok_ref, cot_ref, sx_ref, sdy_ref):
    blocks, rows, _ = tok_ref.shape
    sx_ref[...] = jnp.zeros(sx_ref.shape, BF)
    sdy_ref[...] = jnp.zeros(sdy_ref.shape, BF)
    at = lax.broadcasted_iota(jnp.int32, (rows, 1), 0)
    for b in range(blocks):
        slot = slot_of_block(ids_ref, own_ref, b)
        alive = at < count_ref[b]
        x = jnp.where(alive, tok_ref[b].astype(F32), 0.0)
        dy = jnp.where(alive, cot_ref[b].astype(F32), 0.0)
        sx_ref[slot] = lanes_taken(x, row_order()).astype(BF)
        sdy_ref[slot] = dy.astype(BF)


def smem():
    return pl.BlockSpec(memory_space=pltpu.SMEM)


def vmem():
    return pl.BlockSpec(memory_space=pltpu.VMEM)


def dispatch(ids, count, owner, tokens, cotangent):
    blocks, rows, width = tokens.shape
    out = jax.ShapeDtypeStruct((2 * blocks, rows, width), BF)
    return pl.pallas_call(
        dispatch_body,
        in_specs=[smem(), smem(), smem(), vmem(), vmem()],
        out_shape=(out, out),
        name="dispatch",
    )(ids, count, owner, tokens, cotangent)


def combine_body(ids_ref, own_ref, ret_ref, out_ref):
    for b in range(out_ref.shape[0]):
        slot = slot_of_block(ids_ref, own_ref, b)
        out_ref[b] = lanes_taken(ret_ref[slot].astype(F32), inverse(row_order())).astype(BF)


def combine(ids, owner, returned):
    slots, rows, width = returned.shape
    return pl.pallas_call(
        combine_body,
        in_specs=[smem(), smem(), vmem()],
        out_shape=jax.ShapeDtypeStruct((slots // 2, rows, width), BF),
        name="combine",
    )(ids, owner, returned)


def to_tiles(rows8):
    n = rows8.shape[1] // LANE
    return jnp.concatenate([rows8[:, i * LANE : (i + 1) * LANE] for i in range(n)], axis=0)


def from_tiles(tiles):
    n = tiles.shape[0] // 8
    return jnp.concatenate([tiles[i * 8 : (i + 1) * 8] for i in range(n)], axis=1)


def pack_body(a_ref, b_ref, c_ref, d_ref, out_ref):
    for g in range(out_ref.shape[0]):
        for i, ref in enumerate((a_ref, b_ref)):
            out_ref[g, i] = ref[:, g * LANE : (g + 1) * LANE].astype(BF)
        for i, ref in enumerate((c_ref, d_ref)):
            out_ref[g, 2 + i] = to_tiles(ref[g * 8 : (g + 1) * 8]).astype(BF)


def pack_states(ups, downs, groups):
    rows, cols = ups[0].shape
    return pl.pallas_call(
        pack_body,
        out_shape=jax.ShapeDtypeStruct((groups, 4, rows, cols // groups), BF),
        name="pack_states",
    )(*ups, *downs)


def order_body(old_ref, new_ref, in_ref, out_ref):
    copies = out_ref.shape[0] // in_ref.shape[0]
    for k in range(in_ref.shape[0]):
        for i in range(copies):
            out_ref[new_ref[k] * copies + i] = in_ref[old_ref[k]]


def order_states(old, new, shares, copies):
    shape = (shares.shape[0] * copies,) + shares.shape[1:]
    return pl.pallas_call(
        order_body, in_specs=[smem(), smem(), vmem()], out_shape=jax.ShapeDtypeStruct(shape, BF)
    )(old, new, shares)


def weight_grad_body(half_ref, a_ref, ao_ref, b_ref, bo_ref, out_ref):
    dims = (((0,), (0,)), ((), ()))
    total = lax.dot_general(a_ref[...], b_ref[...], dims, preferred_element_type=F32)
    total += lax.dot_general(ao_ref[...], bo_ref[...], dims, preferred_element_type=F32)
    out_ref[...] = total.astype(BF)


def weight_grad(place, a, a_other, b, b_other, step):
    rows, width = a.shape
    cols = b.shape[1]
    steps = width // 2 // step
    left = pl.BlockSpec(
        (rows, step), lambda i, at: (0, at[0] * steps + lax.rem(at[1] + i, steps))
    )
    right = pl.BlockSpec((rows, cols), lambda i, at: (0, 0))
    return pl.pallas_call(
        weight_grad_body,
        grid_spec=pltpu.PrefetchScalarGridSpec(
            num_scalar_prefetch=1,
            grid=(steps,),
            in_specs=[left, left, right, right],
            out_specs=pl.BlockSpec((step, cols), lambda i, at: (i, 0)),
        ),
        out_shape=jax.ShapeDtypeStruct((width // 2, cols), BF),
    )(place, a, a_other, b, b_other)


def relay_body(part_ref, below_ref, above_ref, up_ref, down_ref):
    tall = below_ref.shape[0]
    wide = 2 * tall
    mine = part_ref[wide : 2 * wide].astype(F32)
    up_ref[0:tall] = (mine[0:tall] + below_ref[...].astype(F32)).astype(BF)
    up_ref[tall:wide] = part_ref[wide + tall : 2 * wide]
    mine = part_ref[3 * wide + tall : 4 * wide].astype(F32)
    down_ref[0:tall] = part_ref[3 * wide : 3 * wide + tall]
    down_ref[tall:wide] = (mine + above_ref[...].astype(F32)).astype(BF)


def relay(part, below, above):
    tall, cols = below.shape
    out = jax.ShapeDtypeStruct((2 * tall, cols), BF)
    return pl.pallas_call(relay_body, out_shape=(out, out), name="relay")(part, below, above)


def finish_body(x_ref, part_ref, below_ref, above_ref, own_ref, send_ref):
    tall = own_ref.shape[0]
    total = part_ref[...].astype(F32) + below_ref[...].astype(F32) + above_ref[...].astype(F32)
    low, high = total[0:tall], total[tall : 2 * tall]
    first = x_ref[0] == 0
    own_ref[...] = jnp.where(first, low, high)
    send_ref[...] = jnp.where(first, high, low).astype(BF)


def finish(x_at, part, below, above):
    wide, cols = below.shape
    whole = pl.BlockSpec((wide, cols), lambda i: (0, 0))
    half_spec = pl.BlockSpec((wide // 2, cols), lambda i: (0, 0))
    return pl.pallas_call(
        finish_body,
        grid=(1,),
        in_specs=[smem(), whole, whole, whole],
        out_specs=(half_spec, half_spec),
        out_shape=(
            jax.ShapeDtypeStruct((wide // 2, cols), F32),
            jax.ShapeDtypeStruct((wide // 2, cols), BF),
        ),
        name="finish",
    )(x_at, part, below, above)


def adam_update(weight, moment, second, gradient):
    moment_new = beta_one * moment + (1.0 - beta_one) * gradient
    second_new = beta_two * second + (1.0 - beta_two) * gradient * gradient
    update = moment_new / bias_one / (jnp.sqrt(second_new / bias_two) + eps_value)
    return (weight - rate_value * (update + decay_value * weight), moment_new, second_new)


def adam_up_body(x_ref, weight_ref, state_ref, grad_ref, *outs):
    grad = lanes_taken(grad_ref[...].astype(F32), inverse(row_order()))
    for g in range(state_ref.shape[0]):
        lanes = slice(g * LANE, (g + 1) * LANE)
        m, v = (state_ref[g, i].astype(F32) for i in range(2))
        w = weight_ref[g * NX + x_ref[0]].astype(F32)
        for ref, value in zip(outs, adam_update(w, m, v, grad[:, lanes])):
            ref[:, lanes] = value


def adam_down_body(x_ref, weight_ref, state_ref, grad_ref, other_ref, *outs):
    for g in range(state_ref.shape[0]):
        rows = slice(g * 8, (g + 1) * 8)
        m, v = (from_tiles(state_ref[g, i].astype(F32)) for i in range(2))
        w = weight_ref[g * NX + x_ref[0]].astype(F32)
        grad = grad_ref[rows] + other_ref[rows].astype(F32)
        for ref, value in zip(outs, adam_update(w, m, v, grad)):
            ref[rows] = value


def adam(body, x_at, weights, states, which, grads, shape):
    groups, _, rows, wide = states.shape
    full = pl.BlockSpec(shape, lambda i: (0, 0))
    return pl.pallas_call(
        body,
        grid=(1,),
        in_specs=[
            smem(),
            pl.BlockSpec(weights.shape, lambda i: (0, 0, 0)),
            pl.BlockSpec((groups, 2, rows, wide), lambda i: (0, which, 0, 0)),
        ]
        + [full] * len(grads),
        out_specs=[full] * 3,
        out_shape=[jax.ShapeDtypeStruct(shape, F32)] * 3,
    )(x_at, weights, states, *grads)


def silu_parts(pre_act):
    sigma = jax.nn.sigmoid(pre_act)
    return (pre_act * sigma, sigma * (1.0 + pre_act * (1.0 - sigma)))


def exchange(array, axis):
    return lax.all_to_all(array, axis, split_axis=0, concat_axis=0, tiled=True)


def from_partner(array):
    return lax.ppermute(array, "core", [(0, 1), (1, 0)])


def step(
    tokens,
    cotangent,
    block_expert,
    block_count,
    old_owner,
    new_owner,
    up_weight,
    down_weight,
    up_first,
    up_second,
    down_first,
    down_second,
):
    groups = lax.axis_size("expert")
    tok_rows, features = tokens.shape
    blocks = block_count.shape[0]
    rows = tok_rows // blocks
    core_at = lax.axis_index("core").astype(jnp.int32)
    y_at = lax.axis_index("y").astype(jnp.int32)
    x_at = lax.axis_index("x").astype(jnp.int32).reshape(1)
    up_place = jnp.stack([core_at, jnp.zeros((), jnp.int32)])
    down_place = jnp.stack([core_at, y_at])
    up_shape, down_shape = up_weight.shape[1:], down_weight.shape[1:]

    up_packed, down_packed = pack_weights(up_weight[0], down_weight[0], groups)

    def weight_moved(packed):
        spread = exchange(packed, "expert")
        ordered = order_states(old_owner, new_owner, spread, NX)
        return exchange(ordered, ("expert", "x"))

    up_shares = weight_moved(up_packed)
    up_pair = unpack(unpack_up_body, up_shares, (NX * up_shape[0], up_shape[1]))
    up_mat = lax.all_gather(up_pair, ("core", "y"), axis=0, tiled=True)

    down_packed, up_pair = lax.optimization_barrier((down_packed, up_pair))
    down_shares = weight_moved(down_packed)
    down_pair = unpack(unpack_down_body, down_shares, (NX * down_shape[0], down_shape[1]))
    down_mat = lax.all_gather(down_pair, ("core", "y"), axis=0, tiled=True)

    send_x, send_dy = dispatch(
        block_expert,
        block_count,
        new_owner,
        tokens.reshape(blocks, rows, features),
        cotangent.reshape(blocks, rows, features),
    )
    send_x, _ = lax.optimization_barrier((send_x, down_pair))
    inputs = exchange(send_x, "expert")
    send_dy, inputs = lax.optimization_barrier((send_dy, inputs))
    inputs = inputs.reshape(-1, features)
    upstream = exchange(send_dy, "expert").reshape(-1, features)
    inputs_other, upstream_other = from_partner(inputs), from_partner(upstream)

    packed = pack_states(
        (up_first[0], up_second[0]), (down_first[0], down_second[0]), groups
    )
    packed, upstream = lax.optimization_barrier((packed, upstream))
    shares = exchange(packed, "expert")

    pre_act = jnp.dot(inputs, up_mat, preferred_element_type=F32)
    active, slopes = silu_parts(pre_act)
    hidden = active.astype(BF)
    hidden_other = from_partner(hidden)
    down_part = weight_grad(down_place, hidden, hidden_other, upstream, upstream_other, 128)
    tall = down_shape[0]
    rising = [(i, (i + 1) % NY) for i in range(NY)]
    falling = [(i, (i - 1) % NY) for i in range(NY)]
    below = lax.ppermute(down_part[4 * tall : 5 * tall], "y", rising)
    above = lax.ppermute(down_part[5 * tall : 6 * tall], "y", falling)
    upstream, _ = lax.optimization_barrier((upstream, down_part))
    back = lax.dot_general(upstream, down_mat, (((1,), (1,)), ((), ())), preferred_element_type=F32)
    pre_grad = (back * slopes).astype(BF)
    pre_grad_other = from_partner(pre_grad)
    up_part = weight_grad(up_place, inputs, inputs_other, pre_grad, pre_grad_other, 256)
    up_grad = lax.psum_scatter(up_part, ("y", "x"), scatter_dimension=0, tiled=True)
    pre_grad, up_part = lax.optimization_barrier((pre_grad, up_part))
    going_up, going_down = relay(down_part, below, above)
    below = lax.ppermute(going_up, "y", rising)
    above = lax.ppermute(going_down, "y", falling)
    input_grad = lax.dot_general(
        pre_grad, up_mat, (((1,), (1,)), ((), ())), preferred_element_type=F32
    ).astype(BF)
    input_grad, shares = lax.optimization_barrier((input_grad, shares))
    returned = exchange(input_grad.reshape(-1, rows, features), "expert")
    ordered = order_states(old_owner, new_owner, shares, 1)
    ordered, returned = lax.optimization_barrier((ordered, returned))
    states = exchange(ordered, "expert")
    token_grad = combine(block_expert, new_owner, returned).reshape(tok_rows, features)

    down_own, down_send = finish(x_at, down_part, below, above)
    down_other = lax.ppermute(down_send, "x", [(0, 1), (1, 0)])
    down_new = adam(
        adam_down_body, x_at, down_shares, states, 1, (down_own, down_other), down_shape,
    )
    up_new = adam(adam_up_body, x_at, up_shares, states, 0, (up_grad,), up_shape)
    return (
        token_grad,
        up_new[0][None],
        down_new[0][None],
        up_new[1][None],
        up_new[2][None],
        down_new[1][None],
        down_new[2][None],
    )


def solution(mesh):
    fine = Mesh(
        mesh.devices.reshape(mesh.devices.shape[0], NX, NY, NC), ("expert", "x", "y", "core")
    )
    every = ("expert", "x", "y", "core")
    dp = ("x", "y", "core")
    state = P("expert", dp, None)
    return jax.shard_map(
        step,
        mesh=fine,
        in_specs=(P(every, None), P(every, None), P(every, None), P(every), P(), P())
        + (state,) * 6,
        out_specs=(P(every, None),) + (state,) * 6,
        check_vma=False,
    )
```

time: 343 us -> 343 us (level)
  waiting for transfers between devices: 107 us -> 94.6 us
  Pallas kernels: 47.3 us -> 54.3 us
  local copies, waits for them, and re-layouts: 5.08 us -> 10.6 us
  blocking collectives: 110 us -> 115 us
  starting transfers between devices: 36.5 us -> 32.2 us
    ppermute x0 -> x5, waiting for transfers between devices: none -> 28 us  [the longest x1 21.1 us: step(): below = lax.ppermute(going_up, 'y', rising)]
    all_to_all x5 -> x3, waiting for transfers between devices: 87.2 us -> 65.5 us  [exchange(): return lax.all_to_all(array, axis, split_axis=0, concat_axis=0, tiled=True)]
    all_to_all x4 -> x6, blocking collectives: 93.9 us -> 115 us  [exchange(): return lax.all_to_all(array, axis, split_axis=0, concat_axis=0, tiled=True)]
    reduce_scatter x2 -> x1, waiting for transfers between devices: 17.9 us -> 0.01 us  [step(): lax.psum_scatter(up_part, ('y', 'x'), scatter_dimension=0, tiled=True)]
    all_gather x1 -> x0, blocking collectives: 16 us -> none  [step(): down_pair = lax.all_gather(down_short, 'x', axis=0, tiled=True)]
    all_to_all x5 -> x3, starting transfers between devices: 35.3 us -> 24.2 us  [exchange(): return lax.all_to_all(array, axis, split_axis=0, concat_axis=0, tiled=True)]
    ppermute x0 -> x5, starting transfers between devices: none -> 6.75 us  [the longest x1 1.96 us: step(): below = lax.ppermute(down_part[4 * tall:5 * tall], 'y', rising)]
    pallas_call x9 -> x11, Pallas kernels: 26.8 us -> 32.6 us  [the longest x2 8.15 us: adam(): pl.pallas_call(body, grid=(1,), in_specs=[smem(), pl.BlockSpec(weights.sh...]
  transfers between devices with their start and end apart: 13 -> 15, of which waited for: 7 -> 5; matrix products, arithmetic and copies ran while one was open for 6% -> 7% of each run, Pallas kernels for 11% -> 10%
where the time goes in v3:
time: 343 us; the launch traced here: 341 us
  blocking collectives  115 us (34%)
  waiting for transfers between devices  94.6 us (28%)
  Pallas kernels  54.3 us (16%)
  starting transfers between devices  32.2 us (9%)
  matrix products  18.9 us (6%)
  between operations  13.8 us (4%)
  local copies, waits for them, and re-layouts  10.6 us (3%)
    all_to_all x6, blocking collectives, exchange(): return lax.all_to_all(array, axis, split_axis=0, concat_axis=0, tiled=True)  115 us
    all_to_all x3, waiting for transfers between devices, exchange(): return lax.all_to_all(array, axis, split_axis=0, concat_axis=0, tiled=True)  65.5 us
    all_to_all x3, starting transfers between devices, exchange(): return lax.all_to_all(array, axis, split_axis=0, concat_axis=0, tiled=True)  24.2 us
    ppermute x1, waiting for transfers between devices, step(): below = lax.ppermute(going_up, 'y', rising)  21.1 us
    pallas_call x2, Pallas kernels, weight_grad(): pl.pallas_call(weight_grad_body, grid_spec=pltpu.PrefetchScalarGridSpec(n...  15.3 us
    unnamed x33, local copies, waits for them, and re-layouts  8.61 us
    pallas_call x2, Pallas kernels, adam(): pl.pallas_call(body, grid=(1,), in_specs=[smem(), pl.BlockSpec(weights.sh...  8.15 us
    pallas_call x3, Pallas kernels, order_states(): pl.pallas_call(order_body, in_specs=[smem(), smem(), vmem()], out_shape=j...  7 us
  transfers between devices with their start and end apart: 15, of which 5 were waited for; matrix products, arithmetic and copies ran while one was open for 7% of the time, Pallas kernels for 10%

profile of v3, /device:TPU:4, one launch (start us, length us, event | category | flops | bytes accessed | tf_op | source)
XLA Modules:
  0.0 341.1 jit_solution(9869455671719228389)
XLA Ops:
  9.7 16.6 %all_to_all.45.in_ref = bf16[8,224,128]{2,1,0:T(8,128)(2,1)} all-to-all(bf16[8,224,128]{2,1,0:T(8,128)(2,1)} %get-tuple-element.36), channel_id=1, replica_groups=mesh['expert'=8,'x'=2,'y'=4,'core'=2] {'expert'}, dimensions={0} | all-to-all | bytes 917504 | tf_op jit(solution)/shard_map/all_to_all | solution.py:295
  28.3 18.9 %all_to_all.46.in_ref.weight_ref = bf16[16,224,128]{2,1,0:T(8,128)(2,1)} all-to-all(bf16[16,224,128]{2,1,0:T(8,128)(2,1)} %shard_map.171), channel_id=1, replica_groups=mesh['expert'=8,'x'=2,'y'=4,'core'=2] {'expert','x'}, dimensions={0} | all-to-all | bytes 1835008 | tf_op jit(solution)/shard_map/all_to_all | solution.py:295
  49.8 13.0 %all_to_all.47.in_ref = bf16[8,8,3584]{2,1,0:T(8,128)(2,1)} all-to-all(bf16[8,8,3584]{2,1,0:T(8,128)(2,1)S(1)} %copy-done.14), channel_id=1, replica_groups=mesh['expert'=8,'x'=2,'y'=4,'core'=2] {'expert'}, dimensions={0} | all-to-all | bytes 917504 | tf_op jit(solution)/shard_map/all_to_all | solution.py:295
  64.8 17.0 %all_to_all.48.in_ref.weight_ref = bf16[16,8,3584]{2,1,0:T(8,128)(2,1)} all-to-all(bf16[16,8,3584]{2,1,0:T(8,128)(2,1)} %shard_map.173), channel_id=1, replica_groups=mesh['expert'=8,'x'=2,'y'=4,'core'=2] {'expert','x'}, dimensions={0} | all-to-all | bytes 1835008 | tf_op jit(solution)/shard_map/all_to_all | solution.py:295
  84.7 3.8 %dispatch.1 = (bf16[16,16,3584]{2,1,0:T(8,128)(2,1)}, bf16[16,16,3584]{2,1,0:T(8,128)(2,1)}) custom-call(s32[8,1]{1,0:T(8,128)} %copy.20.ids_ref, s32[8]{0:T(128)} %count_ref.1, s32[8]{0:T(128)} %own_ref.3, bf16[8,16,3584]{2,1,0:T(8,128)(2,1)} %bitcast.33, bf16[8,16,3584]{2,1,0:T(8,128)(2,1)} %bitcast.34), custom_call_target="tpu_custom_call" | custom-call | tf_op jit(solution)/shard_map/dispatch/pallas_call | solution.py:110
  88.5 25.7 %all_to_all.49 = bf16[16,16,3584]{2,1,0:T(8,128)(2,1)S(1)} all-to-all(bf16[16,16,3584]{2,1,0:T(8,128)(2,1)} %get-tuple-element.38), channel_id=1, replica_groups=mesh['expert'=8,'x'=2,'y'=4,'core'=2] {'expert'}, dimensions={0} | all-to-all | bytes 3670016 | tf_op jit(solution)/shard_map/all_to_all | solution.py:295
  114.3 24.2 %all_to_all.50 = bf16[16,16,3584]{2,1,0:T(8,128)(2,1)} all-to-all(bf16[16,16,3584]{2,1,0:T(8,128)(2,1)S(1)} %copy-done.4), channel_id=1, replica_groups=mesh['expert'=8,'x'=2,'y'=4,'core'=2] {'expert'}, dimensions={0} | all-to-all | bytes 3670016 | tf_op jit(solution)/shard_map/all_to_all | solution.py:295
  138.5 6.2 %multiply_convert_fusion = (bf16[256,1024]{1,0:T(8,128)(2,1)S(1)}, f32[256,1024]{1,0:T(8,128)}) fusion(bf16[256,3584]{1,0:T(8,128)(2,1)S(1)} %bitcast.27, bf16[3584,1024]{1,0:T(8,128)(2,1)} %all-gather.3.cloned.1.call-done), kind=kOutput, calls=%fused_computation.3 | convolution fusion | flops 1880358912 | bytes 10747904 | tf_op jit(solution)/shard_map/dot_general | solution.py:363
  145.3 3.5 %pack_states.1 = bf16[8,4,224,128]{3,2,1,0:T(8,128)(2,1)} custom-call(f32[224,1024]{1,0:T(8,128)} %bitcast.36, f32[224,1024]{1,0:T(8,128)} %bitcast.37, f32[64,3584]{1,0:T(8,128)} %bitcast.38, f32[64,3584]{1,0:T(8,128)} %bitcast.39), custom_call_target="tpu_custom_call" | custom-call | tf_op jit(solution)/shard_map/pack_states/pallas_call | solution.py:154
  150.2 7.0 %shard_map.175.part_ref = bf16[512,3584]{1,0:T(8,128)(2,1)} custom-call(s32[2]{0:T(128)} %pad_add_fusion.half_ref, bf16[256,1024]{1,0:T(8,128)(2,1)} %copy-done.8, bf16[256,1024]{1,0:T(8,128)(2,1)} %copy-done.9, bf16[256,3584]{1,0:T(8,128)(2,1)} %bitcast.8.b_ref, bf16[256,3584]{1,0:T(8,128)(2,1)} %collective-permute-done.1.bo_ref), custom_call_target="tpu_custom_call" | custom-call | tf_op jit(solution)/shard_map/pallas_call | solution.py:190
  157.2 6.0 %fusion.b_ref = bf16[256,1024]{1,0:T(8,128)(2,1)S(1)} fusion(bf16[256,3584]{1,0:T(8,128)(2,1)} %bitcast.8.b_ref, bf16[1024,3584]{1,0:T(8,128)(2,1)} %all-gather.5.cloned.1.call-done, f32[256,1024]{1,0:T(8,128)} %get-tuple-element.62), kind=kOutput, calls=%fused_computation.2 | convolution fusion | flops 1881407488 | bytes 10747904 | tf_op jit(solution)/shard_map/dot_general | solution.py:374
  166.1 8.3 %shard_map.176 = bf16[1792,1024]{1,0:T(8,128)(2,1)} custom-call(s32[2]{0:T(128)} %pad_add_fusion.1.half_ref, bf16[256,3584]{1,0:T(8,128)(2,1)} %bitcast.29, bf16[256,3584]{1,0:T(8,128)(2,1)} %collective-permute-done.2.ao_ref, bf16[256,1024]{1,0:T(8,128)(2,1)} %copy-done.6, bf16[256,1024]{1,0:T(8,128)(2,1)} %copy-done.10), custom_call_target="tpu_custom_call" | custom-call | tf_op jit(solution)/shard_map/pallas_call | solution.py:190
  174.4 6.2 %all-to-all-start.6 = ((bf16[8,4,224,128]{3,2,1,0:T(8,128)(2,1)}), bf16[8,4,224,128]{3,2,1,0:T(8,128)(2,1)S(1)}, u32[]{:S(2)}, u32[]{:S(2)}) async-start(bf16[8,4,224,128]{3,2,1,0:T(8,128)(2,1)} %pack_states.1), calls=%async_computation.6 | async-start | bytes 3670016 | tf_op jit(solution)/shard_map/all_to_all | solution.py:295
  180.6 6.7 %convolution_convert_fusion = bf16[256,3584]{1,0:T(8,128)(2,1)} fusion(bf16[256,1024]{1,0:T(8,128)(2,1)S(1)} %copy-done.7, bf16[3584,1024]{1,0:T(8,128)(2,1)} %all-gather.3.cloned.1.call-done), kind=kOutput, calls=%fused_computation | convolution fusion | flops 1879965696 | bytes 9699328 | tf_op jit(solution)/shard_map/dot_general | solution.py:383
  187.3 33.4 %all-to-all-done.6.in_ref = bf16[8,4,224,128]{3,2,1,0:T(8,128)(2,1)S(1)} async-done(((bf16[8,4,224,128]{3,2,1,0:T(8,128)(2,1)}), bf16[8,4,224,128]{3,2,1,0:T(8,128)(2,1)S(1)}, u32[]{:S(2)}, u32[]{:S(2)}) %all-to-all-start.6) | async-done | bytes 1835040 | tf_op jit(solution)/shard_map/all_to_all | solution.py:295
  222.0 8.9 %all-to-all-start.7 = ((bf16[16,16,3584]{2,1,0:T(8,128)(2,1)}), bf16[16,16,3584]{2,1,0:T(8,128)(2,1)S(1)}, u32[]{:S(2)}, u32[]{:S(2)}) async-start(bf16[16,16,3584]{2,1,0:T(8,128)(2,1)} %bitcast.30), calls=%async_computation.7 | async-start | bytes 3670016 | tf_op jit(solution)/shard_map/all_to_all | solution.py:295
  239.1 32.2 %all-to-all-done.7.ret_ref = bf16[16,16,3584]{2,1,0:T(8,128)(2,1)S(1)} async-done(((bf16[16,16,3584]{2,1,0:T(8,128)(2,1)}), bf16[16,16,3584]{2,1,0:T(8,128)(2,1)S(1)}, u32[]{:S(2)}, u32[]{:S(2)}) %all-to-all-start.7) | async-done | bytes 1835040 | tf_op jit(solution)/shard_map/all_to_all | solution.py:295
  272.5 9.0 %all-to-all-start.8 = ((bf16[8,4,224,128]{3,2,1,0:T(8,128)(2,1)}), bf16[8,4,224,128]{3,2,1,0:T(8,128)(2,1)S(1)}, u32[]{:S(2)}, u32[]{:S(2)}) async-start(bf16[8,4,224,128]{3,2,1,0:T(8,128)(2,1)} %shard_map.177), calls=%async_computation.8 | async-start | bytes 3670016 | tf_op jit(solution)/shard_map/all_to_all | solution.py:295
  283.1 3.6 %relay.1 = (bf16[128,3584]{1,0:T(8,128)(2,1)}, bf16[128,3584]{1,0:T(8,128)(2,1)}) custom-call(bf16[512,3584]{1,0:T(8,128)(2,1)} %shard_map.175.part_ref, bf16[64,3584]{1,0:T(8,128)(2,1)} %copy-done.11, bf16[64,3584]{1,0:T(8,128)(2,1)} %copy-done.12), custom_call_target="tpu_custom_call" | custom-call | tf_op jit(solution)/shard_map/relay/pallas_call | solution.py:216
  289.9 21.1 %collective-permute-done.6.below_ref = bf16[128,3584]{1,0:T(8,128)(2,1)S(1)} collective-permute-done((bf16[128,3584]{1,0:T(8,128)(2,1)}, bf16[128,3584]{1,0:T(8,128)(2,1)S(1)}, u32[]{:S(2)}, u32[]{:S(2)}) %collective-permute-start.6) | collective-permute-done | bytes 917536 | tf_op jit(solution)/shard_map/ppermute | solution.py:381
  311.9 3.1 finish.1
  318.0 7.0 %collective-permute-done.8.other_ref = bf16[64,3584]{1,0:T(8,128)(2,1)S(1)} collective-permute-done((bf16[64,3584]{1,0:T(8,128)(2,1)}, bf16[64,3584]{1,0:T(8,128)(2,1)S(1)}, u32[]{:S(2)}, u32[]{:S(2)}) %collective-permute-start.8) | collective-permute-done | bytes 458784 | tf_op jit(solution)/shard_map/ppermute | solution.py:394
  326.4 4.1 %shard_map.179 = (f32[64,3584]{1,0:T(8,128)}, f32[64,3584]{1,0:T(8,128)}, f32[64,3584]{1,0:T(8,128)}) custom-call(s32[1]{0:T(128)} %bitcast.14.x_ref, bf16[16,8,3584]{2,1,0:T(8,128)(2,1)} %all_to_all.48.in_ref.weight_ref, bf16[8,4,224,128]{3,2,1,0:T(8,128)(2,1)} %copy-done, f32[64,3584]{1,0:T(8,128)} %get-tuple-element.52.grad_ref, bf16[64,3584]{1,0:T(8,128)(2,1)} %copy-done.13), custom_call_target="tpu_custom_call" | custom-call | tf_op jit(solution)/shard_map/pallas_call | solution.py:275
  330.5 4.0 %shard_map.178 = (f32[224,1024]{1,0:T(8,128)}, f32[224,1024]{1,0:T(8,128)}, f32[224,1024]{1,0:T(8,128)}) custom-call(s32[1]{0:T(128)} %bitcast.14.x_ref, bf16[16,224,128]{2,1,0:T(8,128)(2,1)} %all_to_all.46.in_ref.weight_ref, bf16[8,4,224,128]{3,2,1,0:T(8,128)(2,1)} %copy-done, bf16[224,1024]{1,0:T(8,128)(2,1)} %reduce-scatter.2.cloned.1.call-done.grad_ref), custom_call_target="tpu_custom_call" | custom-call | tf_op jit(solution)/shard_map/pallas_call | solution.py:275
  (69 shorter events, 37.7 us)
Async XLA Ops:
  7.2 131.3 %all-gather.3.cloned.1.call-start = ((), (), s32[]{:S(2)}) async-start(), calls=%async_computation.10 | async-start | bytes 8257536 | tf_op jit(solution)/shard_map/all_gather | solution.py:336
  47.2 2.6 copy-start.14
  49.7 107.5 %all-gather.5.cloned.1.call-start = ((), (), s32[]{:S(2)}) async-start(), calls=%async_computation.11 | async-start | bytes 8257536 | tf_op jit(solution)/shard_map/all_gather | solution.py:341
  81.8 2.3 copy-start.15
  84.0 246.5 %reduce-scatter.2.cloned.1.call-start = ((), (), s32[]{:S(2)}) async-start(), calls=%async_computation.12 | async-start | bytes 4128768 | tf_op jit(solution)/shard_map/reduce_scatter | solution.py:378
  88.5 25.7 %copy-start.4 = (bf16[16,16,3584]{2,1,0:T(8,128)(2,1)S(1)}, bf16[16,16,3584]{2,1,0:T(8,128)(2,1)}, u32[]{:S(2)}) copy-start(bf16[16,16,3584]{2,1,0:T(8,128)(2,1)} %get-tuple-element.39) | copy-start | bytes 5505028
  114.3 30.9 %copy-start.1 = (bf16[16,16,3584]{2,1,0:T(8,128)(2,1)}, bf16[16,16,3584]{2,1,0:T(8,128)(2,1)S(1)}, u32[]{:S(2)}) copy-start(bf16[16,16,3584]{2,1,0:T(8,128)(2,1)S(1)} %all_to_all.49) | copy-start | bytes 5505028
  138.5 10.9 %collective-permute-start.1 = (bf16[256,3584]{1,0:T(8,128)(2,1)}, bf16[256,3584]{1,0:T(8,128)(2,1)}, u32[]{:S(2)}, u32[]{:S(2)}) collective-permute-start(bf16[256,3584]{1,0:T(8,128)(2,1)} %bitcast.8.b_ref), channel_id=1, source_target_pairs={{0,1},{1,0},{2,3},{3,2},{4,5},{5,4},{6,7},{7,6},{8,9},{9,8},{10,11... | collective-permute-start | bytes 5505032 | tf_op jit(solution)/shard_map/ppermute | solution.py:299
  144.7 4.1 %copy-start.8 = (bf16[256,1024]{1,0:T(8,128)(2,1)}, bf16[256,1024]{1,0:T(8,128)(2,1)S(1)}, u32[]{:S(2)}) copy-start(bf16[256,1024]{1,0:T(8,128)(2,1)S(1)} %get-tuple-element.61.a_ref) | copy-start | bytes 1572868
  144.7 4.7 %collective-permute-start = (bf16[256,1024]{1,0:T(8,128)(2,1)S(1)}, bf16[256,1024]{1,0:T(8,128)(2,1)S(1)}, u32[]{:S(2)}, u32[]{:S(2)}) collective-permute-start(bf16[256,1024]{1,0:T(8,128)(2,1)S(1)} %get-tuple-element.61.a_ref), channel_id=1, source_target_pairs={{0,1},{1,0},{2,3},{3,2},{4,5},{5,4},{6,7},{7,6},{8,9},{9,8},{10,11... | collective-permute-start | bytes 1572872 | tf_op jit(solution)/shard_map/ppermute | solution.py:299
  145.2 19.1 %collective-permute-start.2 = (bf16[256,3584]{1,0:T(8,128)(2,1)S(1)}, bf16[256,3584]{1,0:T(8,128)(2,1)}, u32[]{:S(2)}, u32[]{:S(2)}) collective-permute-start(bf16[256,3584]{1,0:T(8,128)(2,1)S(1)} %bitcast.28), channel_id=1, source_target_pairs={{0,1},{1,0},{2,3},{3,2},{4,5},{5,4},{6,7},{7,6},{8,9},{9,8},{10,11... | collective-permute-start | bytes 5505032 | tf_op jit(solution)/shard_map/ppermute | solution.py:299
  163.2 2.1 copy-start.6
  163.2 2.0 collective-permute-start.3
  174.3 6.2 %copy-start.7 = (bf16[256,1024]{1,0:T(8,128)(2,1)S(1)}, bf16[256,1024]{1,0:T(8,128)(2,1)}, u32[]{:S(2)}) copy-start(bf16[256,1024]{1,0:T(8,128)(2,1)} %copy-done.6) | copy-start | bytes 1572868
  174.4 46.3 %all-to-all-start.6 = ((bf16[8,4,224,128]{3,2,1,0:T(8,128)(2,1)}), bf16[8,4,224,128]{3,2,1,0:T(8,128)(2,1)S(1)}, u32[]{:S(2)}, u32[]{:S(2)}) async-start(bf16[8,4,224,128]{3,2,1,0:T(8,128)(2,1)} %pack_states.1), calls=%async_computation.6 | async-start | bytes 3670016 | tf_op jit(solution)/shard_map/all_to_all | solution.py:295
  220.7 1.3 copy-start.3
  222.0 49.3 %all-to-all-start.7 = ((bf16[16,16,3584]{2,1,0:T(8,128)(2,1)}), bf16[16,16,3584]{2,1,0:T(8,128)(2,1)S(1)}, u32[]{:S(2)}, u32[]{:S(2)}) async-start(bf16[16,16,3584]{2,1,0:T(8,128)(2,1)} %bitcast.30), calls=%async_computation.7 | async-start | bytes 3670016 | tf_op jit(solution)/shard_map/all_to_all | solution.py:295
  232.9 48.6 %collective-permute-start.4 = (bf16[64,3584]{1,0:T(8,128)(2,1)}, bf16[64,3584]{1,0:T(8,128)(2,1)S(1)}, u32[]{:S(2)}, u32[]{:S(2)}) collective-permute-start(bf16[64,3584]{1,0:T(8,128)(2,1)} %get-tuple-element.60), channel_id=1, source_target_pairs={{0,2},{2,4},{4,6},{6,0},{1,3},{3,5},{5,7},{7,1},{8,10},{10,12},{12... | collective-permute-start | bytes 1376264 | tf_op jit(solution)/shard_map/ppermute | solution.py:371
  234.9 46.7 %collective-permute-start.5 = (bf16[64,3584]{1,0:T(8,128)(2,1)S(1)}, bf16[64,3584]{1,0:T(8,128)(2,1)S(1)}, u32[]{:S(2)}, u32[]{:S(2)}) collective-permute-start(bf16[64,3584]{1,0:T(8,128)(2,1)S(1)} %get-tuple-element.59), channel_id=1, source_target_pairs={{0,6},{2,0},{4,2},{6,4},{1,7},{3,1},{5,3},{7,5},{8,14},{10,8},{12,... | collective-permute-start | bytes 1376264 | tf_op jit(solution)/shard_map/ppermute | solution.py:372
  272.5 52.5 %all-to-all-start.8 = ((bf16[8,4,224,128]{3,2,1,0:T(8,128)(2,1)}), bf16[8,4,224,128]{3,2,1,0:T(8,128)(2,1)S(1)}, u32[]{:S(2)}, u32[]{:S(2)}) async-start(bf16[8,4,224,128]{3,2,1,0:T(8,128)(2,1)} %shard_map.177), calls=%async_computation.8 | async-start | bytes 3670016 | tf_op jit(solution)/shard_map/all_to_all | solution.py:295
  286.7 24.3 %collective-permute-start.6 = (bf16[128,3584]{1,0:T(8,128)(2,1)}, bf16[128,3584]{1,0:T(8,128)(2,1)S(1)}, u32[]{:S(2)}, u32[]{:S(2)}) collective-permute-start(bf16[128,3584]{1,0:T(8,128)(2,1)} %get-tuple-element.50), channel_id=1, source_target_pairs={{0,2},{2,4},{4,6},{6,0},{1,3},{3,5},{5,7},{7,1},{8,10},{10,12},{12... | collective-permute-start | bytes 2752520 | tf_op jit(solution)/shard_map/ppermute | solution.py:381
  288.7 22.3 %collective-permute-start.7 = (bf16[128,3584]{1,0:T(8,128)(2,1)}, bf16[128,3584]{1,0:T(8,128)(2,1)}, u32[]{:S(2)}, u32[]{:S(2)}) collective-permute-start(bf16[128,3584]{1,0:T(8,128)(2,1)} %get-tuple-element.51), channel_id=1, source_target_pairs={{0,6},{2,0},{4,2},{6,4},{1,7},{3,1},{5,3},{7,5},{8,14},{10,8},{12,... | collective-permute-start | bytes 2752520 | tf_op jit(solution)/shard_map/ppermute | solution.py:382
  315.0 9.9 %collective-permute-start.8 = (bf16[64,3584]{1,0:T(8,128)(2,1)}, bf16[64,3584]{1,0:T(8,128)(2,1)S(1)}, u32[]{:S(2)}, u32[]{:S(2)}) collective-permute-start(bf16[64,3584]{1,0:T(8,128)(2,1)} %get-tuple-element.53), channel_id=1, source_target_pairs={{0,8},{8,0},{1,9},{9,1},{2,10},{10,2},{3,11},{11,3},{4,12},{12,4},... | collective-permute-start | bytes 1376264 | tf_op jit(solution)/shard_map/ppermute | solution.py:394
  325.0 1.4 copy-start
  (7 other events, 6.0 us)
Sparse Core Ops, SparseCore 0:
  49.8 44.9 all-gather.2
  97.1 45.6 all-gather.4
  174.5 126.4 reduce-scatter.1

commit v4 on v3

--- a/solution.py
+++ b/solution.py
@@ -37,41 +37,40 @@
     return jnp.concatenate([value[:, r * width : (r + 1) * width] for r in order], axis=1)
 
 
-def pack_weights_body(up_ref, down_ref, u_ref, w_ref):
-    for g in range(u_ref.shape[0]):
-        u_ref[g] = up_ref[:, g * LANE : (g + 1) * LANE].astype(BF)
-        w_ref[g] = down_ref[g * 8 : (g + 1) * 8].astype(BF)
+def pack_weights_body(up_ref, down_ref, out_ref):
+    for g in range(out_ref.shape[0]):
+        out_ref[g, 0] = up_ref[:, g * LANE : (g + 1) * LANE].astype(BF)
+        out_ref[g, 1] = to_tiles(down_ref[g * 8 : (g + 1) * 8]).astype(BF)
 
 
 def pack_weights(up, down, groups):
     return pl.pallas_call(
         pack_weights_body,
-        out_shape=(
-            jax.ShapeDtypeStruct((groups, up.shape[0], LANE), BF),
-            jax.ShapeDtypeStruct((groups, down.shape[0] // groups, down.shape[1]), BF),
-        ),
+        out_shape=jax.ShapeDtypeStruct((groups, 2, up.shape[0], LANE), BF),
         name="pack_weights",
     )(up, down)
 
 
-def unpack_up_body(in_ref, out_ref):
+def unpack_body(in_ref, up_ref, down_ref):
     groups = in_ref.shape[0] // NX
-    rows = in_ref.shape[1]
+    rows, tall = up_ref.shape[0] // NX, down_ref.shape[0] // NX
     for x in range(NX):
-        value = jnp.concatenate([in_ref[g * NX + x].astype(F32) for g in range(groups)], axis=1)
-        out_ref[x * rows : (x + 1) * rows] = lanes_taken(value, row_order()).astype(BF)
-
-
-def unpack_down_body(in_ref, out_ref):
-    groups = in_ref.shape[0] // NX
-    rows = in_ref.shape[1]
-    for x in range(NX):
-        value = jnp.concatenate([in_ref[g * NX + x].astype(F32) for g in range(groups)], axis=0)
-        out_ref[x * groups * rows : (x + 1) * groups * rows] = value.astype(BF)
-
-
-def unpack(body, shares, shape):
-    return pl.pallas_call(body, out_shape=jax.ShapeDtypeStruct(shape, BF))(shares)
+        shares = [in_ref[g * NX + x].astype(F32) for g in range(groups)]
+        up = jnp.concatenate([share[0] for share in shares], axis=1)
+        up_ref[x * rows : (x + 1) * rows] = lanes_taken(up, row_order()).astype(BF)
+        down = jnp.concatenate([from_tiles(share[1]) for share in shares], axis=0)
+        down_ref[x * tall : (x + 1) * tall] = down.astype(BF)
+
+
+def unpack_weights(shares, up_shape, down_shape):
+    return pl.pallas_call(
+        unpack_body,
+        out_shape=(
+            jax.ShapeDtypeStruct((NX * up_shape[0], up_shape[1]), BF),
+            jax.ShapeDtypeStruct((NX * down_shape[0], down_shape[1]), BF),
+        ),
+        name="unpack_weights",
+    )(shares)
 
 
 def slot_of_block(ids_ref, own_ref, b):
@@ -249,12 +248,15 @@
     return (weight - rate_value * (update + decay_value * weight), moment_new, second_new)
 
 
-def adam_up_body(x_ref, weight_ref, state_ref, grad_ref, *outs):
-    grad = lanes_taken(grad_ref[...].astype(F32), inverse(row_order()))
+def adam_up_body(x_ref, weight_ref, state_ref, grad_ref, other_ref, *outs):
+    rows = other_ref.shape[0]
+    own = grad_ref[pl.ds(pl.multiple_of(x_ref[0] * rows, 16), rows)]
+    both = own.astype(F32) + other_ref[...].astype(F32)
+    grad = lanes_taken(both, inverse(row_order()))
     for g in range(state_ref.shape[0]):
         lanes = slice(g * LANE, (g + 1) * LANE)
         m, v = (state_ref[g, i].astype(F32) for i in range(2))
-        w = weight_ref[g * NX + x_ref[0]].astype(F32)
+        w = weight_ref[g * NX + x_ref[0], 0].astype(F32)
         for ref, value in zip(outs, adam_update(w, m, v, grad[:, lanes])):
             ref[:, lanes] = value
 
@@ -263,7 +265,7 @@
     for g in range(state_ref.shape[0]):
         rows = slice(g * 8, (g + 1) * 8)
         m, v = (from_tiles(state_ref[g, i].astype(F32)) for i in range(2))
-        w = weight_ref[g * NX + x_ref[0]].astype(F32)
+        w = from_tiles(weight_ref[g * NX + x_ref[0], 0].astype(F32))
         grad = grad_ref[rows] + other_ref[rows].astype(F32)
         for ref, value in zip(outs, adam_update(w, m, v, grad)):
             ref[rows] = value
@@ -277,10 +279,10 @@
         grid=(1,),
         in_specs=[
             smem(),
-            pl.BlockSpec(weights.shape, lambda i: (0, 0, 0)),
+            pl.BlockSpec((weights.shape[0], 1, rows, wide), lambda i: (0, which, 0, 0)),
             pl.BlockSpec((groups, 2, rows, wide), lambda i: (0, which, 0, 0)),
         ]
-        + [full] * len(grads),
+        + [pl.BlockSpec(g.shape, lambda i: (0, 0)) for g in grads],
         out_specs=[full] * 3,
         out_shape=[jax.ShapeDtypeStruct(shape, F32)] * 3,
     )(x_at, weights, states, *grads)
@@ -324,20 +326,12 @@
     down_place = jnp.stack([core_at, y_at])
     up_shape, down_shape = up_weight.shape[1:], down_weight.shape[1:]
 
-    up_packed, down_packed = pack_weights(up_weight[0], down_weight[0], groups)
-
-    def weight_moved(packed):
-        spread = exchange(packed, "expert")
-        ordered = order_states(old_owner, new_owner, spread, NX)
-        return exchange(ordered, ("expert", "x"))
-
-    up_shares = weight_moved(up_packed)
-    up_pair = unpack(unpack_up_body, up_shares, (NX * up_shape[0], up_shape[1]))
+    packed = pack_weights(up_weight[0], down_weight[0], groups)
+    spread = exchange(packed, "expert")
+    ordered = order_states(old_owner, new_owner, spread, NX)
+    weights = exchange(ordered, ("expert", "x"))
+    up_pair, down_pair = unpack_weights(weights, up_shape, down_shape)
     up_mat = lax.all_gather(up_pair, ("core", "y"), axis=0, tiled=True)
-
-    down_packed, up_pair = lax.optimization_barrier((down_packed, up_pair))
-    down_shares = weight_moved(down_packed)
-    down_pair = unpack(unpack_down_body, down_shares, (NX * down_shape[0], down_shape[1]))
     down_mat = lax.all_gather(down_pair, ("core", "y"), axis=0, tiled=True)
 
     send_x, send_dy = dispatch(
@@ -370,32 +364,31 @@
     falling = [(i, (i - 1) % NY) for i in range(NY)]
     below = lax.ppermute(down_part[4 * tall : 5 * tall], "y", rising)
     above = lax.ppermute(down_part[5 * tall : 6 * tall], "y", falling)
-    upstream, _ = lax.optimization_barrier((upstream, down_part))
+    going_up, going_down = relay(down_part, below, above)
+    below = lax.ppermute(going_up, "y", rising)
+    above = lax.ppermute(going_down, "y", falling)
+    ordered = order_states(old_owner, new_owner, shares, 1)
+    states = exchange(ordered, "expert")
     back = lax.dot_general(upstream, down_mat, (((1,), (1,)), ((), ())), preferred_element_type=F32)
     pre_grad = (back * slopes).astype(BF)
     pre_grad_other = from_partner(pre_grad)
     up_part = weight_grad(up_place, inputs, inputs_other, pre_grad, pre_grad_other, 256)
-    up_grad = lax.psum_scatter(up_part, ("y", "x"), scatter_dimension=0, tiled=True)
+    up_sum = lax.psum_scatter(up_part, "y", scatter_dimension=0, tiled=True)
     pre_grad, up_part = lax.optimization_barrier((pre_grad, up_part))
-    going_up, going_down = relay(down_part, below, above)
-    below = lax.ppermute(going_up, "y", rising)
-    above = lax.ppermute(going_down, "y", falling)
     input_grad = lax.dot_general(
         pre_grad, up_mat, (((1,), (1,)), ((), ())), preferred_element_type=F32
     ).astype(BF)
-    input_grad, shares = lax.optimization_barrier((input_grad, shares))
+    input_grad, states = lax.optimization_barrier((input_grad, states))
     returned = exchange(input_grad.reshape(-1, rows, features), "expert")
-    ordered = order_states(old_owner, new_owner, shares, 1)
-    ordered, returned = lax.optimization_barrier((ordered, returned))
-    states = exchange(ordered, "expert")
     token_grad = combine(block_expert, new_owner, returned).reshape(tok_rows, features)
 
+    swap = [(0, 1), (1, 0)]
     down_own, down_send = finish(x_at, down_part, below, above)
-    down_other = lax.ppermute(down_send, "x", [(0, 1), (1, 0)])
-    down_new = adam(
-        adam_down_body, x_at, down_shares, states, 1, (down_own, down_other), down_shape,
-    )
-    up_new = adam(adam_up_body, x_at, up_shares, states, 0, (up_grad,), up_shape)
+    down_other = lax.ppermute(down_send, "x", swap)
+    up_send = lax.dynamic_slice_in_dim(up_sum, (1 - x_at[0]) * up_shape[0], up_shape[0])
+    up_other = lax.ppermute(up_send, "x", swap)
+    down_new = adam(adam_down_body, x_at, weights, states, 1, (down_own, down_other), down_shape)
+    up_new = adam(adam_up_body, x_at, weights, states, 0, (up_sum, up_other), up_shape)
     return (
         token_grad,
         up_new[0][None],

time: 343 us -> 312 us (0.910)
  blocking collectives: 115 us -> 77.8 us
  starting transfers between devices: 32.2 us -> 36.8 us
  waiting for transfers between devices: 94.6 us -> 98.6 us
    all_to_all x6 -> x3, blocking collectives: 115 us -> 77.8 us  [exchange(): return lax.all_to_all(array, axis, split_axis=0, concat_axis=0, tiled=True)]
    all_gather x1, waiting for transfers between devices: 0.01 us -> 27.3 us  [step(): down_mat = lax.all_gather(down_pair, ('core', 'y'), axis=0, tiled=True)]
    all_to_all x3 -> x4, waiting for transfers between devices: 65.5 us -> 42.3 us  [exchange(): return lax.all_to_all(array, axis, split_axis=0, concat_axis=0, tiled=True)]
    all_to_all x3 -> x4, starting transfers between devices: 24.2 us -> 27.4 us  [exchange(): return lax.all_to_all(array, axis, split_axis=0, concat_axis=0, tiled=True)]
    ppermute x1 -> x2, waiting for transfers between devices: 6.96 us -> 8.78 us  [the longest x1 7.73 us: step(): down_other = lax.ppermute(down_send, 'x', swap)]
    pallas_call x3 -> x2, Pallas kernels: 7 us -> 5.43 us  [order_states(): pl.pallas_call(order_body, in_specs=[smem(), smem(), vmem()], out_shape=j...]
    pallas_call x5 -> x4, Pallas kernels: 15.3 us -> 14 us  [the longest x2 8.41 us: adam(): pl.pallas_call(body, grid=(1,), in_specs=[smem(), pl.BlockSpec((weights.s...]
    unnamed x33 -> x31, local copies, waits for them, and re-layouts: 8.61 us -> 9.17 us
  transfers between devices with their start and end apart: 15 -> 17, of which waited for: 5 -> 8; matrix products, arithmetic and copies ran while one was open for 7% -> 8% of each run, Pallas kernels for 10% -> 10%
where the time goes in v4:
time: 312 us; the launch traced here: 311 us
  waiting for transfers between devices  98.6 us (32%)
  blocking collectives  77.8 us (25%)
  Pallas kernels  51.6 us (17%)
  starting transfers between devices  36.8 us (12%)
  matrix products  18.8 us (6%)
  between operations  13.8 us (4%)
  local copies, waits for them, and re-layouts  12.3 us (4%)
    all_to_all x3, blocking collectives, exchange(): return lax.all_to_all(array, axis, split_axis=0, concat_axis=0, tiled=True)  77.8 us
    all_to_all x4, waiting for transfers between devices, exchange(): return lax.all_to_all(array, axis, split_axis=0, concat_axis=0, tiled=True)  42.3 us
    all_to_all x4, starting transfers between devices, exchange(): return lax.all_to_all(array, axis, split_axis=0, concat_axis=0, tiled=True)  27.4 us
    all_gather x1, waiting for transfers between devices, step(): down_mat = lax.all_gather(down_pair, ('core', 'y'), axis=0, tiled=True)  27.3 us
    ppermute x1, waiting for transfers between devices, step(): below = lax.ppermute(going_up, 'y', rising)  18.4 us
    pallas_call x2, Pallas kernels, weight_grad(): pl.pallas_call(weight_grad_body, grid_spec=pltpu.PrefetchScalarGridSpec(n...  15.3 us
    unnamed x31, local copies, waits for them, and re-layouts  9.17 us
    pallas_call x2, Pallas kernels, adam(): pl.pallas_call(body, grid=(1,), in_specs=[smem(), pl.BlockSpec((weights.s...  8.41 us
  transfers between devices with their start and end apart: 17, of which 8 were waited for; matrix products, arithmetic and copies ran while one was open for 8% of the time, Pallas kernels for 10%

profile of v4, /device:TPU:4, one launch (start us, length us, event | category | flops | bytes accessed | tf_op | source)
XLA Modules:
  0.0 310.8 jit_solution(221269922667678506)
XLA Ops:
  9.7 21.5 %all_to_all.35.in_ref = bf16[8,2,224,128]{3,2,1,0:T(8,128)(2,1)} all-to-all(bf16[8,2,224,128]{3,2,1,0:T(8,128)(2,1)} %pack_weights.1), channel_id=1, replica_groups=mesh['expert'=8,'x'=2,'y'=4,'core'=2] {'expert'}, dimensions={0} | all-to-all | bytes 1835008 | tf_op jit(solution)/shard_map/all_to_all | solution.py:297
  33.8 29.5 %all_to_all.36.in_ref.weight_ref = bf16[16,2,224,128]{3,2,1,0:T(8,128)(2,1)} all-to-all(bf16[16,2,224,128]{3,2,1,0:T(8,128)(2,1)} %shard_map.171), channel_id=1, replica_groups=mesh['expert'=8,'x'=2,'y'=4,'core'=2] {'expert','x'}, dimensions={0} | all-to-all | bytes 3670016 | tf_op jit(solution)/shard_map/all_to_all | solution.py:297
  63.3 3.1 unpack_weights.1
  67.8 3.9 %dispatch.1 = (bf16[16,16,3584]{2,1,0:T(8,128)(2,1)}, bf16[16,16,3584]{2,1,0:T(8,128)(2,1)}) custom-call(s32[8,1]{1,0:T(8,128)} %copy.20.ids_ref, s32[8]{0:T(128)} %count_ref.1, s32[8]{0:T(128)} %own_ref.3, bf16[8,16,3584]{2,1,0:T(8,128)(2,1)} %bitcast.31, bf16[8,16,3584]{2,1,0:T(8,128)(2,1)} %bitcast.32), custom_call_target="tpu_custom_call" | custom-call | tf_op jit(solution)/shard_map/dispatch/pallas_call | solution.py:109
  71.7 26.8 %all_to_all.37 = bf16[16,16,3584]{2,1,0:T(8,128)(2,1)S(1)} all-to-all(bf16[16,16,3584]{2,1,0:T(8,128)(2,1)} %get-tuple-element.32), channel_id=1, replica_groups=mesh['expert'=8,'x'=2,'y'=4,'core'=2] {'expert'}, dimensions={0} | all-to-all | bytes 3670016 | tf_op jit(solution)/shard_map/all_to_all | solution.py:297
  98.5 6.9 %all-to-all-start.3 = ((bf16[16,16,3584]{2,1,0:T(8,128)(2,1)}), bf16[16,16,3584]{2,1,0:T(8,128)(2,1)}, u32[]{:S(2)}, u32[]{:S(2)}) async-start(bf16[16,16,3584]{2,1,0:T(8,128)(2,1)} %get-tuple-element.33), calls=%async_computation.3 | async-start | bytes 3670016 | tf_op jit(solution)/shard_map/all_to_all | solution.py:297
  105.4 3.5 %pack_states.1 = bf16[8,4,224,128]{3,2,1,0:T(8,128)(2,1)} custom-call(f32[224,1024]{1,0:T(8,128)} %bitcast.36, f32[224,1024]{1,0:T(8,128)} %bitcast.37, f32[64,3584]{1,0:T(8,128)} %bitcast.38, f32[64,3584]{1,0:T(8,128)} %bitcast.39), custom_call_target="tpu_custom_call" | custom-call | tf_op jit(solution)/shard_map/pack_states/pallas_call | solution.py:153
  108.9 16.6 %all-to-all-done.3 = bf16[16,16,3584]{2,1,0:T(8,128)(2,1)} async-done(((bf16[16,16,3584]{2,1,0:T(8,128)(2,1)}), bf16[16,16,3584]{2,1,0:T(8,128)(2,1)}, u32[]{:S(2)}, u32[]{:S(2)}) %all-to-all-start.3) | async-done | bytes 1835040 | tf_op jit(solution)/shard_map/all_to_all | solution.py:297
  125.6 6.3 %multiply_convert_fusion = (bf16[256,1024]{1,0:T(8,128)(2,1)S(1)}, f32[256,1024]{1,0:T(8,128)}) fusion(bf16[256,3584]{1,0:T(8,128)(2,1)S(1)} %bitcast.28, bf16[3584,1024]{1,0:T(8,128)(2,1)} %all-gather.5.cloned.1.call-done), kind=kOutput, calls=%fused_computation.3 | convolution fusion | flops 1880358912 | bytes 10747904 | tf_op jit(solution)/shard_map/dot_general | solution.py:357
  131.9 27.3 %all-gather.3.cloned.1.call-done = bf16[1024,3584]{1,0:T(8,128)(2,1)} async-done(((bf16[128,3584]{1,0:T(8,128)(2,1)}), bf16[1024,3584]{1,0:T(8,128)(2,1)}) %all-gather.3.cloned.1.call-update) | async-done | bytes 7340048 | tf_op jit(solution)/shard_map/all_gather | solution.py:335
  159.2 6.0 %fusion.b_ref = bf16[256,1024]{1,0:T(8,128)(2,1)S(1)} fusion(bf16[256,3584]{1,0:T(8,128)(2,1)} %bitcast.8.b_ref, bf16[1024,3584]{1,0:T(8,128)(2,1)} %all-gather.3.cloned.1.call-done, f32[256,1024]{1,0:T(8,128)} %get-tuple-element.54), kind=kOutput, calls=%fused_computation.2 | convolution fusion | flops 1881407488 | bytes 10747904 | tf_op jit(solution)/shard_map/dot_general | solution.py:372
  168.0 8.3 %shard_map.172 = bf16[1792,1024]{1,0:T(8,128)(2,1)} custom-call(s32[2]{0:T(128)} %pad_add_fusion.half_ref, bf16[256,3584]{1,0:T(8,128)(2,1)} %bitcast.29, bf16[256,3584]{1,0:T(8,128)(2,1)} %collective-permute-done.ao_ref, bf16[256,1024]{1,0:T(8,128)(2,1)} %copy-done.5, bf16[256,1024]{1,0:T(8,128)(2,1)} %copy-done.9), custom_call_target="tpu_custom_call" | custom-call | tf_op jit(solution)/shard_map/pallas_call | solution.py:189
  176.6 7.4 %all-to-all-start.4 = ((bf16[8,4,224,128]{3,2,1,0:T(8,128)(2,1)}), bf16[8,4,224,128]{3,2,1,0:T(8,128)(2,1)S(1)}, u32[]{:S(2)}, u32[]{:S(2)}) async-start(bf16[8,4,224,128]{3,2,1,0:T(8,128)(2,1)} %pack_states.1), calls=%async_computation.4 | async-start | bytes 3670016 | tf_op jit(solution)/shard_map/all_to_all | solution.py:297
  184.0 23.4 %all-to-all-done.4.in_ref = bf16[8,4,224,128]{3,2,1,0:T(8,128)(2,1)S(1)} async-done(((bf16[8,4,224,128]{3,2,1,0:T(8,128)(2,1)}), bf16[8,4,224,128]{3,2,1,0:T(8,128)(2,1)S(1)}, u32[]{:S(2)}, u32[]{:S(2)}) %all-to-all-start.4) | async-done | bytes 1835040 | tf_op jit(solution)/shard_map/all_to_all | solution.py:297
  211.6 6.2 %all-to-all-start.5 = ((bf16[8,4,224,128]{3,2,1,0:T(8,128)(2,1)}), bf16[8,4,224,128]{3,2,1,0:T(8,128)(2,1)S(1)}, u32[]{:S(2)}, u32[]{:S(2)}) async-start(bf16[8,4,224,128]{3,2,1,0:T(8,128)(2,1)} %shard_map.173), calls=%async_computation.5 | async-start | bytes 3670016 | tf_op jit(solution)/shard_map/all_to_all | solution.py:297
  219.2 7.0 %shard_map.175.part_ref = bf16[512,3584]{1,0:T(8,128)(2,1)} custom-call(s32[2]{0:T(128)} %pad_add_fusion.1.half_ref, bf16[256,1024]{1,0:T(8,128)(2,1)} %copy-done.7, bf16[256,1024]{1,0:T(8,128)(2,1)} %copy-done.8, bf16[256,3584]{1,0:T(8,128)(2,1)} %bitcast.8.b_ref, bf16[256,3584]{1,0:T(8,128)(2,1)} %collective-permute-done.4.bo_ref), custom_call_target="tpu_custom_call" | custom-call | tf_op jit(solution)/shard_map/pallas_call | solution.py:189
  231.5 6.5 %convolution_convert_fusion = bf16[256,3584]{1,0:T(8,128)(2,1)} fusion(bf16[256,1024]{1,0:T(8,128)(2,1)S(1)} %copy-done.6, bf16[3584,1024]{1,0:T(8,128)(2,1)} %all-gather.5.cloned.1.call-done), kind=kOutput, calls=%fused_computation | convolution fusion | flops 1879965696 | bytes 9699328 | tf_op jit(solution)/shard_map/dot_general | solution.py:378
  241.6 6.9 %all-to-all-start.6 = ((bf16[16,16,3584]{2,1,0:T(8,128)(2,1)}), bf16[16,16,3584]{2,1,0:T(8,128)(2,1)}, u32[]{:S(2)}, u32[]{:S(2)}) async-start(bf16[16,16,3584]{2,1,0:T(8,128)(2,1)} %bitcast.30), calls=%async_computation.6 | async-start | bytes 3670016 | tf_op jit(solution)/shard_map/all_to_all | solution.py:297
  250.0 3.7 %relay.1 = (bf16[128,3584]{1,0:T(8,128)(2,1)}, bf16[128,3584]{1,0:T(8,128)(2,1)}) custom-call(bf16[512,3584]{1,0:T(8,128)(2,1)} %shard_map.175.part_ref, bf16[64,3584]{1,0:T(8,128)(2,1)} %copy-done.10, bf16[64,3584]{1,0:T(8,128)(2,1)} %copy-done.11), custom_call_target="tpu_custom_call" | custom-call | tf_op jit(solution)/shard_map/relay/pallas_call | solution.py:215
  256.9 18.4 %collective-permute-done.7.below_ref = bf16[128,3584]{1,0:T(8,128)(2,1)S(1)} collective-permute-done((bf16[128,3584]{1,0:T(8,128)(2,1)}, bf16[128,3584]{1,0:T(8,128)(2,1)S(1)}, u32[]{:S(2)}, u32[]{:S(2)}) %collective-permute-start.7) | collective-permute-done | bytes 917536 | tf_op jit(solution)/shard_map/ppermute | solution.py:368
  276.5 3.1 %finish.1 = (f32[64,3584]{1,0:T(8,128)}, bf16[64,3584]{1,0:T(8,128)(2,1)}) custom-call(s32[1]{0:T(128)} %bitcast.13.x_ref, bf16[512,3584]{1,0:T(8,128)(2,1)} %shard_map.175.part_ref, bf16[128,3584]{1,0:T(8,128)(2,1)} %copy-done.3, bf16[128,3584]{1,0:T(8,128)(2,1)} %copy-done.4), custom_call_target="tpu_custom_call" | custom-call | tf_op jit(solution)/shard_map/finish/pallas_call | solution.py:231
  285.5 7.7 %collective-permute-done.9.other_ref = bf16[64,3584]{1,0:T(8,128)(2,1)S(1)} collective-permute-done((bf16[64,3584]{1,0:T(8,128)(2,1)}, bf16[64,3584]{1,0:T(8,128)(2,1)S(1)}, u32[]{:S(2)}, u32[]{:S(2)}) %collective-permute-start.9) | collective-permute-done | bytes 458784 | tf_op jit(solution)/shard_map/ppermute | solution.py:387
  294.0 4.1 %shard_map.176 = (f32[64,3584]{1,0:T(8,128)}, f32[64,3584]{1,0:T(8,128)}, f32[64,3584]{1,0:T(8,128)}) custom-call(s32[1]{0:T(128)} %bitcast.13.x_ref, bf16[16,2,224,128]{3,2,1,0:T(8,128)(2,1)} %all_to_all.36.in_ref.weight_ref, bf16[8,4,224,128]{3,2,1,0:T(8,128)(2,1)} %copy-done, f32[64,3584]{1,0:T(8,128)} %get-tuple-element.44.grad_ref, ...), custom_call_target="tpu_custom_call" | custom-call | tf_op jit(solution)/shard_map/pallas_call | solution.py:277
  300.0 4.3 %shard_map.174 = (f32[224,1024]{1,0:T(8,128)}, f32[224,1024]{1,0:T(8,128)}, f32[224,1024]{1,0:T(8,128)}) custom-call(s32[1]{0:T(128)} %bitcast.13.x_ref, bf16[16,2,224,128]{3,2,1,0:T(8,128)(2,1)} %all_to_all.36.in_ref.weight_ref, bf16[8,4,224,128]{3,2,1,0:T(8,128)(2,1)} %copy-done, bf16[448,1024]{1,0:T(8,128)(2,1)} %reduce-scatter.2.cloned.1.call-done.grad_ref, ...), custom_call_target="tpu_custom_call" | custom-call | tf_op jit(solution)/shard_map/pallas_call | solution.py:277
  (67 shorter events, 38.5 us)
Async XLA Ops:
  7.2 118.4 %all-gather.5.cloned.1.call-start = ((), (), s32[]{:S(2)}) async-start(), calls=%async_computation.9 | async-start | bytes 8257536 | tf_op jit(solution)/shard_map/all_gather | solution.py:334
  63.3 3.9 %copy-start.14 = (s32[8,1]{0,1:T(1,128)S(1)}, s32[8,1]{0,1:T(1,128)}, u32[]{:S(2)}) copy-start(s32[8,1]{0,1:T(1,128)} %param.14) | copy-start | bytes 100
  66.4 92.8 %all-gather.3.cloned.1.call-start = ((), (), s32[]{:S(2)}) async-start(), calls=%async_computation.8 | async-start | bytes 8257536 | tf_op jit(solution)/shard_map/all_gather | solution.py:335
  98.5 27.0 %copy-start.1 = (bf16[16,16,3584]{2,1,0:T(8,128)(2,1)}, bf16[16,16,3584]{2,1,0:T(8,128)(2,1)S(1)}, u32[]{:S(2)}) copy-start(bf16[16,16,3584]{2,1,0:T(8,128)(2,1)S(1)} %all_to_all.37) | copy-start | bytes 5505028
  98.5 27.0 %all-to-all-start.3 = ((bf16[16,16,3584]{2,1,0:T(8,128)(2,1)}), bf16[16,16,3584]{2,1,0:T(8,128)(2,1)}, u32[]{:S(2)}, u32[]{:S(2)}) async-start(bf16[16,16,3584]{2,1,0:T(8,128)(2,1)} %get-tuple-element.33), calls=%async_computation.3 | async-start | bytes 3670016 | tf_op jit(solution)/shard_map/all_to_all | solution.py:297
  105.4 175.4 %reduce-scatter.2.cloned.1.call-start = ((), (), s32[]{:S(2)}) async-start(), calls=%async_computation.10 | async-start | bytes 4587520 | tf_op jit(solution)/shard_map/reduce_scatter | solution.py:376
  108.9 57.2 %collective-permute-start = (bf16[256,3584]{1,0:T(8,128)(2,1)S(1)}, bf16[256,3584]{1,0:T(8,128)(2,1)}, u32[]{:S(2)}, u32[]{:S(2)}) collective-permute-start(bf16[256,3584]{1,0:T(8,128)(2,1)S(1)} %bitcast.27), channel_id=1, source_target_pairs={{0,1},{1,0},{2,3},{3,2},{4,5},{5,4},{6,7},{7,6},{8,9},{9,8},{10,11... | collective-permute-start | bytes 5505032 | tf_op jit(solution)/shard_map/ppermute | solution.py:301
  131.9 52.1 %copy-start.7 = (bf16[256,1024]{1,0:T(8,128)(2,1)}, bf16[256,1024]{1,0:T(8,128)(2,1)S(1)}, u32[]{:S(2)}) copy-start(bf16[256,1024]{1,0:T(8,128)(2,1)S(1)} %get-tuple-element.53.a_ref) | copy-start | bytes 1572868
  165.2 2.0 copy-start.5
  165.2 2.0 collective-permute-start.1
  176.3 42.1 %collective-permute-start.4 = (bf16[256,3584]{1,0:T(8,128)(2,1)}, bf16[256,3584]{1,0:T(8,128)(2,1)}, u32[]{:S(2)}, u32[]{:S(2)}) collective-permute-start(bf16[256,3584]{1,0:T(8,128)(2,1)} %bitcast.8.b_ref), channel_id=1, source_target_pairs={{0,1},{1,0},{2,3},{3,2},{4,5},{5,4},{6,7},{7,6},{8,9},{9,8},{10,11... | collective-permute-start | bytes 5505032 | tf_op jit(solution)/shard_map/ppermute | solution.py:301
  176.6 30.8 %all-to-all-start.4 = ((bf16[8,4,224,128]{3,2,1,0:T(8,128)(2,1)}), bf16[8,4,224,128]{3,2,1,0:T(8,128)(2,1)S(1)}, u32[]{:S(2)}, u32[]{:S(2)}) async-start(bf16[8,4,224,128]{3,2,1,0:T(8,128)(2,1)} %pack_states.1), calls=%async_computation.4 | async-start | bytes 3670016 | tf_op jit(solution)/shard_map/all_to_all | solution.py:297
  184.0 34.4 %collective-permute-start.3 = (bf16[256,1024]{1,0:T(8,128)(2,1)S(1)}, bf16[256,1024]{1,0:T(8,128)(2,1)S(1)}, u32[]{:S(2)}, u32[]{:S(2)}) collective-permute-start(bf16[256,1024]{1,0:T(8,128)(2,1)S(1)} %get-tuple-element.53.a_ref), channel_id=1, source_target_pairs={{0,1},{1,0},{2,3},{3,2},{4,5},{5,4},{6,7},{7,6},{8,9},{9,8},{10,11... | collective-permute-start | bytes 1572872 | tf_op jit(solution)/shard_map/ppermute | solution.py:301
  207.4 1.3 copy-start.2
  211.6 28.7 %all-to-all-start.5 = ((bf16[8,4,224,128]{3,2,1,0:T(8,128)(2,1)}), bf16[8,4,224,128]{3,2,1,0:T(8,128)(2,1)S(1)}, u32[]{:S(2)}, u32[]{:S(2)}) async-start(bf16[8,4,224,128]{3,2,1,0:T(8,128)(2,1)} %shard_map.173), calls=%async_computation.5 | async-start | bytes 3670016 | tf_op jit(solution)/shard_map/all_to_all | solution.py:297
  226.2 5.3 %copy-start.6 = (bf16[256,1024]{1,0:T(8,128)(2,1)S(1)}, bf16[256,1024]{1,0:T(8,128)(2,1)}, u32[]{:S(2)}) copy-start(bf16[256,1024]{1,0:T(8,128)(2,1)} %copy-done.5) | copy-start | bytes 1572868
  228.2 20.2 %collective-permute-start.5 = (bf16[64,3584]{1,0:T(8,128)(2,1)}, bf16[64,3584]{1,0:T(8,128)(2,1)S(1)}, u32[]{:S(2)}, u32[]{:S(2)}) collective-permute-start(bf16[64,3584]{1,0:T(8,128)(2,1)} %get-tuple-element.52), channel_id=1, source_target_pairs={{0,2},{2,4},{4,6},{6,0},{1,3},{3,5},{5,7},{7,1},{8,10},{10,12},{12... | collective-permute-start | bytes 1376264 | tf_op jit(solution)/shard_map/ppermute | solution.py:365
  228.9 19.6 %collective-permute-start.6 = (bf16[64,3584]{1,0:T(8,128)(2,1)S(1)}, bf16[64,3584]{1,0:T(8,128)(2,1)S(1)}, u32[]{:S(2)}, u32[]{:S(2)}) collective-permute-start(bf16[64,3584]{1,0:T(8,128)(2,1)S(1)} %get-tuple-element.51), channel_id=1, source_target_pairs={{0,6},{2,0},{4,2},{6,4},{1,7},{3,1},{5,3},{7,5},{8,14},{10,8},{12,... | collective-permute-start | bytes 1376264 | tf_op jit(solution)/shard_map/ppermute | solution.py:366
  240.3 1.3 copy-start
  241.6 41.3 %all-to-all-start.6 = ((bf16[16,16,3584]{2,1,0:T(8,128)(2,1)}), bf16[16,16,3584]{2,1,0:T(8,128)(2,1)}, u32[]{:S(2)}, u32[]{:S(2)}) async-start(bf16[16,16,3584]{2,1,0:T(8,128)(2,1)} %bitcast.30), calls=%async_computation.6 | async-start | bytes 3670016 | tf_op jit(solution)/shard_map/all_to_all | solution.py:297
  253.7 21.6 %collective-permute-start.7 = (bf16[128,3584]{1,0:T(8,128)(2,1)}, bf16[128,3584]{1,0:T(8,128)(2,1)S(1)}, u32[]{:S(2)}, u32[]{:S(2)}) collective-permute-start(bf16[128,3584]{1,0:T(8,128)(2,1)} %get-tuple-element.42), channel_id=1, source_target_pairs={{0,2},{2,4},{4,6},{6,0},{1,3},{3,5},{5,7},{7,1},{8,10},{10,12},{12... | collective-permute-start | bytes 2752520 | tf_op jit(solution)/shard_map/ppermute | solution.py:368
  254.4 20.9 %collective-permute-start.8 = (bf16[128,3584]{1,0:T(8,128)(2,1)}, bf16[128,3584]{1,0:T(8,128)(2,1)S(1)}, u32[]{:S(2)}, u32[]{:S(2)}) collective-permute-start(bf16[128,3584]{1,0:T(8,128)(2,1)} %get-tuple-element.43), channel_id=1, source_target_pairs={{0,6},{2,0},{4,2},{6,4},{1,7},{3,1},{5,3},{7,5},{8,14},{10,8},{12,... | collective-permute-start | bytes 2752520 | tf_op jit(solution)/shard_map/ppermute | solution.py:369
  279.7 13.6 %collective-permute-start.9 = (bf16[64,3584]{1,0:T(8,128)(2,1)}, bf16[64,3584]{1,0:T(8,128)(2,1)S(1)}, u32[]{:S(2)}, u32[]{:S(2)}) collective-permute-start(bf16[64,3584]{1,0:T(8,128)(2,1)} %get-tuple-element.45), channel_id=1, source_target_pairs={{0,8},{8,0},{1,9},{9,1},{2,10},{10,2},{3,11},{11,3},{4,12},{12,4},... | collective-permute-start | bytes 1376264 | tf_op jit(solution)/shard_map/ppermute | solution.py:387
  281.9 17.3 %collective-permute-start.2 = (bf16[224,1024]{1,0:T(8,128)(2,1)S(1)}, bf16[224,1024]{1,0:T(8,128)(2,1)S(1)}, u32[]{:S(2)}, u32[]{:S(2)}) collective-permute-start(bf16[224,1024]{1,0:T(8,128)(2,1)S(1)} %constant_dynamic-slice_fusion), channel_id=1, source_target_pairs={{0,8},{8,0},{1,9},{9,1},{2,10},{10,2},{3,11},{11,3},{4,12},{12,4},... | collective-permute-start | bytes 1376264 | tf_op jit(solution)/shard_map/ppermute | solution.py:389
  (8 other events, 6.8 us)
Sparse Core Ops, SparseCore 0:
  66.5 45.0 all-gather.4
  114.0 45.1 all-gather.2
  176.4 42.6 reduce-scatter.1

commit v5 on v4

--- a/solution.py
+++ b/solution.py
@@ -198,6 +198,53 @@
     )(place, a, a_other, b, b_other)
 
 
+def flip_body(core_ref, own_ref, other_ref, out_ref):
+    rows = own_ref.shape[0]
+    out_ref[:, 0:rows] = own_ref[...].astype(F32).T.astype(BF)
+    out_ref[:, rows : 2 * rows] = other_ref[...].astype(F32).T.astype(BF)
+
+
+def flip(place, own, other, step=256):
+    rows, width = own.shape
+    steps = width // 2 // step
+    part = pl.BlockSpec((rows, step), lambda i, at: (0, at[0] * steps + i))
+    return pl.pallas_call(
+        flip_body,
+        grid_spec=pltpu.PrefetchScalarGridSpec(
+            num_scalar_prefetch=1,
+            grid=(steps,),
+            in_specs=[part, part],
+            out_specs=pl.BlockSpec((step, 2 * rows), lambda i, at: (i, 0)),
+        ),
+        out_shape=jax.ShapeDtypeStruct((width // 2, 2 * rows), BF),
+        name="flip",
+    )(place, own, other)
+
+
+def half_grad_body(at_ref, xt_ref, own_ref, other_ref, out_ref):
+    rows = own_ref.shape[0]
+    total = jnp.dot(xt_ref[:, 0:rows], own_ref[...], preferred_element_type=F32)
+    total += jnp.dot(xt_ref[:, rows : 2 * rows], other_ref[...], preferred_element_type=F32)
+    out_ref[...] = total.astype(BF)
+
+
+def half_grad(which, flipped, own, other):
+    width, deep = flipped.shape
+    rows, cols = own.shape
+    tall = width // (NX * NY)
+    right = pl.BlockSpec((rows, cols), lambda i, at: (0, 0))
+    return pl.pallas_call(
+        half_grad_body,
+        grid_spec=pltpu.PrefetchScalarGridSpec(
+            num_scalar_prefetch=1,
+            grid=(NY,),
+            in_specs=[pl.BlockSpec((tall, deep), lambda i, at: (i * NX + at[0], 0)), right, right],
+            out_specs=pl.BlockSpec((tall, cols), lambda i, at: (i, 0)),
+        ),
+        out_shape=jax.ShapeDtypeStruct((width // NX, cols), BF),
+    )(which, flipped, own, other)
+
+
 def relay_body(part_ref, below_ref, above_ref, up_ref, down_ref):
     tall = below_ref.shape[0]
     wide = 2 * tall
@@ -249,9 +296,7 @@
 
 
 def adam_up_body(x_ref, weight_ref, state_ref, grad_ref, other_ref, *outs):
-    rows = other_ref.shape[0]
-    own = grad_ref[pl.ds(pl.multiple_of(x_ref[0] * rows, 16), rows)]
-    both = own.astype(F32) + other_ref[...].astype(F32)
+    both = grad_ref[...].astype(F32) + other_ref[...].astype(F32)
     grad = lanes_taken(both, inverse(row_order()))
     for g in range(state_ref.shape[0]):
         lanes = slice(g * LANE, (g + 1) * LANE)
@@ -322,7 +367,6 @@
     core_at = lax.axis_index("core").astype(jnp.int32)
     y_at = lax.axis_index("y").astype(jnp.int32)
     x_at = lax.axis_index("x").astype(jnp.int32).reshape(1)
-    up_place = jnp.stack([core_at, jnp.zeros((), jnp.int32)])
     down_place = jnp.stack([core_at, y_at])
     up_shape, down_shape = up_weight.shape[1:], down_weight.shape[1:]
 
@@ -364,17 +408,23 @@
     falling = [(i, (i - 1) % NY) for i in range(NY)]
     below = lax.ppermute(down_part[4 * tall : 5 * tall], "y", rising)
     above = lax.ppermute(down_part[5 * tall : 6 * tall], "y", falling)
+    flipped = flip(down_place, inputs, inputs_other)
+    upstream, flipped, _ = lax.optimization_barrier((upstream, flipped, down_part))
+    back = lax.dot_general(upstream, down_mat, (((1,), (1,)), ((), ())), preferred_element_type=F32)
+    pre_grad = (back * slopes).astype(BF)
+    pre_grad_other = from_partner(pre_grad)
+    ordered = order_states(old_owner, new_owner, shares, 1)
+    ordered, pre_grad = lax.optimization_barrier((ordered, pre_grad))
+    states = exchange(ordered, "expert")
+    up_far = half_grad(1 - x_at, flipped, pre_grad, pre_grad_other)
+    up_far_sum = lax.psum_scatter(up_far, "y", scatter_dimension=0, tiled=True)
+    pre_grad, up_far = lax.optimization_barrier((pre_grad, up_far))
+    up_own = half_grad(x_at, flipped, pre_grad, pre_grad_other)
+    up_sum = lax.psum_scatter(up_own, "y", scatter_dimension=0, tiled=True)
+    pre_grad, down_part, up_own = lax.optimization_barrier((pre_grad, down_part, up_own))
     going_up, going_down = relay(down_part, below, above)
     below = lax.ppermute(going_up, "y", rising)
     above = lax.ppermute(going_down, "y", falling)
-    ordered = order_states(old_owner, new_owner, shares, 1)
-    states = exchange(ordered, "expert")
-    back = lax.dot_general(upstream, down_mat, (((1,), (1,)), ((), ())), preferred_element_type=F32)
-    pre_grad = (back * slopes).astype(BF)
-    pre_grad_other = from_partner(pre_grad)
-    up_part = weight_grad(up_place, inputs, inputs_other, pre_grad, pre_grad_other, 256)
-    up_sum = lax.psum_scatter(up_part, "y", scatter_dimension=0, tiled=True)
-    pre_grad, up_part = lax.optimization_barrier((pre_grad, up_part))
     input_grad = lax.dot_general(
         pre_grad, up_mat, (((1,), (1,)), ((), ())), preferred_element_type=F32
     ).astype(BF)
@@ -385,8 +435,7 @@
     swap = [(0, 1), (1, 0)]
     down_own, down_send = finish(x_at, down_part, below, above)
     down_other = lax.ppermute(down_send, "x", swap)
-    up_send = lax.dynamic_slice_in_dim(up_sum, (1 - x_at[0]) * up_shape[0], up_shape[0])
-    up_other = lax.ppermute(up_send, "x", swap)
+    up_other = lax.ppermute(up_far_sum, "x", swap)
     down_new = adam(adam_down_body, x_at, weights, states, 1, (down_own, down_other), down_shape)
     up_new = adam(adam_up_body, x_at, weights, states, 0, (up_sum, up_other), up_shape)
     return (

time: 312 us -> 301 us (0.965)
  waiting for transfers between devices: 98.6 us -> 80 us
  Pallas kernels: 51.6 us -> 59.2 us
    all_gather x1, waiting for transfers between devices: 27.3 us -> 0.78 us  [step(): down_mat = lax.all_gather(down_pair, ('core', 'y'), axis=0, tiled=True)]
    pallas_call x0 -> x3, Pallas kernels: none -> 15.7 us  [the longest x2 9.39 us: half_grad(): pl.pallas_call(half_grad_body, grid_spec=pltpu.PrefetchScalarGridSpec(num...]
    ppermute x1, waiting for transfers between devices: 18.4 us -> 33.5 us  [step(): below = lax.ppermute(going_up, 'y', rising)]
    all_to_all x4, waiting for transfers between devices: 42.3 us -> 32.9 us  [exchange(): return lax.all_to_all(array, axis, split_axis=0, concat_axis=0, tiled=True)]
    pallas_call x2 -> x1, Pallas kernels: 15.3 us -> 7.06 us  [weight_grad(): pl.pallas_call(weight_grad_body, grid_spec=pltpu.PrefetchScalarGridSpec(n...]
    ppermute x1, waiting for transfers between devices: 7.73 us -> 11.6 us  [step(): down_other = lax.ppermute(down_send, 'x', swap)]
    unnamed x31 -> x29, local copies, waits for them, and re-layouts: 9.17 us -> 9.65 us
  transfers between devices with their start and end apart: 17 -> 18, of which waited for: 8 -> 7; matrix products, arithmetic and copies ran while one was open for 8% -> 8% of each run, Pallas kernels for 10% -> 14%
where the time goes in v5:
time: 301 us; the launch traced here: 299 us
  waiting for transfers between devices  80 us (27%)
  blocking collectives  78.7 us (26%)
  Pallas kernels  59.2 us (20%)
  starting transfers between devices  35.8 us (12%)
  matrix products  19.2 us (6%)
  between operations  13.8 us (5%)
  local copies, waits for them, and re-layouts  11.7 us (4%)
    all_to_all x3, blocking collectives, exchange(): return lax.all_to_all(array, axis, split_axis=0, concat_axis=0, tiled=True)  78.7 us
    ppermute x1, waiting for transfers between devices, step(): below = lax.ppermute(going_up, 'y', rising)  33.5 us
    all_to_all x4, waiting for transfers between devices, exchange(): return lax.all_to_all(array, axis, split_axis=0, concat_axis=0, tiled=True)  32.9 us
    all_to_all x4, starting transfers between devices, exchange(): return lax.all_to_all(array, axis, split_axis=0, concat_axis=0, tiled=True)  26.4 us
    ppermute x1, waiting for transfers between devices, step(): down_other = lax.ppermute(down_send, 'x', swap)  11.6 us
    unnamed x29, local copies, waits for them, and re-layouts  9.65 us
    pallas_call x2, Pallas kernels, half_grad(): pl.pallas_call(half_grad_body, grid_spec=pltpu.PrefetchScalarGridSpec(num...  9.39 us
    pallas_call x2, Pallas kernels, adam(): pl.pallas_call(body, grid=(1,), in_specs=[smem(), pl.BlockSpec((weights.s...  8.28 us
  transfers between devices with their start and end apart: 18, of which 7 were waited for; matrix products, arithmetic and copies ran while one was open for 8% of the time, Pallas kernels for 14%

profile of v5, /device:TPU:4, one launch (start us, length us, event | category | flops | bytes accessed | tf_op | source)
XLA Modules:
  0.0 298.9 jit_solution(507084311425471659)
XLA Ops:
  9.7 21.5 %all_to_all.35.in_ref = bf16[8,2,224,128]{3,2,1,0:T(8,128)(2,1)} all-to-all(bf16[8,2,224,128]{3,2,1,0:T(8,128)(2,1)} %pack_weights.1), channel_id=1, replica_groups=mesh['expert'=8,'x'=2,'y'=4,'core'=2] {'expert'}, dimensions={0} | all-to-all | bytes 1835008 | tf_op jit(solution)/shard_map/all_to_all | solution.py:342
  33.8 29.5 %all_to_all.36.in_ref.weight_ref = bf16[16,2,224,128]{3,2,1,0:T(8,128)(2,1)} all-to-all(bf16[16,2,224,128]{3,2,1,0:T(8,128)(2,1)} %shard_map.171), channel_id=1, replica_groups=mesh['expert'=8,'x'=2,'y'=4,'core'=2] {'expert','x'}, dimensions={0} | all-to-all | bytes 3670016 | tf_op jit(solution)/shard_map/all_to_all | solution.py:342
  67.8 3.8 %dispatch.1 = (bf16[16,16,3584]{2,1,0:T(8,128)(2,1)}, bf16[16,16,3584]{2,1,0:T(8,128)(2,1)}) custom-call(s32[8,1]{1,0:T(8,128)} %copy.20.ids_ref, s32[8]{0:T(128)} %count_ref.1, s32[8]{0:T(128)} %own_ref.3, bf16[8,16,3584]{2,1,0:T(8,128)(2,1)} %bitcast.28, bf16[8,16,3584]{2,1,0:T(8,128)(2,1)} %bitcast.29), custom_call_target="tpu_custom_call" | custom-call | tf_op jit(solution)/shard_map/dispatch/pallas_call | solution.py:109
  71.7 27.7 %all_to_all.37 = bf16[16,16,3584]{2,1,0:T(8,128)(2,1)} all-to-all(bf16[16,16,3584]{2,1,0:T(8,128)(2,1)} %get-tuple-element.38), channel_id=1, replica_groups=mesh['expert'=8,'x'=2,'y'=4,'core'=2] {'expert'}, dimensions={0} | all-to-all | bytes 3670016 | tf_op jit(solution)/shard_map/all_to_all | solution.py:342
  99.3 6.9 %all-to-all-start.3 = ((bf16[16,16,3584]{2,1,0:T(8,128)(2,1)}), bf16[16,16,3584]{2,1,0:T(8,128)(2,1)}, u32[]{:S(2)}, u32[]{:S(2)}) async-start(bf16[16,16,3584]{2,1,0:T(8,128)(2,1)} %get-tuple-element.39), calls=%async_computation.3 | async-start | bytes 3670016 | tf_op jit(solution)/shard_map/all_to_all | solution.py:342
  106.2 20.2 %all-to-all-done.3 = bf16[16,16,3584]{2,1,0:T(8,128)(2,1)} async-done(((bf16[16,16,3584]{2,1,0:T(8,128)(2,1)}), bf16[16,16,3584]{2,1,0:T(8,128)(2,1)}, u32[]{:S(2)}, u32[]{:S(2)}) %all-to-all-start.3) | async-done | bytes 1835040 | tf_op jit(solution)/shard_map/all_to_all | solution.py:342
  126.4 6.7 %multiply_convert_fusion = (bf16[256,1024]{1,0:T(8,128)(2,1)S(1)}, f32[256,1024]{1,0:T(8,128)}) fusion(bf16[256,3584]{1,0:T(8,128)(2,1)} %bitcast.11.own_ref, bf16[3584,1024]{1,0:T(8,128)(2,1)} %all-gather.3.cloned.1.call-done), kind=kOutput, calls=%fused_computation.3 | convolution fusion | flops 1880358912 | bytes 10747904 | tf_op jit(solution)/shard_map/dot_general | solution.py:401
  133.6 3.7 %pack_states.1 = bf16[8,4,224,128]{3,2,1,0:T(8,128)(2,1)} custom-call(f32[224,1024]{1,0:T(8,128)} %bitcast.33, f32[224,1024]{1,0:T(8,128)} %bitcast.34, f32[64,3584]{1,0:T(8,128)} %bitcast.35, f32[64,3584]{1,0:T(8,128)} %bitcast.36), custom_call_target="tpu_custom_call" | custom-call | tf_op jit(solution)/shard_map/pack_states/pallas_call | solution.py:153
  137.3 6.3 %all-to-all-start.4 = ((bf16[8,4,224,128]{3,2,1,0:T(8,128)(2,1)}), bf16[8,4,224,128]{3,2,1,0:T(8,128)(2,1)S(1)}, u32[]{:S(2)}, u32[]{:S(2)}) async-start(bf16[8,4,224,128]{3,2,1,0:T(8,128)(2,1)} %pack_states.1), calls=%async_computation.4 | async-start | bytes 3670016 | tf_op jit(solution)/shard_map/all_to_all | solution.py:342
  144.2 6.3 %flip.1.xt_ref = bf16[1792,512]{1,0:T(8,128)(2,1)} custom-call(s32[2]{0:T(128)} %pad_add_fusion.core_ref.half_ref, bf16[256,3584]{1,0:T(8,128)(2,1)} %bitcast.11.own_ref, bf16[256,3584]{1,0:T(8,128)(2,1)} %collective-permute-done.other_ref), custom_call_target="tpu_custom_call" | custom-call | tf_op jit(solution)/shard_map/flip/pallas_call | solution.py:211
  151.3 7.1 %shard_map.173.part_ref = bf16[512,3584]{1,0:T(8,128)(2,1)} custom-call(s32[2]{0:T(128)} %pad_add_fusion.core_ref.half_ref, bf16[256,1024]{1,0:T(8,128)(2,1)} %copy-done.7, bf16[256,1024]{1,0:T(8,128)(2,1)} %copy-done.8, bf16[256,3584]{1,0:T(8,128)(2,1)} %bitcast.8.b_ref, bf16[256,3584]{1,0:T(8,128)(2,1)} %collective-permute-done.2.bo_ref), custom_call_target="tpu_custom_call" | custom-call | tf_op jit(solution)/shard_map/pallas_call | solution.py:189
  159.2 6.0 %fusion.own_ref = bf16[256,1024]{1,0:T(8,128)(2,1)S(1)} fusion(bf16[256,3584]{1,0:T(8,128)(2,1)} %bitcast.8.b_ref, bf16[1024,3584]{1,0:T(8,128)(2,1)} %all-gather.5.cloned.1.call-done, f32[256,1024]{1,0:T(8,128)} %get-tuple-element.66), kind=kOutput, calls=%fused_computation.2 | convolution fusion | flops 1881407488 | bytes 10747904 | tf_op jit(solution)/shard_map/dot_general | solution.py:413
  172.1 4.6 %shard_map.174 = bf16[896,1024]{1,0:T(8,128)(2,1)} custom-call(s32[1]{0:T(128)S(6)} %sub.7.at_ref, bf16[1792,512]{1,0:T(8,128)(2,1)} %flip.1.xt_ref, bf16[256,1024]{1,0:T(8,128)(2,1)} %copy-done.2, bf16[256,1024]{1,0:T(8,128)(2,1)} %copy-done.4), custom_call_target="tpu_custom_call" | custom-call | tf_op jit(solution)/shard_map/pallas_call | solution.py:236
  176.8 4.7 %shard_map.175 = bf16[896,1024]{1,0:T(8,128)(2,1)} custom-call(s32[1]{0:T(128)} %bitcast.12.at_ref.x_ref, bf16[1792,512]{1,0:T(8,128)(2,1)} %flip.1.xt_ref, bf16[256,1024]{1,0:T(8,128)(2,1)} %copy-done.2, bf16[256,1024]{1,0:T(8,128)(2,1)} %copy-done.4), custom_call_target="tpu_custom_call" | custom-call | tf_op jit(solution)/shard_map/pallas_call | solution.py:236
  181.6 6.2 %all-to-all-start.5 = ((bf16[8,4,224,128]{3,2,1,0:T(8,128)(2,1)}), bf16[8,4,224,128]{3,2,1,0:T(8,128)(2,1)S(1)}, u32[]{:S(2)}, u32[]{:S(2)}) async-start(bf16[8,4,224,128]{3,2,1,0:T(8,128)(2,1)} %shard_map.172), calls=%async_computation.5 | async-start | bytes 3670016 | tf_op jit(solution)/shard_map/all_to_all | solution.py:342
  193.1 6.5 %convolution_convert_fusion = bf16[256,3584]{1,0:T(8,128)(2,1)} fusion(bf16[256,1024]{1,0:T(8,128)(2,1)S(1)} %copy-done.3, bf16[3584,1024]{1,0:T(8,128)(2,1)} %all-gather.3.cloned.1.call-done), kind=kOutput, calls=%fused_computation | convolution fusion | flops 1879965696 | bytes 9699328 | tf_op jit(solution)/shard_map/dot_general | solution.py:428
  199.6 11.1 %all-to-all-done.5.state_ref = bf16[8,4,224,128]{3,2,1,0:T(8,128)(2,1)S(1)} async-done(((bf16[8,4,224,128]{3,2,1,0:T(8,128)(2,1)}), bf16[8,4,224,128]{3,2,1,0:T(8,128)(2,1)S(1)}, u32[]{:S(2)}, u32[]{:S(2)}) %all-to-all-start.5) | async-done | bytes 1835040 | tf_op jit(solution)/shard_map/all_to_all | solution.py:342
  212.0 6.9 %all-to-all-start.6 = ((bf16[16,16,3584]{2,1,0:T(8,128)(2,1)}), bf16[16,16,3584]{2,1,0:T(8,128)(2,1)}, u32[]{:S(2)}, u32[]{:S(2)}) async-start(bf16[16,16,3584]{2,1,0:T(8,128)(2,1)} %bitcast.27), calls=%async_computation.6 | async-start | bytes 3670016 | tf_op jit(solution)/shard_map/all_to_all | solution.py:342
  220.5 3.6 %relay.1 = (bf16[128,3584]{1,0:T(8,128)(2,1)}, bf16[128,3584]{1,0:T(8,128)(2,1)}) custom-call(bf16[512,3584]{1,0:T(8,128)(2,1)} %shard_map.173.part_ref, bf16[64,3584]{1,0:T(8,128)(2,1)} %copy-done.10, bf16[64,3584]{1,0:T(8,128)(2,1)} %copy-done.11), custom_call_target="tpu_custom_call" | custom-call | tf_op jit(solution)/shard_map/relay/pallas_call | solution.py:262
  227.4 33.5 %collective-permute-done.7.below_ref = bf16[128,3584]{1,0:T(8,128)(2,1)S(1)} collective-permute-done((bf16[128,3584]{1,0:T(8,128)(2,1)}, bf16[128,3584]{1,0:T(8,128)(2,1)S(1)}, u32[]{:S(2)}, u32[]{:S(2)}) %collective-permute-start.7) | collective-permute-done | bytes 917536 | tf_op jit(solution)/shard_map/ppermute | solution.py:426
  262.7 3.1 %finish.1 = (f32[64,3584]{1,0:T(8,128)}, bf16[64,3584]{1,0:T(8,128)(2,1)}) custom-call(s32[1]{0:T(128)} %bitcast.12.at_ref.x_ref, bf16[512,3584]{1,0:T(8,128)(2,1)} %shard_map.173.part_ref, bf16[128,3584]{1,0:T(8,128)(2,1)} %copy-done.5, bf16[128,3584]{1,0:T(8,128)(2,1)} %copy-done.6), custom_call_target="tpu_custom_call" | custom-call | tf_op jit(solution)/shard_map/finish/pallas_call | solution.py:278
  267.9 11.6 %collective-permute-done.9.other_ref = bf16[64,3584]{1,0:T(8,128)(2,1)S(1)} collective-permute-done((bf16[64,3584]{1,0:T(8,128)(2,1)}, bf16[64,3584]{1,0:T(8,128)(2,1)S(1)}, u32[]{:S(2)}, u32[]{:S(2)}) %collective-permute-start.9) | collective-permute-done | bytes 458784 | tf_op jit(solution)/shard_map/ppermute | solution.py:437
  280.2 4.1 %shard_map.177 = (f32[64,3584]{1,0:T(8,128)}, f32[64,3584]{1,0:T(8,128)}, f32[64,3584]{1,0:T(8,128)}) custom-call(s32[1]{0:T(128)} %bitcast.12.at_ref.x_ref, bf16[16,2,224,128]{3,2,1,0:T(8,128)(2,1)} %all_to_all.36.in_ref.weight_ref, bf16[8,4,224,128]{3,2,1,0:T(8,128)(2,1)} %copy-done, f32[64,3584]{1,0:T(8,128)} %get-tuple-element.56.grad_ref, ...), custom_call_target="tpu_custom_call" | custom-call | tf_op jit(solution)/shard_map/pallas_call | solution.py:322
  288.2 4.2 %shard_map.176 = (f32[224,1024]{1,0:T(8,128)}, f32[224,1024]{1,0:T(8,128)}, f32[224,1024]{1,0:T(8,128)}) custom-call(s32[1]{0:T(128)} %bitcast.12.at_ref.x_ref, bf16[16,2,224,128]{3,2,1,0:T(8,128)(2,1)} %all_to_all.36.in_ref.weight_ref, bf16[8,4,224,128]{3,2,1,0:T(8,128)(2,1)} %copy-done, bf16[224,1024]{1,0:T(8,128)(2,1)} %reduce-scatter.3.cloned.1.call-done.grad_ref, ...), custom_call_target="tpu_custom_call" | custom-call | tf_op jit(solution)/shard_map/pallas_call | solution.py:322
  (68 shorter events, 39.2 us)
Async XLA Ops:
  7.2 119.2 %all-gather.3.cloned.1.call-start = ((), (), s32[]{:S(2)}) async-start(), calls=%async_computation.9 | async-start | bytes 8257536 | tf_op jit(solution)/shard_map/all_gather | solution.py:378
  63.3 3.9 %copy-start.13 = (s32[8,1]{0,1:T(1,128)S(1)}, s32[8,1]{0,1:T(1,128)}, u32[]{:S(2)}) copy-start(s32[8,1]{0,1:T(1,128)} %param.14) | copy-start | bytes 100
  66.4 92.8 %all-gather.5.cloned.1.call-start = ((), (), s32[]{:S(2)}) async-start(), calls=%async_computation.10 | async-start | bytes 8257536 | tf_op jit(solution)/shard_map/all_gather | solution.py:379
  99.3 27.0 %all-to-all-start.3 = ((bf16[16,16,3584]{2,1,0:T(8,128)(2,1)}), bf16[16,16,3584]{2,1,0:T(8,128)(2,1)}, u32[]{:S(2)}, u32[]{:S(2)}) async-start(bf16[16,16,3584]{2,1,0:T(8,128)(2,1)} %get-tuple-element.39), calls=%async_computation.3 | async-start | bytes 3670016 | tf_op jit(solution)/shard_map/all_to_all | solution.py:342
  106.2 38.0 %collective-permute-start = (bf16[256,3584]{1,0:T(8,128)(2,1)}, bf16[256,3584]{1,0:T(8,128)(2,1)}, u32[]{:S(2)}, u32[]{:S(2)}) collective-permute-start(bf16[256,3584]{1,0:T(8,128)(2,1)} %bitcast.11.own_ref), channel_id=1, source_target_pairs={{0,1},{1,0},{2,3},{3,2},{4,5},{5,4},{6,7},{7,6},{8,9},{9,8},{10,11... | collective-permute-start | bytes 5505032 | tf_op jit(solution)/shard_map/ppermute | solution.py:346
  126.4 24.2 %collective-permute-start.2 = (bf16[256,3584]{1,0:T(8,128)(2,1)}, bf16[256,3584]{1,0:T(8,128)(2,1)}, u32[]{:S(2)}, u32[]{:S(2)}) collective-permute-start(bf16[256,3584]{1,0:T(8,128)(2,1)} %bitcast.8.b_ref), channel_id=1, source_target_pairs={{0,1},{1,0},{2,3},{3,2},{4,5},{5,4},{6,7},{7,6},{8,9},{9,8},{10,11... | collective-permute-start | bytes 5505032 | tf_op jit(solution)/shard_map/ppermute | solution.py:346
  133.1 4.2 %copy-start.7 = (bf16[256,1024]{1,0:T(8,128)(2,1)}, bf16[256,1024]{1,0:T(8,128)(2,1)S(1)}, u32[]{:S(2)}) copy-start(bf16[256,1024]{1,0:T(8,128)(2,1)S(1)} %get-tuple-element.65.a_ref) | copy-start | bytes 1572868
  133.1 17.5 %collective-permute-start.1 = (bf16[256,1024]{1,0:T(8,128)(2,1)S(1)}, bf16[256,1024]{1,0:T(8,128)(2,1)S(1)}, u32[]{:S(2)}, u32[]{:S(2)}) collective-permute-start(bf16[256,1024]{1,0:T(8,128)(2,1)S(1)} %get-tuple-element.65.a_ref), channel_id=1, source_target_pairs={{0,1},{1,0},{2,3},{3,2},{4,5},{5,4},{6,7},{7,6},{8,9},{9,8},{10,11... | collective-permute-start | bytes 1572872 | tf_op jit(solution)/shard_map/ppermute | solution.py:346
  137.3 29.8 %all-to-all-start.4 = ((bf16[8,4,224,128]{3,2,1,0:T(8,128)(2,1)}), bf16[8,4,224,128]{3,2,1,0:T(8,128)(2,1)S(1)}, u32[]{:S(2)}, u32[]{:S(2)}) async-start(bf16[8,4,224,128]{3,2,1,0:T(8,128)(2,1)} %pack_states.1), calls=%async_computation.4 | async-start | bytes 3670016 | tf_op jit(solution)/shard_map/all_to_all | solution.py:342
  143.6 123.4 %reduce-scatter.5.cloned.1.call-start = ((), (), s32[]{:S(2)}) async-start(), calls=%async_computation.12 | async-start | bytes 2293760 | tf_op jit(solution)/shard_map/reduce_scatter | solution.py:420
  165.2 6.1 %copy-start.2 = (bf16[256,1024]{1,0:T(8,128)(2,1)}, bf16[256,1024]{1,0:T(8,128)(2,1)S(1)}, u32[]{:S(2)}) copy-start(bf16[256,1024]{1,0:T(8,128)(2,1)S(1)} %fusion.own_ref) | copy-start | bytes 1572868
  165.2 6.1 %collective-permute-start.3 = (bf16[256,1024]{1,0:T(8,128)(2,1)S(1)}, bf16[256,1024]{1,0:T(8,128)(2,1)S(1)}, u32[]{:S(2)}, u32[]{:S(2)}) collective-permute-start(bf16[256,1024]{1,0:T(8,128)(2,1)S(1)} %fusion.own_ref), channel_id=1, source_target_pairs={{0,1},{1,0},{2,3},{3,2},{4,5},{5,4},{6,7},{7,6},{8,9},{9,8},{10,11... | collective-permute-start | bytes 1572872 | tf_op jit(solution)/shard_map/ppermute | solution.py:346
  167.1 1.2 copy-start.1
  176.8 110.2 %reduce-scatter.3.cloned.1.call-start = ((), (), s32[]{:S(2)}) async-start(), calls=%async_computation.11 | async-start | bytes 2293760 | tf_op jit(solution)/shard_map/reduce_scatter | solution.py:423
  181.6 29.2 %all-to-all-start.5 = ((bf16[8,4,224,128]{3,2,1,0:T(8,128)(2,1)}), bf16[8,4,224,128]{3,2,1,0:T(8,128)(2,1)S(1)}, u32[]{:S(2)}, u32[]{:S(2)}) async-start(bf16[8,4,224,128]{3,2,1,0:T(8,128)(2,1)} %shard_map.172), calls=%async_computation.5 | async-start | bytes 3670016 | tf_op jit(solution)/shard_map/all_to_all | solution.py:342
  187.8 5.3 %copy-start.3 = (bf16[256,1024]{1,0:T(8,128)(2,1)S(1)}, bf16[256,1024]{1,0:T(8,128)(2,1)}, u32[]{:S(2)}) copy-start(bf16[256,1024]{1,0:T(8,128)(2,1)} %copy-done.2) | copy-start | bytes 1572868
  189.9 29.1 %collective-permute-start.5 = (bf16[64,3584]{1,0:T(8,128)(2,1)}, bf16[64,3584]{1,0:T(8,128)(2,1)S(1)}, u32[]{:S(2)}, u32[]{:S(2)}) collective-permute-start(bf16[64,3584]{1,0:T(8,128)(2,1)} %get-tuple-element.64), channel_id=1, source_target_pairs={{0,2},{2,4},{4,6},{6,0},{1,3},{3,5},{5,7},{7,1},{8,10},{10,12},{12... | collective-permute-start | bytes 1376264 | tf_op jit(solution)/shard_map/ppermute | solution.py:409
  191.5 27.5 %collective-permute-start.6 = (bf16[64,3584]{1,0:T(8,128)(2,1)S(1)}, bf16[64,3584]{1,0:T(8,128)(2,1)S(1)}, u32[]{:S(2)}, u32[]{:S(2)}) collective-permute-start(bf16[64,3584]{1,0:T(8,128)(2,1)S(1)} %get-tuple-element.63), channel_id=1, source_target_pairs={{0,6},{2,0},{4,2},{6,4},{1,7},{3,1},{5,3},{7,5},{8,14},{10,8},{12,... | collective-permute-start | bytes 1376264 | tf_op jit(solution)/shard_map/ppermute | solution.py:410
  210.8 1.3 copy-start
  212.0 72.3 %all-to-all-start.6 = ((bf16[16,16,3584]{2,1,0:T(8,128)(2,1)}), bf16[16,16,3584]{2,1,0:T(8,128)(2,1)}, u32[]{:S(2)}, u32[]{:S(2)}) async-start(bf16[16,16,3584]{2,1,0:T(8,128)(2,1)} %bitcast.27), calls=%async_computation.6 | async-start | bytes 3670016 | tf_op jit(solution)/shard_map/all_to_all | solution.py:342
  224.1 36.7 %collective-permute-start.7 = (bf16[128,3584]{1,0:T(8,128)(2,1)}, bf16[128,3584]{1,0:T(8,128)(2,1)S(1)}, u32[]{:S(2)}, u32[]{:S(2)}) collective-permute-start(bf16[128,3584]{1,0:T(8,128)(2,1)} %get-tuple-element.54), channel_id=1, source_target_pairs={{0,2},{2,4},{4,6},{6,0},{1,3},{3,5},{5,7},{7,1},{8,10},{10,12},{12... | collective-permute-start | bytes 2752520 | tf_op jit(solution)/shard_map/ppermute | solution.py:426
  225.5 35.3 %collective-permute-start.8 = (bf16[128,3584]{1,0:T(8,128)(2,1)}, bf16[128,3584]{1,0:T(8,128)(2,1)S(1)}, u32[]{:S(2)}, u32[]{:S(2)}) collective-permute-start(bf16[128,3584]{1,0:T(8,128)(2,1)} %get-tuple-element.55), channel_id=1, source_target_pairs={{0,6},{2,0},{4,2},{6,4},{1,7},{3,1},{5,3},{7,5},{8,14},{10,8},{12,... | collective-permute-start | bytes 2752520 | tf_op jit(solution)/shard_map/ppermute | solution.py:427
  265.8 13.6 %collective-permute-start.9 = (bf16[64,3584]{1,0:T(8,128)(2,1)}, bf16[64,3584]{1,0:T(8,128)(2,1)S(1)}, u32[]{:S(2)}, u32[]{:S(2)}) collective-permute-start(bf16[64,3584]{1,0:T(8,128)(2,1)} %get-tuple-element.57), channel_id=1, source_target_pairs={{0,8},{8,0},{1,9},{9,1},{2,10},{10,2},{3,11},{11,3},{4,12},{12,4},... | collective-permute-start | bytes 1376264 | tf_op jit(solution)/shard_map/ppermute | solution.py:437
  267.0 20.4 %collective-permute-start.4 = (bf16[224,1024]{1,0:T(8,128)(2,1)}, bf16[224,1024]{1,0:T(8,128)(2,1)S(1)}, u32[]{:S(2)}, u32[]{:S(2)}) collective-permute-start(bf16[224,1024]{1,0:T(8,128)(2,1)} %reduce-scatter.5.cloned.1.call-done), channel_id=1, source_target_pairs={{0,8},{8,0},{1,9},{9,1},{2,10},{10,2},{3,11},{11,3},{4,12},{12,4},... | collective-permute-start | bytes 1376264 | tf_op jit(solution)/shard_map/ppermute | solution.py:438
  (8 other events, 6.5 us)
Sparse Core Ops, SparseCore 0:
  66.5 44.7 all-gather.2
  113.6 45.5 all-gather.4
  176.9 36.6 reduce-scatter.4
  215.8 40.5 reduce-scatter.2

commit v6 on v5

--- a/solution.py
+++ b/solution.py
@@ -221,28 +221,53 @@
     )(place, own, other)
 
 
-def half_grad_body(at_ref, xt_ref, own_ref, other_ref, out_ref):
+def up_grad_body(xt_ref, own_ref, other_ref, out_ref):
     rows = own_ref.shape[0]
     total = jnp.dot(xt_ref[:, 0:rows], own_ref[...], preferred_element_type=F32)
     total += jnp.dot(xt_ref[:, rows : 2 * rows], other_ref[...], preferred_element_type=F32)
     out_ref[...] = total.astype(BF)
 
 
-def half_grad(which, flipped, own, other):
+def up_grad_part(flipped, own, other, steps=4):
     width, deep = flipped.shape
     rows, cols = own.shape
-    tall = width // (NX * NY)
-    right = pl.BlockSpec((rows, cols), lambda i, at: (0, 0))
-    return pl.pallas_call(
-        half_grad_body,
-        grid_spec=pltpu.PrefetchScalarGridSpec(
-            num_scalar_prefetch=1,
-            grid=(NY,),
-            in_specs=[pl.BlockSpec((tall, deep), lambda i, at: (i * NX + at[0], 0)), right, right],
-            out_specs=pl.BlockSpec((tall, cols), lambda i, at: (i, 0)),
-        ),
-        out_shape=jax.ShapeDtypeStruct((width // NX, cols), BF),
-    )(which, flipped, own, other)
+    right = pl.BlockSpec((rows, cols), lambda i: (0, 0))
+    return pl.pallas_call(
+        up_grad_body,
+        grid=(steps,),
+        in_specs=[pl.BlockSpec((width // steps, deep), lambda i: (i, 0)), right, right],
+        out_specs=pl.BlockSpec((width // steps, cols), lambda i: (i, 0)),
+        out_shape=jax.ShapeDtypeStruct((width, cols), BF),
+        name="up_part",
+    )(flipped, own, other)
+
+
+def back_body(at_ref, dy_ref, slopes_ref, *refs):
+    pieces, out_ref = refs[:-1], refs[-1]
+    dims = (((1,), (1,)), ((), ()))
+    per_core = len(pieces) // NC
+    dy = dy_ref[...]
+    for k in range(NC):
+        own, above, low, high, below = (p[...] for p in pieces[k * per_core : (k + 1) * per_core])
+        core = at_ref[0] if k == 0 else 1 - at_ref[0]
+        for first, group in ((0, [own, above]), (2, [low, high, below])):
+            both = lax.dot_general(
+                dy, jnp.concatenate(group, axis=0), dims, preferred_element_type=F32
+            )
+            for i in range(2):
+                tile = core * NY + lax.rem(at_ref[1] + first + i, NY)
+                lanes = pl.ds(pl.multiple_of(tile * LANE, LANE), LANE)
+                value = both[:, i * LANE : (i + 1) * LANE] * slopes_ref[:, lanes]
+                out_ref[:, lanes] = value.astype(BF)
+
+
+def back_grad(place, dy, slopes, pieces):
+    return pl.pallas_call(
+        back_body,
+        in_specs=[smem(), vmem(), vmem()] + [vmem()] * len(pieces),
+        out_shape=jax.ShapeDtypeStruct(slopes.shape, BF),
+        name="back",
+    )(place, dy, slopes, *pieces)
 
 
 def relay_body(part_ref, below_ref, above_ref, up_ref, down_ref):
@@ -296,7 +321,9 @@
 
 
 def adam_up_body(x_ref, weight_ref, state_ref, grad_ref, other_ref, *outs):
-    both = grad_ref[...].astype(F32) + other_ref[...].astype(F32)
+    rows = other_ref.shape[0]
+    own = grad_ref[pl.ds(pl.multiple_of(x_ref[0] * rows, 16), rows)]
+    both = own.astype(F32) + other_ref[...].astype(F32)
     grad = lanes_taken(both, inverse(row_order()))
     for g in range(state_ref.shape[0]):
         lanes = slice(g * LANE, (g + 1) * LANE)
@@ -376,7 +403,15 @@
     weights = exchange(ordered, ("expert", "x"))
     up_pair, down_pair = unpack_weights(weights, up_shape, down_shape)
     up_mat = lax.all_gather(up_pair, ("core", "y"), axis=0, tiled=True)
-    down_mat = lax.all_gather(down_pair, ("core", "y"), axis=0, tiled=True)
+    rising = [(i, (i + 1) % NY) for i in range(NY)]
+    falling = [(i, (i - 1) % NY) for i in range(NY)]
+    tall = down_shape[0]
+    w_below = lax.ppermute(down_pair, "y", rising)
+    w_above = lax.ppermute(down_pair, "y", falling)
+    w_low = lax.ppermute(w_below[:tall], "y", rising)
+    w_high = lax.ppermute(w_above[tall:], "y", falling)
+    pieces = (down_pair, w_above, w_low, w_high, w_below)
+    pieces += tuple(from_partner(piece) for piece in pieces)
 
     send_x, send_dy = dispatch(
         block_expert,
@@ -392,10 +427,12 @@
     upstream = exchange(send_dy, "expert").reshape(-1, features)
     inputs_other, upstream_other = from_partner(inputs), from_partner(upstream)
 
+    flipped = flip(down_place, inputs, inputs_other)
+
     packed = pack_states(
         (up_first[0], up_second[0]), (down_first[0], down_second[0]), groups
     )
-    packed, upstream = lax.optimization_barrier((packed, upstream))
+    packed, upstream, flipped = lax.optimization_barrier((packed, upstream, flipped))
     shares = exchange(packed, "expert")
 
     pre_act = jnp.dot(inputs, up_mat, preferred_element_type=F32)
@@ -403,25 +440,18 @@
     hidden = active.astype(BF)
     hidden_other = from_partner(hidden)
     down_part = weight_grad(down_place, hidden, hidden_other, upstream, upstream_other, 128)
-    tall = down_shape[0]
-    rising = [(i, (i + 1) % NY) for i in range(NY)]
-    falling = [(i, (i - 1) % NY) for i in range(NY)]
     below = lax.ppermute(down_part[4 * tall : 5 * tall], "y", rising)
     above = lax.ppermute(down_part[5 * tall : 6 * tall], "y", falling)
-    flipped = flip(down_place, inputs, inputs_other)
-    upstream, flipped, _ = lax.optimization_barrier((upstream, flipped, down_part))
-    back = lax.dot_general(upstream, down_mat, (((1,), (1,)), ((), ())), preferred_element_type=F32)
-    pre_grad = (back * slopes).astype(BF)
+    slopes, _ = lax.optimization_barrier((slopes, down_part))
+    pre_grad = back_grad(down_place, upstream, slopes, pieces)
     pre_grad_other = from_partner(pre_grad)
+    up_part = up_grad_part(flipped, pre_grad, pre_grad_other)
+    up_sum = lax.psum_scatter(up_part, "y", scatter_dimension=0, tiled=True)
     ordered = order_states(old_owner, new_owner, shares, 1)
-    ordered, pre_grad = lax.optimization_barrier((ordered, pre_grad))
+    ordered, up_part, pre_grad, down_part = lax.optimization_barrier(
+        (ordered, up_part, pre_grad, down_part)
+    )
     states = exchange(ordered, "expert")
-    up_far = half_grad(1 - x_at, flipped, pre_grad, pre_grad_other)
-    up_far_sum = lax.psum_scatter(up_far, "y", scatter_dimension=0, tiled=True)
-    pre_grad, up_far = lax.optimization_barrier((pre_grad, up_far))
-    up_own = half_grad(x_at, flipped, pre_grad, pre_grad_other)
-    up_sum = lax.psum_scatter(up_own, "y", scatter_dimension=0, tiled=True)
-    pre_grad, down_part, up_own = lax.optimization_barrier((pre_grad, down_part, up_own))
     going_up, going_down = relay(down_part, below, above)
     below = lax.ppermute(going_up, "y", rising)
     above = lax.ppermute(going_down, "y", falling)
@@ -435,7 +465,8 @@
     swap = [(0, 1), (1, 0)]
     down_own, down_send = finish(x_at, down_part, below, above)
     down_other = lax.ppermute(down_send, "x", swap)
-    up_other = lax.ppermute(up_far_sum, "x", swap)
+    up_send = lax.dynamic_slice_in_dim(up_sum, (1 - x_at[0]) * up_shape[0], up_shape[0])
+    up_other = lax.ppermute(up_send, "x", swap)
     down_new = adam(adam_down_body, x_at, weights, states, 1, (down_own, down_other), down_shape)
     up_new = adam(adam_up_body, x_at, weights, states, 0, (up_sum, up_other), up_shape)
     return (

time: 301 us -> 318 us (1.056)
  blocking collectives: 78.7 us -> 109 us
  waiting for transfers between devices: 80 us -> 64.9 us
  matrix products: 19.2 us -> 13.4 us
  local copies, waits for them, and re-layouts: 11.7 us -> 15.9 us
    all_to_all x3 -> x4, blocking collectives: 78.7 us -> 109 us  [exchange(): return lax.all_to_all(array, axis, split_axis=0, concat_axis=0, tiled=True)]
    ppermute x1, waiting for transfers between devices: 33.5 us -> 18.6 us  [step(): below = lax.ppermute(going_up, 'y', rising)]
    all_to_all x4 -> x3, starting transfers between devices: 26.4 us -> 19.2 us  [exchange(): return lax.all_to_all(array, axis, split_axis=0, concat_axis=0, tiled=True)]
    ppermute x1 -> x5, waiting for transfers between devices: 0.44 us -> 7.23 us  [the longest x1 4.4 us: step(): w_below = lax.ppermute(down_pair, 'y', rising)]
    ppermute x1 -> x5, starting transfers between devices: 0.81 us -> 7.49 us  [the longest x1 3.12 us: step(): w_high = lax.ppermute(w_above[tall:], 'y', falling)]
    all_to_all x4 -> x3, waiting for transfers between devices: 32.9 us -> 26.5 us  [exchange(): return lax.all_to_all(array, axis, split_axis=0, concat_axis=0, tiled=True)]
    dot_general x1 -> x0, matrix products: 5.99 us -> none  [step(): lax.dot_general(upstream, down_mat, (((1,), (1,)), ((), ())), preferred_e...]
    unnamed x29 -> x35, local copies, waits for them, and re-layouts: 9.65 us -> 10.2 us
  transfers between devices with their start and end apart: 18 -> 24, of which waited for: 7 -> 8; matrix products, arithmetic and copies ran while one was open for 8% -> 6% of each run, Pallas kernels for 14% -> 12%
where the time goes in v6:
time: 318 us; the launch traced here: 317 us
  blocking collectives  109 us (34%)
  waiting for transfers between devices  64.9 us (20%)
  Pallas kernels  62.1 us (20%)
  starting transfers between devices  36.5 us (11%)
  local copies, waits for them, and re-layouts  15.9 us (5%)
  between operations  14.2 us (4%)
  matrix products  13.4 us (4%)
    all_to_all x4, blocking collectives, exchange(): return lax.all_to_all(array, axis, split_axis=0, concat_axis=0, tiled=True)  109 us
    all_to_all x3, waiting for transfers between devices, exchange(): return lax.all_to_all(array, axis, split_axis=0, concat_axis=0, tiled=True)  26.5 us
    all_to_all x3, starting transfers between devices, exchange(): return lax.all_to_all(array, axis, split_axis=0, concat_axis=0, tiled=True)  19.2 us
    ppermute x1, waiting for transfers between devices, step(): below = lax.ppermute(going_up, 'y', rising)  18.6 us
    ppermute x1, waiting for transfers between devices, step(): down_other = lax.ppermute(down_send, 'x', swap)  10.4 us
    unnamed x35, local copies, waits for them, and re-layouts  10.2 us
    pallas_call x2, Pallas kernels, adam(): pl.pallas_call(body, grid=(1,), in_specs=[smem(), pl.BlockSpec((weights.s...  8.41 us
    pallas_call x1, Pallas kernels, weight_grad(): pl.pallas_call(weight_grad_body, grid_spec=pltpu.PrefetchScalarGridSpec(n...  7.06 us
  transfers between devices with their start and end apart: 24, of which 8 were waited for; matrix products, arithmetic and copies ran while one was open for 6% of the time, Pallas kernels for 12%

profile of v6, /device:TPU:4, one launch (start us, length us, event | category | flops | bytes accessed | tf_op | source)
XLA Modules:
  0.0 317.0 jit_solution(15998259030150810314)
XLA Ops:
  9.7 21.5 %all_to_all.35.in_ref = bf16[8,2,224,128]{3,2,1,0:T(8,128)(2,1)} all-to-all(bf16[8,2,224,128]{3,2,1,0:T(8,128)(2,1)} %pack_weights.1), channel_id=1, replica_groups=mesh['expert'=8,'x'=2,'y'=4,'core'=2] {'expert'}, dimensions={0} | all-to-all | bytes 1835008 | tf_op jit(solution)/shard_map/all_to_all | solution.py:369
  33.7 29.5 %all_to_all.36.in_ref.weight_ref = bf16[16,2,224,128]{3,2,1,0:T(8,128)(2,1)} all-to-all(bf16[16,2,224,128]{3,2,1,0:T(8,128)(2,1)} %shard_map.171), channel_id=1, replica_groups=mesh['expert'=8,'x'=2,'y'=4,'core'=2] {'expert','x'}, dimensions={0} | all-to-all | bytes 3670016 | tf_op jit(solution)/shard_map/all_to_all | solution.py:369
  67.0 3.9 %dispatch.1 = (bf16[16,16,3584]{2,1,0:T(8,128)(2,1)}, bf16[16,16,3584]{2,1,0:T(8,128)(2,1)}) custom-call(s32[8,1]{1,0:T(8,128)} %copy.20.ids_ref, s32[8]{0:T(128)} %count_ref.1, s32[8]{0:T(128)} %own_ref.3, bf16[8,16,3584]{2,1,0:T(8,128)(2,1)} %bitcast.32, bf16[8,16,3584]{2,1,0:T(8,128)(2,1)} %bitcast.33), custom_call_target="tpu_custom_call" | custom-call | tf_op jit(solution)/shard_map/dispatch/pallas_call | solution.py:109
  70.9 27.7 %all_to_all.37 = bf16[16,16,3584]{2,1,0:T(8,128)(2,1)} all-to-all(bf16[16,16,3584]{2,1,0:T(8,128)(2,1)} %get-tuple-element.36), channel_id=1, replica_groups=mesh['expert'=8,'x'=2,'y'=4,'core'=2] {'expert'}, dimensions={0} | all-to-all | bytes 3670016 | tf_op jit(solution)/shard_map/all_to_all | solution.py:369
  98.6 6.2 %all-to-all-start.3 = ((bf16[16,16,3584]{2,1,0:T(8,128)(2,1)}), bf16[16,16,3584]{2,1,0:T(8,128)(2,1)S(1)}, u32[]{:S(2)}, u32[]{:S(2)}) async-start(bf16[16,16,3584]{2,1,0:T(8,128)(2,1)} %get-tuple-element.37), calls=%async_computation.3 | async-start | bytes 3670016 | tf_op jit(solution)/shard_map/all_to_all | solution.py:369
  108.1 16.7 %all-to-all-done.3 = bf16[16,16,3584]{2,1,0:T(8,128)(2,1)S(1)} async-done(((bf16[16,16,3584]{2,1,0:T(8,128)(2,1)}), bf16[16,16,3584]{2,1,0:T(8,128)(2,1)S(1)}, u32[]{:S(2)}, u32[]{:S(2)}) %all-to-all-start.3) | async-done | bytes 1835040 | tf_op jit(solution)/shard_map/all_to_all | solution.py:369
  124.8 4.4 %collective-permute-done.4.refs_4_ = bf16[128,3584]{1,0:T(8,128)(2,1)S(1)} collective-permute-done((bf16[128,3584]{1,0:T(8,128)(2,1)}, bf16[128,3584]{1,0:T(8,128)(2,1)S(1)}, u32[]{:S(2)}, u32[]{:S(2)}) %collective-permute-start.4) | collective-permute-done | bytes 917536 | tf_op jit(solution)/shard_map/ppermute | solution.py:409
  135.1 7.0 %multiply_convert_fusion = (bf16[256,1024]{1,0:T(8,128)(2,1)S(1)}, f32[256,1024]{1,0:T(8,128)}) fusion(bf16[256,3584]{1,0:T(8,128)(2,1)} %bitcast.29, bf16[3584,1024]{1,0:T(8,128)(2,1)} %all-gather.2.cloned.1.call-done), kind=kOutput, calls=%fused_computation.1 | convolution fusion | flops 1881407488 | bytes 10747904 | tf_op jit(solution)/shard_map/dot_general | solution.py:438
  146.8 3.5 %pack_states.1 = bf16[8,4,224,128]{3,2,1,0:T(8,128)(2,1)} custom-call(f32[224,1024]{1,0:T(8,128)} %bitcast.37, f32[224,1024]{1,0:T(8,128)} %bitcast.38, f32[64,3584]{1,0:T(8,128)} %bitcast.39, f32[64,3584]{1,0:T(8,128)} %bitcast.40), custom_call_target="tpu_custom_call" | custom-call | tf_op jit(solution)/shard_map/pack_states/pallas_call | solution.py:153
  150.9 6.3 %flip.1.xt_ref = bf16[1792,512]{1,0:T(8,128)(2,1)} custom-call(s32[2]{0:T(128)} %pad_add_fusion.core_ref.half_ref.at_ref, bf16[256,3584]{1,0:T(8,128)(2,1)} %bitcast.30, bf16[256,3584]{1,0:T(8,128)(2,1)} %collective-permute-done.other_ref), custom_call_target="tpu_custom_call" | custom-call | tf_op jit(solution)/shard_map/flip/pallas_call | solution.py:211
  157.2 7.1 %shard_map.173.part_ref = bf16[512,3584]{1,0:T(8,128)(2,1)} custom-call(s32[2]{0:T(128)} %pad_add_fusion.core_ref.half_ref.at_ref, bf16[256,1024]{1,0:T(8,128)(2,1)} %copy-done.7, bf16[256,1024]{1,0:T(8,128)(2,1)} %copy-done.8, bf16[256,3584]{1,0:T(8,128)(2,1)} %bitcast.26, bf16[256,3584]{1,0:T(8,128)(2,1)} %collective-permute-done.2.bo_ref), custom_call_target="tpu_custom_call" | custom-call | tf_op jit(solution)/shard_map/pallas_call | solution.py:189
  165.2 6.9 %back.1.own_ref = bf16[256,1024]{1,0:T(8,128)(2,1)} custom-call(s32[2]{0:T(128)} %pad_add_fusion.core_ref.half_ref.at_ref, bf16[256,3584]{1,0:T(8,128)(2,1)} %bitcast.27, f32[256,1024]{1,0:T(8,128)} %get-tuple-element.43.slopes_ref, bf16[128,3584]{1,0:T(8,128)(2,1)} %get-tuple-element.35.refs_0_, bf16[128,3584]{1,0:T(8,128)(2,1)} %collective-permute-done.3.refs_1_, ...), custom_call_target="tpu_custom_call" | custom-call | tf_op jit(solution)/shard_map/back/pallas_call | solution.py:265
  175.0 5.6 %up_part.1 = bf16[1792,1024]{1,0:T(8,128)(2,1)} custom-call(bf16[1792,512]{1,0:T(8,128)(2,1)} %flip.1.xt_ref, bf16[256,1024]{1,0:T(8,128)(2,1)} %back.1.own_ref, bf16[256,1024]{1,0:T(8,128)(2,1)} %copy-done.9), custom_call_target="tpu_custom_call" | custom-call | tf_op jit(solution)/shard_map/up_part/pallas_call | solution.py:235
  182.1 30.6 %all_to_all.38.in_ref = bf16[8,4,224,128]{3,2,1,0:T(8,128)(2,1)} all-to-all(bf16[8,4,224,128]{3,2,1,0:T(8,128)(2,1)S(1)} %copy-done.2), channel_id=1, replica_groups=mesh['expert'=8,'x'=2,'y'=4,'core'=2] {'expert'}, dimensions={0} | all-to-all | bytes 3670016 | tf_op jit(solution)/shard_map/all_to_all | solution.py:369
  215.7 6.1 %all-to-all-start.5 = ((bf16[8,4,224,128]{3,2,1,0:T(8,128)(2,1)}), bf16[8,4,224,128]{3,2,1,0:T(8,128)(2,1)S(1)}, u32[]{:S(2)}, u32[]{:S(2)}) async-start(bf16[8,4,224,128]{3,2,1,0:T(8,128)(2,1)} %shard_map.172), calls=%async_computation.5 | async-start | bytes 3670016 | tf_op jit(solution)/shard_map/all_to_all | solution.py:369
  224.4 3.2 %collective-permute-start.15 = (bf16[64,3584]{1,0:T(8,128)(2,1)S(1)}, bf16[64,3584]{1,0:T(8,128)(2,1)S(1)}, u32[]{:S(2)}, u32[]{:S(2)}) collective-permute-start(bf16[64,3584]{1,0:T(8,128)(2,1)S(1)} %get-tuple-element.59), channel_id=1, source_target_pairs={{0,6},{2,0},{4,2},{6,4},{1,7},{3,1},{5,3},{7,5},{8,14},{10,8},{12,... | collective-permute-start | bytes 1376264 | tf_op jit(solution)/shard_map/ppermute | solution.py:444
  227.6 6.5 %convolution_convert_fusion = bf16[256,3584]{1,0:T(8,128)(2,1)} fusion(bf16[256,1024]{1,0:T(8,128)(2,1)S(1)} %copy-done.3, bf16[3584,1024]{1,0:T(8,128)(2,1)} %all-gather.2.cloned.1.call-done), kind=kOutput, calls=%fused_computation | convolution fusion | flops 1879965696 | bytes 9699328 | tf_op jit(solution)/shard_map/dot_general | solution.py:458
  234.1 9.8 %all-to-all-done.5.state_ref = bf16[8,4,224,128]{3,2,1,0:T(8,128)(2,1)S(1)} async-done(((bf16[8,4,224,128]{3,2,1,0:T(8,128)(2,1)}), bf16[8,4,224,128]{3,2,1,0:T(8,128)(2,1)S(1)}, u32[]{:S(2)}, u32[]{:S(2)}) %all-to-all-start.5) | async-done | bytes 1835040 | tf_op jit(solution)/shard_map/all_to_all | solution.py:369
  245.1 6.9 %all-to-all-start.6 = ((bf16[16,16,3584]{2,1,0:T(8,128)(2,1)}), bf16[16,16,3584]{2,1,0:T(8,128)(2,1)}, u32[]{:S(2)}, u32[]{:S(2)}) async-start(bf16[16,16,3584]{2,1,0:T(8,128)(2,1)} %bitcast.31), calls=%async_computation.6 | async-start | bytes 3670016 | tf_op jit(solution)/shard_map/all_to_all | solution.py:369
  253.6 3.6 %relay.1 = (bf16[128,3584]{1,0:T(8,128)(2,1)}, bf16[128,3584]{1,0:T(8,128)(2,1)}) custom-call(bf16[512,3584]{1,0:T(8,128)(2,1)} %shard_map.173.part_ref, bf16[64,3584]{1,0:T(8,128)(2,1)} %copy-done.10, bf16[64,3584]{1,0:T(8,128)(2,1)} %copy-done.11), custom_call_target="tpu_custom_call" | custom-call | tf_op jit(solution)/shard_map/relay/pallas_call | solution.py:287
  260.9 18.6 %collective-permute-done.16.below_ref = bf16[128,3584]{1,0:T(8,128)(2,1)S(1)} collective-permute-done((bf16[128,3584]{1,0:T(8,128)(2,1)}, bf16[128,3584]{1,0:T(8,128)(2,1)S(1)}, u32[]{:S(2)}, u32[]{:S(2)}) %collective-permute-start.16) | collective-permute-done | bytes 917536 | tf_op jit(solution)/shard_map/ppermute | solution.py:456
  287.1 10.4 %collective-permute-done.18.other_ref = bf16[64,3584]{1,0:T(8,128)(2,1)S(1)} collective-permute-done((bf16[64,3584]{1,0:T(8,128)(2,1)}, bf16[64,3584]{1,0:T(8,128)(2,1)S(1)}, u32[]{:S(2)}, u32[]{:S(2)}) %collective-permute-start.18) | collective-permute-done | bytes 458784 | tf_op jit(solution)/shard_map/ppermute | solution.py:467
  298.3 4.1 %shard_map.175 = (f32[64,3584]{1,0:T(8,128)}, f32[64,3584]{1,0:T(8,128)}, f32[64,3584]{1,0:T(8,128)}) custom-call(s32[1]{0:T(128)} %bitcast.14.x_ref, bf16[16,2,224,128]{3,2,1,0:T(8,128)(2,1)} %all_to_all.36.in_ref.weight_ref, bf16[8,4,224,128]{3,2,1,0:T(8,128)(2,1)} %copy-done.1, f32[64,3584]{1,0:T(8,128)} %get-tuple-element.52.grad_ref, ...), custom_call_target="tpu_custom_call" | custom-call | tf_op jit(solution)/shard_map/pallas_call | solution.py:349
  305.9 4.3 %shard_map.174 = (f32[224,1024]{1,0:T(8,128)}, f32[224,1024]{1,0:T(8,128)}, f32[224,1024]{1,0:T(8,128)}) custom-call(s32[1]{0:T(128)} %bitcast.14.x_ref, bf16[16,2,224,128]{3,2,1,0:T(8,128)(2,1)} %all_to_all.36.in_ref.weight_ref, bf16[8,4,224,128]{3,2,1,0:T(8,128)(2,1)} %copy-done.1, bf16[448,1024]{1,0:T(8,128)(2,1)} %reduce-scatter.2.cloned.1.call-done.grad_ref, ...), custom_call_target="tpu_custom_call" | custom-call | tf_op jit(solution)/shard_map/pallas_call | solution.py:349
  (87 shorter events, 52.5 us)
Async XLA Ops:
  7.2 128.0 %all-gather.2.cloned.1.call-start = ((), (), s32[]{:S(2)}) async-start(), calls=%async_computation.8 | async-start | bytes 8257536 | tf_op jit(solution)/shard_map/all_gather | solution.py:405
  98.6 26.2 %all-to-all-start.3 = ((bf16[16,16,3584]{2,1,0:T(8,128)(2,1)}), bf16[16,16,3584]{2,1,0:T(8,128)(2,1)S(1)}, u32[]{:S(2)}, u32[]{:S(2)}) async-start(bf16[16,16,3584]{2,1,0:T(8,128)(2,1)} %get-tuple-element.37), calls=%async_computation.3 | async-start | bytes 3670016 | tf_op jit(solution)/shard_map/all_to_all | solution.py:369
  104.7 180.3 %reduce-scatter.2.cloned.1.call-start = ((), (), s32[]{:S(2)}) async-start(), calls=%async_computation.9 | async-start | bytes 4587520 | tf_op jit(solution)/shard_map/reduce_scatter | solution.py:449
  104.7 40.2 %collective-permute-start = (bf16[256,3584]{1,0:T(8,128)(2,1)}, bf16[256,3584]{1,0:T(8,128)(2,1)}, u32[]{:S(2)}, u32[]{:S(2)}) collective-permute-start(bf16[256,3584]{1,0:T(8,128)(2,1)} %bitcast.28), channel_id=1, source_target_pairs={{0,1},{1,0},{2,3},{3,2},{4,5},{5,4},{6,7},{7,6},{8,9},{9,8},{10,11... | collective-permute-start | bytes 5505032 | tf_op jit(solution)/shard_map/ppermute | solution.py:373
  104.8 24.4 %collective-permute-start.4 = (bf16[128,3584]{1,0:T(8,128)(2,1)}, bf16[128,3584]{1,0:T(8,128)(2,1)S(1)}, u32[]{:S(2)}, u32[]{:S(2)}) collective-permute-start(bf16[128,3584]{1,0:T(8,128)(2,1)} %get-tuple-element.35.refs_0_), channel_id=1, source_target_pairs={{0,2},{2,4},{4,6},{6,0},{1,3},{3,5},{5,7},{7,1},{8,10},{10,12},{12... | collective-permute-start | bytes 2752520 | tf_op jit(solution)/shard_map/ppermute | solution.py:409
  106.4 23.8 %collective-permute-start.3 = (bf16[128,3584]{1,0:T(8,128)(2,1)}, bf16[128,3584]{1,0:T(8,128)(2,1)}, u32[]{:S(2)}, u32[]{:S(2)}) collective-permute-start(bf16[128,3584]{1,0:T(8,128)(2,1)} %get-tuple-element.35.refs_0_), channel_id=1, source_target_pairs={{0,6},{2,0},{4,2},{6,4},{1,7},{3,1},{5,3},{7,5},{8,14},{10,8},{12,... | collective-permute-start | bytes 2752520 | tf_op jit(solution)/shard_map/ppermute | solution.py:410
  124.8 20.7 %collective-permute-start.2 = (bf16[256,3584]{1,0:T(8,128)(2,1)S(1)}, bf16[256,3584]{1,0:T(8,128)(2,1)}, u32[]{:S(2)}, u32[]{:S(2)}) collective-permute-start(bf16[256,3584]{1,0:T(8,128)(2,1)S(1)} %bitcast.25), channel_id=1, source_target_pairs={{0,1},{1,0},{2,3},{3,2},{4,5},{5,4},{6,7},{7,6},{8,9},{9,8},{10,11... | collective-permute-start | bytes 5505032 | tf_op jit(solution)/shard_map/ppermute | solution.py:373
  130.1 13.8 %collective-permute-start.5 = (bf16[64,3584]{1,0:T(8,128)(2,1)}, bf16[64,3584]{1,0:T(8,128)(2,1)}, u32[]{:S(2)}, u32[]{:S(2)}) collective-permute-start(bf16[64,3584]{1,0:T(8,128)(2,1)} %slice.16), channel_id=1, source_target_pairs={{0,2},{2,4},{4,6},{6,0},{1,3},{3,5},{5,7},{7,1},{8,10},{10,12},{12... | collective-permute-start | bytes 1376264 | tf_op jit(solution)/shard_map/ppermute | solution.py:411
  132.0 12.9 %collective-permute-start.6 = (bf16[64,3584]{1,0:T(8,128)(2,1)}, bf16[64,3584]{1,0:T(8,128)(2,1)}, u32[]{:S(2)}, u32[]{:S(2)}) collective-permute-start(bf16[64,3584]{1,0:T(8,128)(2,1)} %slice.17), channel_id=1, source_target_pairs={{0,6},{2,0},{4,2},{6,4},{1,7},{3,1},{5,3},{7,5},{8,14},{10,8},{12,... | collective-permute-start | bytes 1376264 | tf_op jit(solution)/shard_map/ppermute | solution.py:412
  142.1 3.5 %collective-permute-start.1 = (bf16[256,1024]{1,0:T(8,128)(2,1)S(1)}, bf16[256,1024]{1,0:T(8,128)(2,1)S(1)}, u32[]{:S(2)}, u32[]{:S(2)}) collective-permute-start(bf16[256,1024]{1,0:T(8,128)(2,1)S(1)} %get-tuple-element.61.a_ref), channel_id=1, source_target_pairs={{0,1},{1,0},{2,3},{3,2},{4,5},{5,4},{6,7},{7,6},{8,9},{9,8},{10,11... | collective-permute-start | bytes 1572872 | tf_op jit(solution)/shard_map/ppermute | solution.py:373
  143.8 20.4 %collective-permute-start.7 = (bf16[128,3584]{1,0:T(8,128)(2,1)}, bf16[128,3584]{1,0:T(8,128)(2,1)}, u32[]{:S(2)}, u32[]{:S(2)}) collective-permute-start(bf16[128,3584]{1,0:T(8,128)(2,1)} %get-tuple-element.35.refs_0_), channel_id=1, source_target_pairs={{0,1},{1,0},{2,3},{3,2},{4,5},{5,4},{6,7},{7,6},{8,9},{9,8},{10,11... | collective-permute-start | bytes 2752520 | tf_op jit(solution)/shard_map/ppermute | solution.py:373
  144.9 19.3 %collective-permute-start.8 = (bf16[128,3584]{1,0:T(8,128)(2,1)}, bf16[128,3584]{1,0:T(8,128)(2,1)}, u32[]{:S(2)}, u32[]{:S(2)}) collective-permute-start(bf16[128,3584]{1,0:T(8,128)(2,1)} %collective-permute-done.3.refs_1_), channel_id=1, source_target_pairs={{0,1},{1,0},{2,3},{3,2},{4,5},{5,4},{6,7},{7,6},{8,9},{9,8},{10,11... | collective-permute-start | bytes 2752520 | tf_op jit(solution)/shard_map/ppermute | solution.py:373
  144.9 19.4 %collective-permute-start.11 = (bf16[128,3584]{1,0:T(8,128)(2,1)S(1)}, bf16[128,3584]{1,0:T(8,128)(2,1)}, u32[]{:S(2)}, u32[]{:S(2)}) collective-permute-start(bf16[128,3584]{1,0:T(8,128)(2,1)S(1)} %collective-permute-done.4.refs_4_), channel_id=1, source_target_pairs={{0,1},{1,0},{2,3},{3,2},{4,5},{5,4},{6,7},{7,6},{8,9},{9,8},{10,11... | collective-permute-start | bytes 2752520 | tf_op jit(solution)/shard_map/ppermute | solution.py:373
  145.4 18.8 %collective-permute-start.9 = (bf16[64,3584]{1,0:T(8,128)(2,1)}, bf16[64,3584]{1,0:T(8,128)(2,1)S(1)}, u32[]{:S(2)}, u32[]{:S(2)}) collective-permute-start(bf16[64,3584]{1,0:T(8,128)(2,1)} %collective-permute-done.5.refs_2_), channel_id=1, source_target_pairs={{0,1},{1,0},{2,3},{3,2},{4,5},{5,4},{6,7},{7,6},{8,9},{9,8},{10,11... | collective-permute-start | bytes 1376264 | tf_op jit(solution)/shard_map/ppermute | solution.py:373
  146.3 17.9 %collective-permute-start.10 = (bf16[64,3584]{1,0:T(8,128)(2,1)}, bf16[64,3584]{1,0:T(8,128)(2,1)S(1)}, u32[]{:S(2)}, u32[]{:S(2)}) collective-permute-start(bf16[64,3584]{1,0:T(8,128)(2,1)} %collective-permute-done.6.refs_3_), channel_id=1, source_target_pairs={{0,1},{1,0},{2,3},{3,2},{4,5},{5,4},{6,7},{7,6},{8,9},{9,8},{10,11... | collective-permute-start | bytes 1376264 | tf_op jit(solution)/shard_map/ppermute | solution.py:373
  172.1 2.1 collective-permute-start.12
  215.7 28.2 %all-to-all-start.5 = ((bf16[8,4,224,128]{3,2,1,0:T(8,128)(2,1)}), bf16[8,4,224,128]{3,2,1,0:T(8,128)(2,1)S(1)}, u32[]{:S(2)}, u32[]{:S(2)}) async-start(bf16[8,4,224,128]{3,2,1,0:T(8,128)(2,1)} %shard_map.172), calls=%async_computation.5 | async-start | bytes 3670016 | tf_op jit(solution)/shard_map/all_to_all | solution.py:369
  223.8 28.2 %collective-permute-start.14 = (bf16[64,3584]{1,0:T(8,128)(2,1)}, bf16[64,3584]{1,0:T(8,128)(2,1)S(1)}, u32[]{:S(2)}, u32[]{:S(2)}) collective-permute-start(bf16[64,3584]{1,0:T(8,128)(2,1)} %get-tuple-element.60), channel_id=1, source_target_pairs={{0,2},{2,4},{4,6},{6,0},{1,3},{3,5},{5,7},{7,1},{8,10},{10,12},{12... | collective-permute-start | bytes 1376264 | tf_op jit(solution)/shard_map/ppermute | solution.py:443
  224.4 27.7 %collective-permute-start.15 = (bf16[64,3584]{1,0:T(8,128)(2,1)S(1)}, bf16[64,3584]{1,0:T(8,128)(2,1)S(1)}, u32[]{:S(2)}, u32[]{:S(2)}) collective-permute-start(bf16[64,3584]{1,0:T(8,128)(2,1)S(1)} %get-tuple-element.59), channel_id=1, source_target_pairs={{0,6},{2,0},{4,2},{6,4},{1,7},{3,1},{5,3},{7,5},{8,14},{10,8},{12,... | collective-permute-start | bytes 1376264 | tf_op jit(solution)/shard_map/ppermute | solution.py:444
  245.1 57.3 %all-to-all-start.6 = ((bf16[16,16,3584]{2,1,0:T(8,128)(2,1)}), bf16[16,16,3584]{2,1,0:T(8,128)(2,1)}, u32[]{:S(2)}, u32[]{:S(2)}) async-start(bf16[16,16,3584]{2,1,0:T(8,128)(2,1)} %bitcast.31), calls=%async_computation.6 | async-start | bytes 3670016 | tf_op jit(solution)/shard_map/all_to_all | solution.py:369
  257.2 22.4 %collective-permute-start.16 = (bf16[128,3584]{1,0:T(8,128)(2,1)}, bf16[128,3584]{1,0:T(8,128)(2,1)S(1)}, u32[]{:S(2)}, u32[]{:S(2)}) collective-permute-start(bf16[128,3584]{1,0:T(8,128)(2,1)} %get-tuple-element.50), channel_id=1, source_target_pairs={{0,2},{2,4},{4,6},{6,0},{1,3},{3,5},{5,7},{7,1},{8,10},{10,12},{12... | collective-permute-start | bytes 2752520 | tf_op jit(solution)/shard_map/ppermute | solution.py:456
  257.8 21.8 %collective-permute-start.17 = (bf16[128,3584]{1,0:T(8,128)(2,1)}, bf16[128,3584]{1,0:T(8,128)(2,1)S(1)}, u32[]{:S(2)}, u32[]{:S(2)}) collective-permute-start(bf16[128,3584]{1,0:T(8,128)(2,1)} %get-tuple-element.51), channel_id=1, source_target_pairs={{0,6},{2,0},{4,2},{6,4},{1,7},{3,1},{5,3},{7,5},{8,14},{10,8},{12,... | collective-permute-start | bytes 2752520 | tf_op jit(solution)/shard_map/ppermute | solution.py:457
  283.9 13.6 %collective-permute-start.18 = (bf16[64,3584]{1,0:T(8,128)(2,1)}, bf16[64,3584]{1,0:T(8,128)(2,1)S(1)}, u32[]{:S(2)}, u32[]{:S(2)}) collective-permute-start(bf16[64,3584]{1,0:T(8,128)(2,1)} %get-tuple-element.53), channel_id=1, source_target_pairs={{0,8},{8,0},{1,9},{9,1},{2,10},{10,2},{3,11},{11,3},{4,12},{12,4},... | collective-permute-start | bytes 1376264 | tf_op jit(solution)/shard_map/ppermute | solution.py:467
  286.1 19.0 %collective-permute-start.13 = (bf16[224,1024]{1,0:T(8,128)(2,1)S(1)}, bf16[224,1024]{1,0:T(8,128)(2,1)S(1)}, u32[]{:S(2)}, u32[]{:S(2)}) collective-permute-start(bf16[224,1024]{1,0:T(8,128)(2,1)S(1)} %constant_dynamic-slice_fusion), channel_id=1, source_target_pairs={{0,8},{8,0},{1,9},{9,1},{2,10},{10,2},{3,11},{11,3},{4,12},{12,4},... | collective-permute-start | bytes 1376264 | tf_op jit(solution)/shard_map/ppermute | solution.py:469
  (17 other events, 61.4 us)
Sparse Core Ops, SparseCore 0:
  66.5 44.8 all-gather.1
  180.8 44.5 reduce-scatter.1

commit v7 on v5

--- a/solution.py
+++ b/solution.py
@@ -221,28 +221,25 @@
     )(place, own, other)
 
 
-def half_grad_body(at_ref, xt_ref, own_ref, other_ref, out_ref):
+def up_grad_body(xt_ref, own_ref, other_ref, out_ref):
     rows = own_ref.shape[0]
     total = jnp.dot(xt_ref[:, 0:rows], own_ref[...], preferred_element_type=F32)
     total += jnp.dot(xt_ref[:, rows : 2 * rows], other_ref[...], preferred_element_type=F32)
     out_ref[...] = total.astype(BF)
 
 
-def half_grad(which, flipped, own, other):
+def up_grad_part(flipped, own, other, steps=4):
     width, deep = flipped.shape
     rows, cols = own.shape
-    tall = width // (NX * NY)
-    right = pl.BlockSpec((rows, cols), lambda i, at: (0, 0))
-    return pl.pallas_call(
-        half_grad_body,
-        grid_spec=pltpu.PrefetchScalarGridSpec(
-            num_scalar_prefetch=1,
-            grid=(NY,),
-            in_specs=[pl.BlockSpec((tall, deep), lambda i, at: (i * NX + at[0], 0)), right, right],
-            out_specs=pl.BlockSpec((tall, cols), lambda i, at: (i, 0)),
-        ),
-        out_shape=jax.ShapeDtypeStruct((width // NX, cols), BF),
-    )(which, flipped, own, other)
+    right = pl.BlockSpec((rows, cols), lambda i: (0, 0))
+    return pl.pallas_call(
+        up_grad_body,
+        grid=(steps,),
+        in_specs=[pl.BlockSpec((width // steps, deep), lambda i: (i, 0)), right, right],
+        out_specs=pl.BlockSpec((width // steps, cols), lambda i: (i, 0)),
+        out_shape=jax.ShapeDtypeStruct((width, cols), BF),
+        name="up_part",
+    )(flipped, own, other)
 
 
 def relay_body(part_ref, below_ref, above_ref, up_ref, down_ref):
@@ -296,7 +293,9 @@
 
 
 def adam_up_body(x_ref, weight_ref, state_ref, grad_ref, other_ref, *outs):
-    both = grad_ref[...].astype(F32) + other_ref[...].astype(F32)
+    rows = other_ref.shape[0]
+    own = grad_ref[pl.ds(pl.multiple_of(x_ref[0] * rows, 16), rows)]
+    both = own.astype(F32) + other_ref[...].astype(F32)
     grad = lanes_taken(both, inverse(row_order()))
     for g in range(state_ref.shape[0]):
         lanes = slice(g * LANE, (g + 1) * LANE)
@@ -392,10 +391,12 @@
     upstream = exchange(send_dy, "expert").reshape(-1, features)
     inputs_other, upstream_other = from_partner(inputs), from_partner(upstream)
 
+    flipped = flip(down_place, inputs, inputs_other)
+
     packed = pack_states(
         (up_first[0], up_second[0]), (down_first[0], down_second[0]), groups
     )
-    packed, upstream = lax.optimization_barrier((packed, upstream))
+    packed, upstream, flipped = lax.optimization_barrier((packed, upstream, flipped))
     shares = exchange(packed, "expert")
 
     pre_act = jnp.dot(inputs, up_mat, preferred_element_type=F32)
@@ -408,23 +409,19 @@
     falling = [(i, (i - 1) % NY) for i in range(NY)]
     below = lax.ppermute(down_part[4 * tall : 5 * tall], "y", rising)
     above = lax.ppermute(down_part[5 * tall : 6 * tall], "y", falling)
-    flipped = flip(down_place, inputs, inputs_other)
-    upstream, flipped, _ = lax.optimization_barrier((upstream, flipped, down_part))
+    upstream, _ = lax.optimization_barrier((upstream, down_part))
     back = lax.dot_general(upstream, down_mat, (((1,), (1,)), ((), ())), preferred_element_type=F32)
     pre_grad = (back * slopes).astype(BF)
     pre_grad_other = from_partner(pre_grad)
-    ordered = order_states(old_owner, new_owner, shares, 1)
-    ordered, pre_grad = lax.optimization_barrier((ordered, pre_grad))
-    states = exchange(ordered, "expert")
-    up_far = half_grad(1 - x_at, flipped, pre_grad, pre_grad_other)
-    up_far_sum = lax.psum_scatter(up_far, "y", scatter_dimension=0, tiled=True)
-    pre_grad, up_far = lax.optimization_barrier((pre_grad, up_far))
-    up_own = half_grad(x_at, flipped, pre_grad, pre_grad_other)
-    up_sum = lax.psum_scatter(up_own, "y", scatter_dimension=0, tiled=True)
-    pre_grad, down_part, up_own = lax.optimization_barrier((pre_grad, down_part, up_own))
+    down_part, pre_grad = lax.optimization_barrier((down_part, pre_grad))
     going_up, going_down = relay(down_part, below, above)
     below = lax.ppermute(going_up, "y", rising)
     above = lax.ppermute(going_down, "y", falling)
+    up_part = up_grad_part(flipped, pre_grad, pre_grad_other)
+    up_sum = lax.psum_scatter(up_part, "y", scatter_dimension=0, tiled=True)
+    ordered = order_states(old_owner, new_owner, shares, 1)
+    ordered, up_part, pre_grad = lax.optimization_barrier((ordered, up_part, pre_grad))
+    states = exchange(ordered, "expert")
     input_grad = lax.dot_general(
         pre_grad, up_mat, (((1,), (1,)), ((), ())), preferred_element_type=F32
     ).astype(BF)
@@ -435,7 +432,8 @@
     swap = [(0, 1), (1, 0)]
     down_own, down_send = finish(x_at, down_part, below, above)
     down_other = lax.ppermute(down_send, "x", swap)
-    up_other = lax.ppermute(up_far_sum, "x", swap)
+    up_send = lax.dynamic_slice_in_dim(up_sum, (1 - x_at[0]) * up_shape[0], up_shape[0])
+    up_other = lax.ppermute(up_send, "x", swap)
     down_new = adam(adam_down_body, x_at, weights, states, 1, (down_own, down_other), down_shape)
     up_new = adam(adam_up_body, x_at, weights, states, 0, (up_sum, up_other), up_shape)
     return (

time: 301 us -> 310 us (1.030)
  blocking collectives: 78.7 us -> 108 us
  waiting for transfers between devices: 80 us -> 70.5 us
  starting transfers between devices: 35.8 us -> 29.4 us
  Pallas kernels: 59.2 us -> 55.3 us
    all_to_all x3 -> x4, blocking collectives: 78.7 us -> 108 us  [exchange(): return lax.all_to_all(array, axis, split_axis=0, concat_axis=0, tiled=True)]
    ppermute x1, waiting for transfers between devices: 33.5 us -> 18.4 us  [step(): below = lax.ppermute(going_up, 'y', rising)]
    all_gather x1, waiting for transfers between devices: 0.78 us -> 8.64 us  [step(): down_mat = lax.all_gather(down_pair, ('core', 'y'), axis=0, tiled=True)]
    all_to_all x4 -> x3, starting transfers between devices: 26.4 us -> 19.9 us  [exchange(): return lax.all_to_all(array, axis, split_axis=0, concat_axis=0, tiled=True)]
    pallas_call x2 -> x1, Pallas kernels: 9.39 us -> 5.62 us  [up_grad_part(): pl.pallas_call(up_grad_body, grid=(steps,), in_specs=[pl.BlockSpec((width...]
    all_to_all x4 -> x3, waiting for transfers between devices: 32.9 us -> 30.6 us  [exchange(): return lax.all_to_all(array, axis, split_axis=0, concat_axis=0, tiled=True)]
    unnamed x29 -> x33, local copies, waits for them, and re-layouts: 9.65 us -> 9.37 us
  transfers between devices with their start and end apart: 18 -> 16, of which waited for: 7 -> 6; matrix products, arithmetic and copies ran while one was open for 8% -> 6% of each run, Pallas kernels for 14% -> 12%
where the time goes in v7:
time: 310 us; the launch traced here: 309 us
  blocking collectives  108 us (35%)
  waiting for transfers between devices  70.5 us (23%)
  Pallas kernels  55.3 us (18%)
  starting transfers between devices  29.4 us (9%)
  matrix products  18.5 us (6%)
  between operations  13.8 us (4%)
  local copies, waits for them, and re-layouts  12.5 us (4%)
    all_to_all x4, blocking collectives, exchange(): return lax.all_to_all(array, axis, split_axis=0, concat_axis=0, tiled=True)  108 us
    all_to_all x3, waiting for transfers between devices, exchange(): return lax.all_to_all(array, axis, split_axis=0, concat_axis=0, tiled=True)  30.6 us
    all_to_all x3, starting transfers between devices, exchange(): return lax.all_to_all(array, axis, split_axis=0, concat_axis=0, tiled=True)  19.9 us
    ppermute x1, waiting for transfers between devices, step(): below = lax.ppermute(going_up, 'y', rising)  18.4 us
    ppermute x1, waiting for transfers between devices, step(): down_other = lax.ppermute(down_send, 'x', swap)  10.4 us
    unnamed x33, local copies, waits for them, and re-layouts  9.37 us
    all_gather x1, waiting for transfers between devices, step(): down_mat = lax.all_gather(down_pair, ('core', 'y'), axis=0, tiled=True)  8.64 us
    pallas_call x2, Pallas kernels, adam(): pl.pallas_call(body, grid=(1,), in_specs=[smem(), pl.BlockSpec((weights.s...  8.41 us
  transfers between devices with their start and end apart: 16, of which 6 were waited for; matrix products, arithmetic and copies ran while one was open for 6% of the time, Pallas kernels for 12%

profile of v7, /device:TPU:4, one launch (start us, length us, event | category | flops | bytes accessed | tf_op | source)
XLA Modules:
  0.0 309.0 jit_solution(16525311181940198581)
XLA Ops:
  9.7 21.5 %all_to_all.35.in_ref = bf16[8,2,224,128]{3,2,1,0:T(8,128)(2,1)} all-to-all(bf16[8,2,224,128]{3,2,1,0:T(8,128)(2,1)} %pack_weights.1), channel_id=1, replica_groups=mesh['expert'=8,'x'=2,'y'=4,'core'=2] {'expert'}, dimensions={0} | all-to-all | bytes 1835008 | tf_op jit(solution)/shard_map/all_to_all | solution.py:341
  33.8 29.5 %all_to_all.36.in_ref.weight_ref = bf16[16,2,224,128]{3,2,1,0:T(8,128)(2,1)} all-to-all(bf16[16,2,224,128]{3,2,1,0:T(8,128)(2,1)} %shard_map.171), channel_id=1, replica_groups=mesh['expert'=8,'x'=2,'y'=4,'core'=2] {'expert','x'}, dimensions={0} | all-to-all | bytes 3670016 | tf_op jit(solution)/shard_map/all_to_all | solution.py:341
  67.8 3.8 %dispatch.1 = (bf16[16,16,3584]{2,1,0:T(8,128)(2,1)}, bf16[16,16,3584]{2,1,0:T(8,128)(2,1)}) custom-call(s32[8,1]{1,0:T(8,128)} %copy.20.ids_ref, s32[8]{0:T(128)} %count_ref.1, s32[8]{0:T(128)} %own_ref.3, bf16[8,16,3584]{2,1,0:T(8,128)(2,1)} %bitcast.31, bf16[8,16,3584]{2,1,0:T(8,128)(2,1)} %bitcast.32), custom_call_target="tpu_custom_call" | custom-call | tf_op jit(solution)/shard_map/dispatch/pallas_call | solution.py:109
  71.6 26.8 %all_to_all.37 = bf16[16,16,3584]{2,1,0:T(8,128)(2,1)S(1)} all-to-all(bf16[16,16,3584]{2,1,0:T(8,128)(2,1)} %get-tuple-element.37), channel_id=1, replica_groups=mesh['expert'=8,'x'=2,'y'=4,'core'=2] {'expert'}, dimensions={0} | all-to-all | bytes 3670016 | tf_op jit(solution)/shard_map/all_to_all | solution.py:341
  98.5 6.9 %all-to-all-start.3 = ((bf16[16,16,3584]{2,1,0:T(8,128)(2,1)}), bf16[16,16,3584]{2,1,0:T(8,128)(2,1)}, u32[]{:S(2)}, u32[]{:S(2)}) async-start(bf16[16,16,3584]{2,1,0:T(8,128)(2,1)} %get-tuple-element.38), calls=%async_computation.3 | async-start | bytes 3670016 | tf_op jit(solution)/shard_map/all_to_all | solution.py:341
  105.4 20.1 %all-to-all-done.3 = bf16[16,16,3584]{2,1,0:T(8,128)(2,1)} async-done(((bf16[16,16,3584]{2,1,0:T(8,128)(2,1)}), bf16[16,16,3584]{2,1,0:T(8,128)(2,1)}, u32[]{:S(2)}, u32[]{:S(2)}) %all-to-all-start.3) | async-done | bytes 1835040 | tf_op jit(solution)/shard_map/all_to_all | solution.py:341
  125.5 6.2 %multiply_convert_fusion = (bf16[256,1024]{1,0:T(8,128)(2,1)S(1)}, f32[256,1024]{1,0:T(8,128)}) fusion(bf16[256,3584]{1,0:T(8,128)(2,1)S(1)} %bitcast.28, bf16[3584,1024]{1,0:T(8,128)(2,1)} %all-gather.3.cloned.1.call-done), kind=kOutput, calls=%fused_computation.3 | convolution fusion | flops 1880358912 | bytes 10747904 | tf_op jit(solution)/shard_map/dot_general | solution.py:402
  132.1 3.5 %pack_states.1 = bf16[8,4,224,128]{3,2,1,0:T(8,128)(2,1)} custom-call(f32[224,1024]{1,0:T(8,128)} %bitcast.36, f32[224,1024]{1,0:T(8,128)} %bitcast.37, f32[64,3584]{1,0:T(8,128)} %bitcast.38, f32[64,3584]{1,0:T(8,128)} %bitcast.39), custom_call_target="tpu_custom_call" | custom-call | tf_op jit(solution)/shard_map/pack_states/pallas_call | solution.py:153
  136.2 6.3 %flip.1.xt_ref = bf16[1792,512]{1,0:T(8,128)(2,1)} custom-call(s32[2]{0:T(128)} %pad_add_fusion.core_ref.half_ref, bf16[256,3584]{1,0:T(8,128)(2,1)} %bitcast.29, bf16[256,3584]{1,0:T(8,128)(2,1)} %collective-permute-done.other_ref), custom_call_target="tpu_custom_call" | custom-call | tf_op jit(solution)/shard_map/flip/pallas_call | solution.py:211
  143.3 7.0 %shard_map.173.part_ref = bf16[512,3584]{1,0:T(8,128)(2,1)} custom-call(s32[2]{0:T(128)} %pad_add_fusion.core_ref.half_ref, bf16[256,1024]{1,0:T(8,128)(2,1)} %copy-done.7, bf16[256,1024]{1,0:T(8,128)(2,1)} %copy-done.8, bf16[256,3584]{1,0:T(8,128)(2,1)} %bitcast.8.b_ref, bf16[256,3584]{1,0:T(8,128)(2,1)} %collective-permute-done.2.bo_ref), custom_call_target="tpu_custom_call" | custom-call | tf_op jit(solution)/shard_map/pallas_call | solution.py:189
  150.4 8.6 %all-gather.5.cloned.1.call-done = bf16[1024,3584]{1,0:T(8,128)(2,1)} async-done(((bf16[128,3584]{1,0:T(8,128)(2,1)}), bf16[1024,3584]{1,0:T(8,128)(2,1)}) %all-gather.5.cloned.1.call-update) | async-done | bytes 7340048 | tf_op jit(solution)/shard_map/all_gather | solution.py:378
  159.0 5.8 %fusion.own_ref = bf16[256,1024]{1,0:T(8,128)(2,1)S(1)} fusion(bf16[256,3584]{1,0:T(8,128)(2,1)} %bitcast.8.b_ref, bf16[1024,3584]{1,0:T(8,128)(2,1)} %all-gather.5.cloned.1.call-done, f32[256,1024]{1,0:T(8,128)S(1)} %copy-done.15), kind=kOutput, calls=%fused_computation.2 | convolution fusion | flops 1881407488 | bytes 10747904 | tf_op jit(solution)/shard_map/dot_general | solution.py:413
  167.6 5.6 %up_part.1 = bf16[1792,1024]{1,0:T(8,128)(2,1)} custom-call(bf16[1792,512]{1,0:T(8,128)(2,1)} %flip.1.xt_ref, bf16[256,1024]{1,0:T(8,128)(2,1)} %copy-done.5, bf16[256,1024]{1,0:T(8,128)(2,1)} %copy-done.9), custom_call_target="tpu_custom_call" | custom-call | tf_op jit(solution)/shard_map/up_part/pallas_call | solution.py:235
  174.8 30.7 %all_to_all.38.in_ref = bf16[8,4,224,128]{3,2,1,0:T(8,128)(2,1)} all-to-all(bf16[8,4,224,128]{3,2,1,0:T(8,128)(2,1)S(1)} %copy-done.2), channel_id=1, replica_groups=mesh['expert'=8,'x'=2,'y'=4,'core'=2] {'expert'}, dimensions={0} | all-to-all | bytes 3670016 | tf_op jit(solution)/shard_map/all_to_all | solution.py:341
  208.4 6.2 %all-to-all-start.5 = ((bf16[8,4,224,128]{3,2,1,0:T(8,128)(2,1)}), bf16[8,4,224,128]{3,2,1,0:T(8,128)(2,1)S(1)}, u32[]{:S(2)}, u32[]{:S(2)}) async-start(bf16[8,4,224,128]{3,2,1,0:T(8,128)(2,1)} %shard_map.172), calls=%async_computation.5 | async-start | bytes 3670016 | tf_op jit(solution)/shard_map/all_to_all | solution.py:341
  219.8 6.4 %convolution_convert_fusion = bf16[256,3584]{1,0:T(8,128)(2,1)} fusion(bf16[256,1024]{1,0:T(8,128)(2,1)S(1)} %copy-done.6, bf16[3584,1024]{1,0:T(8,128)(2,1)} %all-gather.3.cloned.1.call-done), kind=kOutput, calls=%fused_computation | convolution fusion | flops 1879965696 | bytes 9699328 | tf_op jit(solution)/shard_map/dot_general | solution.py:425
  226.3 10.5 %all-to-all-done.5.state_ref = bf16[8,4,224,128]{3,2,1,0:T(8,128)(2,1)S(1)} async-done(((bf16[8,4,224,128]{3,2,1,0:T(8,128)(2,1)}), bf16[8,4,224,128]{3,2,1,0:T(8,128)(2,1)S(1)}, u32[]{:S(2)}, u32[]{:S(2)}) %all-to-all-start.5) | async-done | bytes 1835040 | tf_op jit(solution)/shard_map/all_to_all | solution.py:341
  238.1 6.9 %all-to-all-start.6 = ((bf16[16,16,3584]{2,1,0:T(8,128)(2,1)}), bf16[16,16,3584]{2,1,0:T(8,128)(2,1)}, u32[]{:S(2)}, u32[]{:S(2)}) async-start(bf16[16,16,3584]{2,1,0:T(8,128)(2,1)} %bitcast.30), calls=%async_computation.6 | async-start | bytes 3670016 | tf_op jit(solution)/shard_map/all_to_all | solution.py:341
  246.6 3.6 %relay.1 = (bf16[128,3584]{1,0:T(8,128)(2,1)}, bf16[128,3584]{1,0:T(8,128)(2,1)}) custom-call(bf16[512,3584]{1,0:T(8,128)(2,1)} %shard_map.173.part_ref, bf16[64,3584]{1,0:T(8,128)(2,1)} %copy-done.10, bf16[64,3584]{1,0:T(8,128)(2,1)} %copy-done.11), custom_call_target="tpu_custom_call" | custom-call | tf_op jit(solution)/shard_map/relay/pallas_call | solution.py:259
  253.5 18.4 %collective-permute-done.7.below_ref = bf16[128,3584]{1,0:T(8,128)(2,1)S(1)} collective-permute-done((bf16[128,3584]{1,0:T(8,128)(2,1)}, bf16[128,3584]{1,0:T(8,128)(2,1)S(1)}, u32[]{:S(2)}, u32[]{:S(2)}) %collective-permute-start.7) | collective-permute-done | bytes 917536 | tf_op jit(solution)/shard_map/ppermute | solution.py:418
  273.0 3.1 %finish.1 = (f32[64,3584]{1,0:T(8,128)}, bf16[64,3584]{1,0:T(8,128)(2,1)}) custom-call(s32[1]{0:T(128)} %bitcast.14.x_ref, bf16[512,3584]{1,0:T(8,128)(2,1)} %shard_map.173.part_ref, bf16[128,3584]{1,0:T(8,128)(2,1)} %copy-done.3, bf16[128,3584]{1,0:T(8,128)(2,1)} %copy-done.4), custom_call_target="tpu_custom_call" | custom-call | tf_op jit(solution)/shard_map/finish/pallas_call | solution.py:275
  279.3 10.4 %collective-permute-done.9.other_ref = bf16[64,3584]{1,0:T(8,128)(2,1)S(1)} collective-permute-done((bf16[64,3584]{1,0:T(8,128)(2,1)}, bf16[64,3584]{1,0:T(8,128)(2,1)S(1)}, u32[]{:S(2)}, u32[]{:S(2)}) %collective-permute-start.9) | collective-permute-done | bytes 458784 | tf_op jit(solution)/shard_map/ppermute | solution.py:434
  290.5 4.1 %shard_map.175 = (f32[64,3584]{1,0:T(8,128)}, f32[64,3584]{1,0:T(8,128)}, f32[64,3584]{1,0:T(8,128)}) custom-call(s32[1]{0:T(128)} %bitcast.14.x_ref, bf16[16,2,224,128]{3,2,1,0:T(8,128)(2,1)} %all_to_all.36.in_ref.weight_ref, bf16[8,4,224,128]{3,2,1,0:T(8,128)(2,1)} %copy-done, f32[64,3584]{1,0:T(8,128)} %get-tuple-element.54.grad_ref, ...), custom_call_target="tpu_custom_call" | custom-call | tf_op jit(solution)/shard_map/pallas_call | solution.py:321
  298.1 4.3 %shard_map.174 = (f32[224,1024]{1,0:T(8,128)}, f32[224,1024]{1,0:T(8,128)}, f32[224,1024]{1,0:T(8,128)}) custom-call(s32[1]{0:T(128)} %bitcast.14.x_ref, bf16[16,2,224,128]{3,2,1,0:T(8,128)(2,1)} %all_to_all.36.in_ref.weight_ref, bf16[8,4,224,128]{3,2,1,0:T(8,128)(2,1)} %copy-done, bf16[448,1024]{1,0:T(8,128)(2,1)} %reduce-scatter.2.cloned.1.call-done.grad_ref, ...), custom_call_target="tpu_custom_call" | custom-call | tf_op jit(solution)/shard_map/pallas_call | solution.py:321
  (68 shorter events, 38.7 us)
Async XLA Ops:
  7.2 118.3 %all-gather.3.cloned.1.call-start = ((), (), s32[]{:S(2)}) async-start(), calls=%async_computation.8 | async-start | bytes 8257536 | tf_op jit(solution)/shard_map/all_gather | solution.py:377
  63.3 3.9 %copy-start.14 = (s32[8,1]{0,1:T(1,128)S(1)}, s32[8,1]{0,1:T(1,128)}, u32[]{:S(2)}) copy-start(s32[8,1]{0,1:T(1,128)} %param.14) | copy-start | bytes 100
  66.4 92.6 %all-gather.5.cloned.1.call-start = ((), (), s32[]{:S(2)}) async-start(), calls=%async_computation.9 | async-start | bytes 8257536 | tf_op jit(solution)/shard_map/all_gather | solution.py:378
  98.5 27.0 %copy-start.1 = (bf16[16,16,3584]{2,1,0:T(8,128)(2,1)}, bf16[16,16,3584]{2,1,0:T(8,128)(2,1)S(1)}, u32[]{:S(2)}) copy-start(bf16[16,16,3584]{2,1,0:T(8,128)(2,1)S(1)} %all_to_all.37) | copy-start | bytes 5505028
  98.5 27.0 %all-to-all-start.3 = ((bf16[16,16,3584]{2,1,0:T(8,128)(2,1)}), bf16[16,16,3584]{2,1,0:T(8,128)(2,1)}, u32[]{:S(2)}, u32[]{:S(2)}) async-start(bf16[16,16,3584]{2,1,0:T(8,128)(2,1)} %get-tuple-element.38), calls=%async_computation.3 | async-start | bytes 3670016 | tf_op jit(solution)/shard_map/all_to_all | solution.py:341
  105.4 172.0 %reduce-scatter.2.cloned.1.call-start = ((), (), s32[]{:S(2)}) async-start(), calls=%async_computation.10 | async-start | bytes 4587520 | tf_op jit(solution)/shard_map/reduce_scatter | solution.py:421
  105.4 30.8 %collective-permute-start = (bf16[256,3584]{1,0:T(8,128)(2,1)S(1)}, bf16[256,3584]{1,0:T(8,128)(2,1)}, u32[]{:S(2)}, u32[]{:S(2)}) collective-permute-start(bf16[256,3584]{1,0:T(8,128)(2,1)S(1)} %bitcast.27), channel_id=1, source_target_pairs={{0,1},{1,0},{2,3},{3,2},{4,5},{5,4},{6,7},{7,6},{8,9},{9,8},{10,11... | collective-permute-start | bytes 5505032 | tf_op jit(solution)/shard_map/ppermute | solution.py:345
  125.5 17.0 %collective-permute-start.2 = (bf16[256,3584]{1,0:T(8,128)(2,1)}, bf16[256,3584]{1,0:T(8,128)(2,1)}, u32[]{:S(2)}, u32[]{:S(2)}) collective-permute-start(bf16[256,3584]{1,0:T(8,128)(2,1)} %bitcast.8.b_ref), channel_id=1, source_target_pairs={{0,1},{1,0},{2,3},{3,2},{4,5},{5,4},{6,7},{7,6},{8,9},{9,8},{10,11... | collective-permute-start | bytes 5505032 | tf_op jit(solution)/shard_map/ppermute | solution.py:345
  131.7 3.9 %copy-start.7 = (bf16[256,1024]{1,0:T(8,128)(2,1)}, bf16[256,1024]{1,0:T(8,128)(2,1)S(1)}, u32[]{:S(2)}) copy-start(bf16[256,1024]{1,0:T(8,128)(2,1)S(1)} %get-tuple-element.63.a_ref) | copy-start | bytes 1572868
  131.7 10.8 %collective-permute-start.1 = (bf16[256,1024]{1,0:T(8,128)(2,1)S(1)}, bf16[256,1024]{1,0:T(8,128)(2,1)S(1)}, u32[]{:S(2)}, u32[]{:S(2)}) collective-permute-start(bf16[256,1024]{1,0:T(8,128)(2,1)S(1)} %get-tuple-element.63.a_ref), channel_id=1, source_target_pairs={{0,1},{1,0},{2,3},{3,2},{4,5},{5,4},{6,7},{7,6},{8,9},{9,8},{10,11... | collective-permute-start | bytes 1572872 | tf_op jit(solution)/shard_map/ppermute | solution.py:345
  142.5 16.5 %copy-start.15 = (f32[256,1024]{1,0:T(8,128)S(1)}, f32[256,1024]{1,0:T(8,128)}, u32[]{:S(2)}) copy-start(f32[256,1024]{1,0:T(8,128)} %get-tuple-element.64) | copy-start | bytes 3145732
  164.8 2.0 copy-start.5
  164.9 2.0 collective-permute-start.3
  173.3 1.5 copy-start.2
  208.4 28.4 %all-to-all-start.5 = ((bf16[8,4,224,128]{3,2,1,0:T(8,128)(2,1)}), bf16[8,4,224,128]{3,2,1,0:T(8,128)(2,1)S(1)}, u32[]{:S(2)}, u32[]{:S(2)}) async-start(bf16[8,4,224,128]{3,2,1,0:T(8,128)(2,1)} %shard_map.172), calls=%async_computation.5 | async-start | bytes 3670016 | tf_op jit(solution)/shard_map/all_to_all | solution.py:341
  214.6 5.3 %copy-start.6 = (bf16[256,1024]{1,0:T(8,128)(2,1)S(1)}, bf16[256,1024]{1,0:T(8,128)(2,1)}, u32[]{:S(2)}) copy-start(bf16[256,1024]{1,0:T(8,128)(2,1)} %copy-done.5) | copy-start | bytes 1572868
  216.6 28.5 %collective-permute-start.5 = (bf16[64,3584]{1,0:T(8,128)(2,1)}, bf16[64,3584]{1,0:T(8,128)(2,1)S(1)}, u32[]{:S(2)}, u32[]{:S(2)}) collective-permute-start(bf16[64,3584]{1,0:T(8,128)(2,1)} %get-tuple-element.62), channel_id=1, source_target_pairs={{0,2},{2,4},{4,6},{6,0},{1,3},{3,5},{5,7},{7,1},{8,10},{10,12},{12... | collective-permute-start | bytes 1376264 | tf_op jit(solution)/shard_map/ppermute | solution.py:410
  217.3 27.8 %collective-permute-start.6 = (bf16[64,3584]{1,0:T(8,128)(2,1)S(1)}, bf16[64,3584]{1,0:T(8,128)(2,1)S(1)}, u32[]{:S(2)}, u32[]{:S(2)}) collective-permute-start(bf16[64,3584]{1,0:T(8,128)(2,1)S(1)} %get-tuple-element.61), channel_id=1, source_target_pairs={{0,6},{2,0},{4,2},{6,4},{1,7},{3,1},{5,3},{7,5},{8,14},{10,8},{12,... | collective-permute-start | bytes 1376264 | tf_op jit(solution)/shard_map/ppermute | solution.py:411
  236.8 1.3 copy-start
  238.1 56.5 %all-to-all-start.6 = ((bf16[16,16,3584]{2,1,0:T(8,128)(2,1)}), bf16[16,16,3584]{2,1,0:T(8,128)(2,1)}, u32[]{:S(2)}, u32[]{:S(2)}) async-start(bf16[16,16,3584]{2,1,0:T(8,128)(2,1)} %bitcast.30), calls=%async_computation.6 | async-start | bytes 3670016 | tf_op jit(solution)/shard_map/all_to_all | solution.py:341
  250.2 21.6 %collective-permute-start.7 = (bf16[128,3584]{1,0:T(8,128)(2,1)}, bf16[128,3584]{1,0:T(8,128)(2,1)S(1)}, u32[]{:S(2)}, u32[]{:S(2)}) collective-permute-start(bf16[128,3584]{1,0:T(8,128)(2,1)} %get-tuple-element.52), channel_id=1, source_target_pairs={{0,2},{2,4},{4,6},{6,0},{1,3},{3,5},{5,7},{7,1},{8,10},{10,12},{12... | collective-permute-start | bytes 2752520 | tf_op jit(solution)/shard_map/ppermute | solution.py:418
  250.8 21.0 %collective-permute-start.8 = (bf16[128,3584]{1,0:T(8,128)(2,1)}, bf16[128,3584]{1,0:T(8,128)(2,1)S(1)}, u32[]{:S(2)}, u32[]{:S(2)}) collective-permute-start(bf16[128,3584]{1,0:T(8,128)(2,1)} %get-tuple-element.53), channel_id=1, source_target_pairs={{0,6},{2,0},{4,2},{6,4},{1,7},{3,1},{5,3},{7,5},{8,14},{10,8},{12,... | collective-permute-start | bytes 2752520 | tf_op jit(solution)/shard_map/ppermute | solution.py:419
  276.2 13.6 %collective-permute-start.9 = (bf16[64,3584]{1,0:T(8,128)(2,1)}, bf16[64,3584]{1,0:T(8,128)(2,1)S(1)}, u32[]{:S(2)}, u32[]{:S(2)}) collective-permute-start(bf16[64,3584]{1,0:T(8,128)(2,1)} %get-tuple-element.55), channel_id=1, source_target_pairs={{0,8},{8,0},{1,9},{9,1},{2,10},{10,2},{3,11},{11,3},{4,12},{12,4},... | collective-permute-start | bytes 1376264 | tf_op jit(solution)/shard_map/ppermute | solution.py:434
  278.4 18.9 %collective-permute-start.4 = (bf16[224,1024]{1,0:T(8,128)(2,1)S(1)}, bf16[224,1024]{1,0:T(8,128)(2,1)S(1)}, u32[]{:S(2)}, u32[]{:S(2)}) collective-permute-start(bf16[224,1024]{1,0:T(8,128)(2,1)S(1)} %constant_dynamic-slice_fusion), channel_id=1, source_target_pairs={{0,8},{8,0},{1,9},{9,1},{2,10},{10,2},{3,11},{11,3},{4,12},{12,4},... | collective-permute-start | bytes 1376264 | tf_op jit(solution)/shard_map/ppermute | solution.py:436
  (8 other events, 6.8 us)
Sparse Core Ops, SparseCore 0:
  66.5 44.7 all-gather.2
  113.6 45.3 all-gather.4
  173.4 42.6 reduce-scatter.1

commit v8 on v6

--- a/solution.py
+++ b/solution.py
@@ -439,25 +439,24 @@
     active, slopes = silu_parts(pre_act)
     hidden = active.astype(BF)
     hidden_other = from_partner(hidden)
-    down_part = weight_grad(down_place, hidden, hidden_other, upstream, upstream_other, 128)
-    below = lax.ppermute(down_part[4 * tall : 5 * tall], "y", rising)
-    above = lax.ppermute(down_part[5 * tall : 6 * tall], "y", falling)
-    slopes, _ = lax.optimization_barrier((slopes, down_part))
     pre_grad = back_grad(down_place, upstream, slopes, pieces)
     pre_grad_other = from_partner(pre_grad)
     up_part = up_grad_part(flipped, pre_grad, pre_grad_other)
     up_sum = lax.psum_scatter(up_part, "y", scatter_dimension=0, tiled=True)
+    down_late, _ = lax.optimization_barrier((down_place, up_part))
+    down_part = weight_grad(down_late, hidden, hidden_other, upstream, upstream_other, 128)
+    below = lax.ppermute(down_part[4 * tall : 5 * tall], "y", rising)
+    above = lax.ppermute(down_part[5 * tall : 6 * tall], "y", falling)
     ordered = order_states(old_owner, new_owner, shares, 1)
-    ordered, up_part, pre_grad, down_part = lax.optimization_barrier(
-        (ordered, up_part, pre_grad, down_part)
-    )
+    ordered, pre_grad, _ = lax.optimization_barrier((ordered, pre_grad, down_part))
     states = exchange(ordered, "expert")
+    input_grad = lax.dot_general(
+        pre_grad, up_mat, (((1,), (1,)), ((), ())), preferred_element_type=F32
+    ).astype(BF)
+    down_part, input_grad = lax.optimization_barrier((down_part, input_grad))
     going_up, going_down = relay(down_part, below, above)
     below = lax.ppermute(going_up, "y", rising)
     above = lax.ppermute(going_down, "y", falling)
-    input_grad = lax.dot_general(
-        pre_grad, up_mat, (((1,), (1,)), ((), ())), preferred_element_type=F32
-    ).astype(BF)
     input_grad, states = lax.optimization_barrier((input_grad, states))
     returned = exchange(input_grad.reshape(-1, rows, features), "expert")
     token_grad = combine(block_expert, new_owner, returned).reshape(tok_rows, features)

time: 318 us -> 324 us (1.019)
  blocking collectives: 109 us -> 78.7 us
  waiting for transfers between devices: 64.9 us -> 94.5 us
  starting transfers between devices: 36.5 us -> 43.6 us
    all_to_all x4 -> x3, blocking collectives: 109 us -> 78.7 us  [exchange(): return lax.all_to_all(array, axis, split_axis=0, concat_axis=0, tiled=True)]
    ppermute x1, waiting for transfers between devices: 4.4 us -> 21.2 us  [step(): w_below = lax.ppermute(down_pair, 'y', rising)]
    all_to_all x3 -> x4, waiting for transfers between devices: 26.5 us -> 34.1 us  [exchange(): return lax.all_to_all(array, axis, split_axis=0, concat_axis=0, tiled=True)]
    all_to_all x3 -> x4, starting transfers between devices: 19.2 us -> 26.7 us  [exchange(): return lax.all_to_all(array, axis, split_axis=0, concat_axis=0, tiled=True)]
    ppermute x1, waiting for transfers between devices: 1.75 us -> 8.6 us  [step(): w_low = lax.ppermute(w_below[:tall], 'y', rising)]
    unnamed x35 -> x33, local copies, waits for them, and re-layouts: 10.2 us -> 10.1 us
  transfers between devices with their start and end apart: 24 -> 25, of which waited for: 8 -> 7; matrix products, arithmetic and copies ran while one was open for 6% -> 6% of each run, Pallas kernels for 12% -> 12%
where the time goes in v8:
time: 324 us; the launch traced here: 322 us
  waiting for transfers between devices  94.5 us (29%)
  blocking collectives  78.7 us (24%)
  Pallas kernels  62.3 us (19%)
  starting transfers between devices  43.6 us (13%)
  local copies, waits for them, and re-layouts  14.5 us (4%)
  between operations  14.2 us (4%)
  matrix products  14.1 us (4%)
    all_to_all x3, blocking collectives, exchange(): return lax.all_to_all(array, axis, split_axis=0, concat_axis=0, tiled=True)  78.7 us
    all_to_all x4, waiting for transfers between devices, exchange(): return lax.all_to_all(array, axis, split_axis=0, concat_axis=0, tiled=True)  34.1 us
    all_to_all x4, starting transfers between devices, exchange(): return lax.all_to_all(array, axis, split_axis=0, concat_axis=0, tiled=True)  26.7 us
    ppermute x1, waiting for transfers between devices, step(): w_below = lax.ppermute(down_pair, 'y', rising)  21.2 us
    ppermute x1, waiting for transfers between devices, step(): below = lax.ppermute(going_up, 'y', rising)  18.4 us
    ppermute x1, waiting for transfers between devices, step(): down_other = lax.ppermute(down_send, 'x', swap)  10.4 us
    unnamed x33, local copies, waits for them, and re-layouts  10.1 us
    ppermute x1, waiting for transfers between devices, step(): w_low = lax.ppermute(w_below[:tall], 'y', rising)  8.6 us
  transfers between devices with their start and end apart: 25, of which 7 were waited for; matrix products, arithmetic and copies ran while one was open for 6% of the time, Pallas kernels for 12%

profile of v8, /device:TPU:4, one launch (start us, length us, event | category | flops | bytes accessed | tf_op | source)
XLA Modules:
  0.0 322.4 jit_solution(5428005694657648650)
XLA Ops:
  9.7 21.5 %all_to_all.35.in_ref = bf16[8,2,224,128]{3,2,1,0:T(8,128)(2,1)} all-to-all(bf16[8,2,224,128]{3,2,1,0:T(8,128)(2,1)} %pack_weights.1), channel_id=1, replica_groups=mesh['expert'=8,'x'=2,'y'=4,'core'=2] {'expert'}, dimensions={0} | all-to-all | bytes 1835008 | tf_op jit(solution)/shard_map/all_to_all | solution.py:369
  33.7 29.5 %all_to_all.36.in_ref.weight_ref = bf16[16,2,224,128]{3,2,1,0:T(8,128)(2,1)} all-to-all(bf16[16,2,224,128]{3,2,1,0:T(8,128)(2,1)} %shard_map.171), channel_id=1, replica_groups=mesh['expert'=8,'x'=2,'y'=4,'core'=2] {'expert','x'}, dimensions={0} | all-to-all | bytes 3670016 | tf_op jit(solution)/shard_map/all_to_all | solution.py:369
  67.0 3.9 %dispatch.1 = (bf16[16,16,3584]{2,1,0:T(8,128)(2,1)}, bf16[16,16,3584]{2,1,0:T(8,128)(2,1)}) custom-call(s32[8,1]{1,0:T(8,128)} %copy.20.ids_ref, s32[8]{0:T(128)} %count_ref.1, s32[8]{0:T(128)} %own_ref.3, bf16[8,16,3584]{2,1,0:T(8,128)(2,1)} %bitcast.29, bf16[8,16,3584]{2,1,0:T(8,128)(2,1)} %bitcast.30), custom_call_target="tpu_custom_call" | custom-call | tf_op jit(solution)/shard_map/dispatch/pallas_call | solution.py:109
  70.9 27.7 %all_to_all.37 = bf16[16,16,3584]{2,1,0:T(8,128)(2,1)} all-to-all(bf16[16,16,3584]{2,1,0:T(8,128)(2,1)} %get-tuple-element.37), channel_id=1, replica_groups=mesh['expert'=8,'x'=2,'y'=4,'core'=2] {'expert'}, dimensions={0} | all-to-all | bytes 3670016 | tf_op jit(solution)/shard_map/all_to_all | solution.py:369
  98.6 6.2 %all-to-all-start.3 = ((bf16[16,16,3584]{2,1,0:T(8,128)(2,1)}), bf16[16,16,3584]{2,1,0:T(8,128)(2,1)S(1)}, u32[]{:S(2)}, u32[]{:S(2)}) async-start(bf16[16,16,3584]{2,1,0:T(8,128)(2,1)} %get-tuple-element.38), calls=%async_computation.3 | async-start | bytes 3670016 | tf_op jit(solution)/shard_map/all_to_all | solution.py:369
  108.0 21.2 %collective-permute-done.2.refs_4_ = bf16[128,3584]{1,0:T(8,128)(2,1)S(1)} collective-permute-done((bf16[128,3584]{1,0:T(8,128)(2,1)}, bf16[128,3584]{1,0:T(8,128)(2,1)S(1)}, u32[]{:S(2)}, u32[]{:S(2)}) %collective-permute-start.2) | collective-permute-done | bytes 917536 | tf_op jit(solution)/shard_map/ppermute | solution.py:409
  134.2 8.6 %collective-permute-done.3.refs_2_ = bf16[64,3584]{1,0:T(8,128)(2,1)S(1)} collective-permute-done((bf16[64,3584]{1,0:T(8,128)(2,1)S(1)}, bf16[64,3584]{1,0:T(8,128)(2,1)S(1)}, u32[]{:S(2)}, u32[]{:S(2)}) %collective-permute-start.3) | collective-permute-done | bytes 458784 | tf_op jit(solution)/shard_map/ppermute | solution.py:411
  143.5 3.5 %pack_states.1 = bf16[8,4,224,128]{3,2,1,0:T(8,128)(2,1)} custom-call(f32[224,1024]{1,0:T(8,128)} %bitcast.34, f32[224,1024]{1,0:T(8,128)} %bitcast.35, f32[64,3584]{1,0:T(8,128)} %bitcast.36, f32[64,3584]{1,0:T(8,128)} %bitcast.37), custom_call_target="tpu_custom_call" | custom-call | tf_op jit(solution)/shard_map/pack_states/pallas_call | solution.py:153
  148.2 6.3 %flip.1.xt_ref = bf16[1792,512]{1,0:T(8,128)(2,1)} custom-call(s32[2]{0:T(128)} %pad_add_fusion.core_ref.at_ref.half_ref, bf16[256,3584]{1,0:T(8,128)(2,1)} %bitcast.11.own_ref, bf16[256,3584]{1,0:T(8,128)(2,1)} %collective-permute-done.other_ref), custom_call_target="tpu_custom_call" | custom-call | tf_op jit(solution)/shard_map/flip/pallas_call | solution.py:211
  154.5 7.6 %multiply_convert_fusion = (bf16[256,1024]{1,0:T(8,128)(2,1)S(1)}, f32[256,1024]{1,0:T(8,128)}) fusion(bf16[256,3584]{1,0:T(8,128)(2,1)} %bitcast.11.own_ref, bf16[3584,1024]{1,0:T(8,128)(2,1)} %all-gather.2.cloned.1.call-done), kind=kOutput, calls=%fused_computation.1 | convolution fusion | flops 1881407488 | bytes 10747904 | tf_op jit(solution)/shard_map/dot_general | solution.py:438
  162.2 7.1 %back.1.own_ref = bf16[256,1024]{1,0:T(8,128)(2,1)} custom-call(s32[2]{0:T(128)} %pad_add_fusion.core_ref.at_ref.half_ref, bf16[256,3584]{1,0:T(8,128)(2,1)} %bitcast.25, f32[256,1024]{1,0:T(8,128)} %get-tuple-element.64.slopes_ref, bf16[128,3584]{1,0:T(8,128)(2,1)} %get-tuple-element.36.refs_0_, bf16[128,3584]{1,0:T(8,128)(2,1)} %collective-permute-done.1.refs_1_, ...), custom_call_target="tpu_custom_call" | custom-call | tf_op jit(solution)/shard_map/back/pallas_call | solution.py:265
  172.2 5.6 %up_part.1 = bf16[1792,1024]{1,0:T(8,128)(2,1)} custom-call(bf16[1792,512]{1,0:T(8,128)(2,1)} %flip.1.xt_ref, bf16[256,1024]{1,0:T(8,128)(2,1)} %back.1.own_ref, bf16[256,1024]{1,0:T(8,128)(2,1)} %copy-done.9), custom_call_target="tpu_custom_call" | custom-call | tf_op jit(solution)/shard_map/up_part/pallas_call | solution.py:235
  179.7 7.4 %all-to-all-start.4 = ((bf16[8,4,224,128]{3,2,1,0:T(8,128)(2,1)}), bf16[8,4,224,128]{3,2,1,0:T(8,128)(2,1)}, u32[]{:S(2)}, u32[]{:S(2)}) async-start(bf16[8,4,224,128]{3,2,1,0:T(8,128)(2,1)} %pack_states.1), calls=%async_computation.4 | async-start | bytes 3670016 | tf_op jit(solution)/shard_map/all_to_all | solution.py:369
  187.2 23.4 %all-to-all-done.4.in_ref = bf16[8,4,224,128]{3,2,1,0:T(8,128)(2,1)} async-done(((bf16[8,4,224,128]{3,2,1,0:T(8,128)(2,1)}), bf16[8,4,224,128]{3,2,1,0:T(8,128)(2,1)}, u32[]{:S(2)}, u32[]{:S(2)}) %all-to-all-start.4) | async-done | bytes 1835040 | tf_op jit(solution)/shard_map/all_to_all | solution.py:369
  214.2 7.0 %shard_map.172.part_ref = bf16[512,3584]{1,0:T(8,128)(2,1)} custom-call(s32[2]{0:T(128)} %pad_add_fusion.core_ref.at_ref.half_ref, bf16[256,1024]{1,0:T(8,128)(2,1)} %copy-done.7, bf16[256,1024]{1,0:T(8,128)(2,1)} %copy-done.8, bf16[256,3584]{1,0:T(8,128)(2,1)} %bitcast.26, bf16[256,3584]{1,0:T(8,128)(2,1)} %collective-permute-done.12.bo_ref), custom_call_target="tpu_custom_call" | custom-call | tf_op jit(solution)/shard_map/pallas_call | solution.py:189
  221.3 6.2 %all-to-all-start.5 = ((bf16[8,4,224,128]{3,2,1,0:T(8,128)(2,1)}), bf16[8,4,224,128]{3,2,1,0:T(8,128)(2,1)S(1)}, u32[]{:S(2)}, u32[]{:S(2)}) async-start(bf16[8,4,224,128]{3,2,1,0:T(8,128)(2,1)} %shard_map.173), calls=%async_computation.5 | async-start | bytes 3670016 | tf_op jit(solution)/shard_map/all_to_all | solution.py:369
  232.8 6.5 %convolution_convert_fusion = bf16[256,3584]{1,0:T(8,128)(2,1)} fusion(bf16[256,1024]{1,0:T(8,128)(2,1)S(1)} %copy-done.3, bf16[3584,1024]{1,0:T(8,128)(2,1)} %all-gather.2.cloned.1.call-done), kind=kOutput, calls=%fused_computation | convolution fusion | flops 1879965696 | bytes 9699328 | tf_op jit(solution)/shard_map/dot_general | solution.py:453
  239.2 10.7 %all-to-all-done.5.state_ref = bf16[8,4,224,128]{3,2,1,0:T(8,128)(2,1)S(1)} async-done(((bf16[8,4,224,128]{3,2,1,0:T(8,128)(2,1)}), bf16[8,4,224,128]{3,2,1,0:T(8,128)(2,1)S(1)}, u32[]{:S(2)}, u32[]{:S(2)}) %all-to-all-start.5) | async-done | bytes 1835040 | tf_op jit(solution)/shard_map/all_to_all | solution.py:369
  251.2 6.9 %all-to-all-start.6 = ((bf16[16,16,3584]{2,1,0:T(8,128)(2,1)}), bf16[16,16,3584]{2,1,0:T(8,128)(2,1)}, u32[]{:S(2)}, u32[]{:S(2)}) async-start(bf16[16,16,3584]{2,1,0:T(8,128)(2,1)} %bitcast.28), calls=%async_computation.6 | async-start | bytes 3670016 | tf_op jit(solution)/shard_map/all_to_all | solution.py:369
  259.7 3.6 %relay.1 = (bf16[128,3584]{1,0:T(8,128)(2,1)}, bf16[128,3584]{1,0:T(8,128)(2,1)}) custom-call(bf16[512,3584]{1,0:T(8,128)(2,1)} %shard_map.172.part_ref, bf16[64,3584]{1,0:T(8,128)(2,1)} %copy-done.10, bf16[64,3584]{1,0:T(8,128)(2,1)} %copy-done.11), custom_call_target="tpu_custom_call" | custom-call | tf_op jit(solution)/shard_map/relay/pallas_call | solution.py:287
  266.5 18.4 %collective-permute-done.16.below_ref = bf16[128,3584]{1,0:T(8,128)(2,1)S(1)} collective-permute-done((bf16[128,3584]{1,0:T(8,128)(2,1)}, bf16[128,3584]{1,0:T(8,128)(2,1)S(1)}, u32[]{:S(2)}, u32[]{:S(2)}) %collective-permute-start.16) | collective-permute-done | bytes 917536 | tf_op jit(solution)/shard_map/ppermute | solution.py:458
  292.4 10.4 %collective-permute-done.18.other_ref = bf16[64,3584]{1,0:T(8,128)(2,1)S(1)} collective-permute-done((bf16[64,3584]{1,0:T(8,128)(2,1)}, bf16[64,3584]{1,0:T(8,128)(2,1)S(1)}, u32[]{:S(2)}, u32[]{:S(2)}) %collective-permute-start.18) | collective-permute-done | bytes 458784 | tf_op jit(solution)/shard_map/ppermute | solution.py:466
  303.6 4.1 %shard_map.175 = (f32[64,3584]{1,0:T(8,128)}, f32[64,3584]{1,0:T(8,128)}, f32[64,3584]{1,0:T(8,128)}) custom-call(s32[1]{0:T(128)} %bitcast.14.x_ref, bf16[16,2,224,128]{3,2,1,0:T(8,128)(2,1)} %all_to_all.36.in_ref.weight_ref, bf16[8,4,224,128]{3,2,1,0:T(8,128)(2,1)} %copy-done.2, f32[64,3584]{1,0:T(8,128)} %get-tuple-element.54.grad_ref, ...), custom_call_target="tpu_custom_call" | custom-call | tf_op jit(solution)/shard_map/pallas_call | solution.py:349
  311.2 4.3 %shard_map.174 = (f32[224,1024]{1,0:T(8,128)}, f32[224,1024]{1,0:T(8,128)}, f32[224,1024]{1,0:T(8,128)}) custom-call(s32[1]{0:T(128)} %bitcast.14.x_ref, bf16[16,2,224,128]{3,2,1,0:T(8,128)(2,1)} %all_to_all.36.in_ref.weight_ref, bf16[8,4,224,128]{3,2,1,0:T(8,128)(2,1)} %copy-done.2, bf16[448,1024]{1,0:T(8,128)(2,1)} %reduce-scatter.2.cloned.1.call-done.grad_ref, ...), custom_call_target="tpu_custom_call" | custom-call | tf_op jit(solution)/shard_map/pallas_call | solution.py:349
  (86 shorter events, 50.7 us)
Async XLA Ops:
  7.2 147.4 %all-gather.2.cloned.1.call-start = ((), (), s32[]{:S(2)}) async-start(), calls=%async_computation.8 | async-start | bytes 8257536 | tf_op jit(solution)/shard_map/all_gather | solution.py:405
  98.6 49.5 %collective-permute-start = (bf16[256,3584]{1,0:T(8,128)(2,1)}, bf16[256,3584]{1,0:T(8,128)(2,1)}, u32[]{:S(2)}, u32[]{:S(2)}) collective-permute-start(bf16[256,3584]{1,0:T(8,128)(2,1)} %bitcast.11.own_ref), channel_id=1, source_target_pairs={{0,1},{1,0},{2,3},{3,2},{4,5},{5,4},{6,7},{7,6},{8,9},{9,8},{10,11... | collective-permute-start | bytes 5505032 | tf_op jit(solution)/shard_map/ppermute | solution.py:373
  98.6 55.9 %all-to-all-start.3 = ((bf16[16,16,3584]{2,1,0:T(8,128)(2,1)}), bf16[16,16,3584]{2,1,0:T(8,128)(2,1)S(1)}, u32[]{:S(2)}, u32[]{:S(2)}) async-start(bf16[16,16,3584]{2,1,0:T(8,128)(2,1)} %get-tuple-element.38), calls=%async_computation.3 | async-start | bytes 3670016 | tf_op jit(solution)/shard_map/all_to_all | solution.py:369
  104.8 185.7 %reduce-scatter.2.cloned.1.call-start = ((), (), s32[]{:S(2)}) async-start(), calls=%async_computation.9 | async-start | bytes 4587520 | tf_op jit(solution)/shard_map/reduce_scatter | solution.py:445
  104.8 24.4 %collective-permute-start.2 = (bf16[128,3584]{1,0:T(8,128)(2,1)}, bf16[128,3584]{1,0:T(8,128)(2,1)S(1)}, u32[]{:S(2)}, u32[]{:S(2)}) collective-permute-start(bf16[128,3584]{1,0:T(8,128)(2,1)} %get-tuple-element.36.refs_0_), channel_id=1, source_target_pairs={{0,2},{2,4},{4,6},{6,0},{1,3},{3,5},{5,7},{7,1},{8,10},{10,12},{12... | collective-permute-start | bytes 2752520 | tf_op jit(solution)/shard_map/ppermute | solution.py:409
  106.3 23.0 %collective-permute-start.1 = (bf16[128,3584]{1,0:T(8,128)(2,1)}, bf16[128,3584]{1,0:T(8,128)(2,1)}, u32[]{:S(2)}, u32[]{:S(2)}) collective-permute-start(bf16[128,3584]{1,0:T(8,128)(2,1)} %get-tuple-element.36.refs_0_), channel_id=1, source_target_pairs={{0,6},{2,0},{4,2},{6,4},{1,7},{3,1},{5,3},{7,5},{8,14},{10,8},{12,... | collective-permute-start | bytes 2752520 | tf_op jit(solution)/shard_map/ppermute | solution.py:410
  129.2 13.5 %collective-permute-start.3 = (bf16[64,3584]{1,0:T(8,128)(2,1)S(1)}, bf16[64,3584]{1,0:T(8,128)(2,1)S(1)}, u32[]{:S(2)}, u32[]{:S(2)}) collective-permute-start(bf16[64,3584]{1,0:T(8,128)(2,1)S(1)} %slice.16), channel_id=1, source_target_pairs={{0,2},{2,4},{4,6},{6,0},{1,3},{3,5},{5,7},{7,1},{8,10},{10,12},{12... | collective-permute-start | bytes 1376264 | tf_op jit(solution)/shard_map/ppermute | solution.py:411
  130.6 17.0 %collective-permute-start.4 = (bf16[64,3584]{1,0:T(8,128)(2,1)S(1)}, bf16[64,3584]{1,0:T(8,128)(2,1)}, u32[]{:S(2)}, u32[]{:S(2)}) collective-permute-start(bf16[64,3584]{1,0:T(8,128)(2,1)S(1)} %slice.17), channel_id=1, source_target_pairs={{0,6},{2,0},{4,2},{6,4},{1,7},{3,1},{5,3},{7,5},{8,14},{10,8},{12,... | collective-permute-start | bytes 1376264 | tf_op jit(solution)/shard_map/ppermute | solution.py:412
  133.7 28.5 %collective-permute-start.5 = (bf16[128,3584]{1,0:T(8,128)(2,1)}, bf16[128,3584]{1,0:T(8,128)(2,1)}, u32[]{:S(2)}, u32[]{:S(2)}) collective-permute-start(bf16[128,3584]{1,0:T(8,128)(2,1)} %get-tuple-element.36.refs_0_), channel_id=1, source_target_pairs={{0,1},{1,0},{2,3},{3,2},{4,5},{5,4},{6,7},{7,6},{8,9},{9,8},{10,11... | collective-permute-start | bytes 2752520 | tf_op jit(solution)/shard_map/ppermute | solution.py:373
  133.7 28.5 %collective-permute-start.6 = (bf16[128,3584]{1,0:T(8,128)(2,1)}, bf16[128,3584]{1,0:T(8,128)(2,1)}, u32[]{:S(2)}, u32[]{:S(2)}) collective-permute-start(bf16[128,3584]{1,0:T(8,128)(2,1)} %collective-permute-done.1.refs_1_), channel_id=1, source_target_pairs={{0,1},{1,0},{2,3},{3,2},{4,5},{5,4},{6,7},{7,6},{8,9},{9,8},{10,11... | collective-permute-start | bytes 2752520 | tf_op jit(solution)/shard_map/ppermute | solution.py:373
  143.5 18.7 %collective-permute-start.9 = (bf16[128,3584]{1,0:T(8,128)(2,1)S(1)}, bf16[128,3584]{1,0:T(8,128)(2,1)}, u32[]{:S(2)}, u32[]{:S(2)}) collective-permute-start(bf16[128,3584]{1,0:T(8,128)(2,1)S(1)} %collective-permute-done.2.refs_4_), channel_id=1, source_target_pairs={{0,1},{1,0},{2,3},{3,2},{4,5},{5,4},{6,7},{7,6},{8,9},{9,8},{10,11... | collective-permute-start | bytes 2752520 | tf_op jit(solution)/shard_map/ppermute | solution.py:373
  147.6 14.5 %collective-permute-start.7 = (bf16[64,3584]{1,0:T(8,128)(2,1)}, bf16[64,3584]{1,0:T(8,128)(2,1)}, u32[]{:S(2)}, u32[]{:S(2)}) collective-permute-start(bf16[64,3584]{1,0:T(8,128)(2,1)} %copy-done.14), channel_id=1, source_target_pairs={{0,1},{1,0},{2,3},{3,2},{4,5},{5,4},{6,7},{7,6},{8,9},{9,8},{10,11... | collective-permute-start | bytes 1376264 | tf_op jit(solution)/shard_map/ppermute | solution.py:373
  148.1 14.0 %collective-permute-start.8 = (bf16[64,3584]{1,0:T(8,128)(2,1)}, bf16[64,3584]{1,0:T(8,128)(2,1)}, u32[]{:S(2)}, u32[]{:S(2)}) collective-permute-start(bf16[64,3584]{1,0:T(8,128)(2,1)} %collective-permute-done.4.refs_3_), channel_id=1, source_target_pairs={{0,1},{1,0},{2,3},{3,2},{4,5},{5,4},{6,7},{7,6},{8,9},{9,8},{10,11... | collective-permute-start | bytes 1376264 | tf_op jit(solution)/shard_map/ppermute | solution.py:373
  179.4 34.1 %collective-permute-start.12 = (bf16[256,3584]{1,0:T(8,128)(2,1)S(1)}, bf16[256,3584]{1,0:T(8,128)(2,1)}, u32[]{:S(2)}, u32[]{:S(2)}) collective-permute-start(bf16[256,3584]{1,0:T(8,128)(2,1)S(1)} %bitcast.27), channel_id=1, source_target_pairs={{0,1},{1,0},{2,3},{3,2},{4,5},{5,4},{6,7},{7,6},{8,9},{9,8},{10,11... | collective-permute-start | bytes 5505032 | tf_op jit(solution)/shard_map/ppermute | solution.py:373
  179.7 30.8 %all-to-all-start.4 = ((bf16[8,4,224,128]{3,2,1,0:T(8,128)(2,1)}), bf16[8,4,224,128]{3,2,1,0:T(8,128)(2,1)}, u32[]{:S(2)}, u32[]{:S(2)}) async-start(bf16[8,4,224,128]{3,2,1,0:T(8,128)(2,1)} %pack_states.1), calls=%async_computation.4 | async-start | bytes 3670016 | tf_op jit(solution)/shard_map/all_to_all | solution.py:369
  187.2 26.3 %collective-permute-start.11 = (bf16[256,1024]{1,0:T(8,128)(2,1)S(1)}, bf16[256,1024]{1,0:T(8,128)(2,1)S(1)}, u32[]{:S(2)}, u32[]{:S(2)}) collective-permute-start(bf16[256,1024]{1,0:T(8,128)(2,1)S(1)} %get-tuple-element.63.a_ref), channel_id=1, source_target_pairs={{0,1},{1,0},{2,3},{3,2},{4,5},{5,4},{6,7},{7,6},{8,9},{9,8},{10,11... | collective-permute-start | bytes 1572872 | tf_op jit(solution)/shard_map/ppermute | solution.py:373
  221.3 28.6 %all-to-all-start.5 = ((bf16[8,4,224,128]{3,2,1,0:T(8,128)(2,1)}), bf16[8,4,224,128]{3,2,1,0:T(8,128)(2,1)S(1)}, u32[]{:S(2)}, u32[]{:S(2)}) async-start(bf16[8,4,224,128]{3,2,1,0:T(8,128)(2,1)} %shard_map.173), calls=%async_computation.5 | async-start | bytes 3670016 | tf_op jit(solution)/shard_map/all_to_all | solution.py:369
  229.5 28.6 %collective-permute-start.14 = (bf16[64,3584]{1,0:T(8,128)(2,1)}, bf16[64,3584]{1,0:T(8,128)(2,1)S(1)}, u32[]{:S(2)}, u32[]{:S(2)}) collective-permute-start(bf16[64,3584]{1,0:T(8,128)(2,1)} %get-tuple-element.62), channel_id=1, source_target_pairs={{0,2},{2,4},{4,6},{6,0},{1,3},{3,5},{5,7},{7,1},{8,10},{10,12},{12... | collective-permute-start | bytes 1376264 | tf_op jit(solution)/shard_map/ppermute | solution.py:448
  229.5 28.6 %collective-permute-start.15 = (bf16[64,3584]{1,0:T(8,128)(2,1)S(1)}, bf16[64,3584]{1,0:T(8,128)(2,1)S(1)}, u32[]{:S(2)}, u32[]{:S(2)}) collective-permute-start(bf16[64,3584]{1,0:T(8,128)(2,1)S(1)} %get-tuple-element.61), channel_id=1, source_target_pairs={{0,6},{2,0},{4,2},{6,4},{1,7},{3,1},{5,3},{7,5},{8,14},{10,8},{12,... | collective-permute-start | bytes 1376264 | tf_op jit(solution)/shard_map/ppermute | solution.py:449
  251.2 56.5 %all-to-all-start.6 = ((bf16[16,16,3584]{2,1,0:T(8,128)(2,1)}), bf16[16,16,3584]{2,1,0:T(8,128)(2,1)}, u32[]{:S(2)}, u32[]{:S(2)}) async-start(bf16[16,16,3584]{2,1,0:T(8,128)(2,1)} %bitcast.28), calls=%async_computation.6 | async-start | bytes 3670016 | tf_op jit(solution)/shard_map/all_to_all | solution.py:369
  263.3 21.6 %collective-permute-start.16 = (bf16[128,3584]{1,0:T(8,128)(2,1)}, bf16[128,3584]{1,0:T(8,128)(2,1)S(1)}, u32[]{:S(2)}, u32[]{:S(2)}) collective-permute-start(bf16[128,3584]{1,0:T(8,128)(2,1)} %get-tuple-element.52), channel_id=1, source_target_pairs={{0,2},{2,4},{4,6},{6,0},{1,3},{3,5},{5,7},{7,1},{8,10},{10,12},{12... | collective-permute-start | bytes 2752520 | tf_op jit(solution)/shard_map/ppermute | solution.py:458
  263.3 21.6 %collective-permute-start.17 = (bf16[128,3584]{1,0:T(8,128)(2,1)}, bf16[128,3584]{1,0:T(8,128)(2,1)S(1)}, u32[]{:S(2)}, u32[]{:S(2)}) collective-permute-start(bf16[128,3584]{1,0:T(8,128)(2,1)} %get-tuple-element.53), channel_id=1, source_target_pairs={{0,6},{2,0},{4,2},{6,4},{1,7},{3,1},{5,3},{7,5},{8,14},{10,8},{12,... | collective-permute-start | bytes 2752520 | tf_op jit(solution)/shard_map/ppermute | solution.py:459
  289.2 13.6 %collective-permute-start.18 = (bf16[64,3584]{1,0:T(8,128)(2,1)}, bf16[64,3584]{1,0:T(8,128)(2,1)S(1)}, u32[]{:S(2)}, u32[]{:S(2)}) collective-permute-start(bf16[64,3584]{1,0:T(8,128)(2,1)} %get-tuple-element.55), channel_id=1, source_target_pairs={{0,8},{8,0},{1,9},{9,1},{2,10},{10,2},{3,11},{11,3},{4,12},{12,4},... | collective-permute-start | bytes 1376264 | tf_op jit(solution)/shard_map/ppermute | solution.py:466
  291.5 18.9 %collective-permute-start.13 = (bf16[224,1024]{1,0:T(8,128)(2,1)S(1)}, bf16[224,1024]{1,0:T(8,128)(2,1)S(1)}, u32[]{:S(2)}, u32[]{:S(2)}) collective-permute-start(bf16[224,1024]{1,0:T(8,128)(2,1)S(1)} %constant_dynamic-slice_fusion), channel_id=1, source_target_pairs={{0,8},{8,0},{1,9},{9,1},{2,10},{10,2},{3,11},{11,3},{4,12},{12,4},... | collective-permute-start | bytes 1376264 | tf_op jit(solution)/shard_map/ppermute | solution.py:468
  (17 other events, 71.4 us)
Sparse Core Ops, SparseCore 0:
  66.5 45.1 all-gather.1
  178.0 41.4 reduce-scatter.1
